TPU v7x, 32 devices: a whole 2x2x4 slice. The times are simulated.
32 devices in a mesh: dp: 8 (over z, x), seq: 4 (over y, core).
Axes of the slice: x: 2, y: 2, z: 4, core: 2. Of those that a mesh axis runs over, the one named last changes fastest.
Arguments:
- hidden_in: bfloat16 [8, 1536, 1280], P('dp', 'seq'), may hold values from -6 to 6
- cotangent: bfloat16 [8, 1536, 1280], P('dp', 'seq'), may hold values from -6 to 6
- clip_lengths: int32 [8], replicated, may hold values from 384 to 1500, as said below
- clip_order: int32 [8], P('dp'), may hold values from 0 to 7, each once
- first_gain: bfloat16 [1280], P('dp'), may hold values from 0.099609375 to 1.8984375
- first_shift: bfloat16 [1280], P('dp'), may hold values from -3 to 3
- query_weight: bfloat16 [1280, 1280], P('dp'), may hold values from -0.15625 to 0.15625
- query_bias: bfloat16 [1280], P('dp'), may hold values from -3 to 3
- key_weight: bfloat16 [1280, 1280], P('dp'), may hold values from -0.15625 to 0.15625
- value_weight: bfloat16 [1280, 1280], P('dp'), may hold values from -0.15625 to 0.15625
- value_bias: bfloat16 [1280], P('dp'), may hold values from -3 to 3
- output_weight: bfloat16 [1280, 1280], P('dp'), may hold values from -3.5 to 3.5
- output_bias: bfloat16 [1280], P('dp'), may hold values from -3 to 3
- second_gain: bfloat16 [1280], P('dp'), may hold values from 0.099609375 to 1.8984375
- second_shift: bfloat16 [1280], P('dp'), may hold values from -3 to 3
- expand_weight: bfloat16 [1280, 5120], P('dp'), may hold values from -0.15625 to 0.15625
- expand_bias: bfloat16 [5120], P('dp'), may hold values from -3 to 3
- reduce_weight: bfloat16 [5120, 1280], P('dp'), may hold values from -0.078125 to 0.078125
- reduce_bias: bfloat16 [1280], P('dp'), may hold values from -3 to 3
Outputs:
- layer_output: bfloat16 [8, 1536, 1280], P('dp', 'seq')
- input_grad: bfloat16 [8, 1536, 1280], P('dp', 'seq')
- first_gain_grad: float32 [1280], P('dp')
- first_shift_grad: float32 [1280], P('dp')
- query_weight_grad: float32 [1280, 1280], P('dp')
- query_bias_grad: float32 [1280], P('dp')
- key_weight_grad: float32 [1280, 1280], P('dp')
- value_weight_grad: float32 [1280, 1280], P('dp')
- value_bias_grad: float32 [1280], P('dp')
- output_weight_grad: float32 [1280, 1280], P('dp')
- output_bias_grad: float32 [1280], P('dp')
- second_gain_grad: float32 [1280], P('dp')
- second_shift_grad: float32 [1280], P('dp')
- expand_weight_grad: float32 [1280, 5120], P('dp')
- expand_bias_grad: float32 [5120], P('dp')
- reduce_weight_grad: float32 [5120, 1280], P('dp')
- reduce_bias_grad: float32 [1280], P('dp')
Inputs may be any that keep to these rules, and one draw needn't show every extreme that they name: `clip_lengths`: some clip is exactly 1500 long and some other exactly 384. `clip_order`: A permutation of the clips.
All inputs are finite; a program needn't handle non-finite values.
Results may differ from a plain program's by a relative error of at most 0.018.
Values may be sent and summed in bfloat16 or wider, within the bound.
A program may use at most 256 MiB of HBM per device.

v0:
```python
import jax
import jax.numpy as jnp
from jax import lax
from jax.sharding import PartitionSpec as P

D = 1280
HEADS = 16


EPSILON = 1e-05


def layer_norm(values, norm_gain, norm_shift):
    average = jnp.mean(values, axis=-1, keepdims=True)
    centered = values - average
    variance = jnp.mean(centered * centered, axis=-1, keepdims=True)
    return centered * lax.rsqrt(variance + EPSILON) * norm_gain + norm_shift


def gelu_exact(values):
    return jax.nn.gelu(values, approximate=False)


def own_lengths(clip_lengths, clip_order):
    clip_index = jnp.arange(clip_lengths.shape[0], dtype=jnp.int32)
    matches = clip_order[:, None] == clip_index[None, :]
    return jnp.sum(jnp.where(matches, clip_lengths[None, :], 0), axis=1)


def clip_scores(query_block, key_clip, key_valid, score_scale):
    scores = (
        jnp.einsum("qhd,khd->hqk", query_block, key_clip, preferred_element_type=jnp.float32)
        * score_scale
    )
    return jnp.where(key_valid[None, None, :], scores, -1e30)


def attention_forward(query_clip, key_clip, value_clip, length):
    slots, heads_here, head_dim = key_clip.shape
    block_rows = min(slots, 512)
    score_scale = head_dim ** (-0.5)
    key_valid = jnp.arange(slots, dtype=jnp.int32) < length
    blocks = query_clip.reshape(slots // block_rows, block_rows, heads_here, head_dim)

    def one_block(query_block):
        scores = clip_scores(query_block, key_clip, key_valid, score_scale)
        row_max = jnp.max(scores, axis=-1, keepdims=True)
        exponent = jnp.exp(scores - row_max)
        row_total = jnp.sum(exponent, axis=-1, keepdims=True)
        probability = (exponent / row_total).astype(jnp.bfloat16)
        mixture = jnp.einsum(
            "hqk,khd->qhd", probability, value_clip, preferred_element_type=jnp.float32
        )
        return (mixture.astype(jnp.bfloat16), (row_max + jnp.log(row_total))[:, :, 0])

    mixture, log_total = lax.map(one_block, blocks)
    return (mixture.reshape(slots, heads_here, head_dim), log_total)


def attention_backward(query_clip, key_clip, value_clip, length, grad_clip, log_total):
    slots, heads_here, head_dim = key_clip.shape
    block_rows = min(slots, 512)
    score_scale = head_dim ** (-0.5)
    key_valid = jnp.arange(slots, dtype=jnp.int32) < length
    blocks = query_clip.reshape(slots // block_rows, block_rows, heads_here, head_dim)
    grad_blocks = grad_clip.reshape(slots // block_rows, block_rows, heads_here, head_dim)

    def one_block(running, block_item):
        key_sum, value_sum = running
        query_block, grad_block, total_block = block_item
        scores = clip_scores(query_block, key_clip, key_valid, score_scale)
        probability = jnp.exp(scores - total_block[:, :, None])
        grad_probs = jnp.einsum(
            "qhd,khd->hqk", grad_block, value_clip, preferred_element_type=jnp.float32
        )
        row_inner = jnp.sum(probability * grad_probs, axis=-1, keepdims=True)
        grad_scores = (probability * (grad_probs - row_inner)).astype(jnp.bfloat16)
        grad_query = (
            jnp.einsum("hqk,khd->qhd", grad_scores, key_clip, preferred_element_type=jnp.float32)
            * score_scale
        )
        key_sum = (
            key_sum
            + jnp.einsum(
                "hqk,qhd->khd", grad_scores, query_block, preferred_element_type=jnp.float32
            )
            * score_scale
        )
        value_sum = value_sum + jnp.einsum(
            "hqk,qhd->khd",
            probability.astype(jnp.bfloat16),
            grad_block,
            preferred_element_type=jnp.float32,
        )
        return ((key_sum, value_sum), grad_query)

    zeros_start = jnp.zeros((slots, heads_here, head_dim), jnp.float32)
    (key_sum, value_sum), grad_query = lax.scan(
        one_block, (zeros_start, zeros_start), (blocks, grad_blocks, log_total)
    )
    grad_query = grad_query.reshape(slots, heads_here, head_dim)
    return (
        grad_query.astype(jnp.bfloat16),
        key_sum.astype(jnp.bfloat16),
        value_sum.astype(jnp.bfloat16),
    )


def per_device(
    hidden_in,
    cotangent,
    clip_lengths,
    clip_order,
    first_gain,
    first_shift,
    query_weight,
    query_bias,
    key_weight,
    value_weight,
    value_bias,
    output_weight,
    output_bias,
    second_gain,
    second_shift,
    expand_weight,
    expand_bias,
    reduce_weight,
    reduce_bias,
):
    clips_here, rows_here, features = hidden_in.shape
    seq_count = lax.axis_size("seq")
    heads_here = HEADS // seq_count
    head_dim = D // HEADS
    slots = rows_here * seq_count
    lengths_here = own_lengths(clip_lengths, clip_order)
    positions = lax.axis_index("seq") * rows_here + jnp.arange(rows_here, dtype=jnp.int32)
    row_valid = (positions[None, :] < lengths_here[:, None]).astype(jnp.float32)
    (
        gain_one,
        shift_one,
        weight_query,
        bias_query,
        weight_key,
        weight_value,
        bias_value,
        weight_out,
        bias_out,
    ) = (
        lax.all_gather(first_gain, "dp", axis=0, tiled=True),
        lax.all_gather(first_shift, "dp", axis=0, tiled=True),
        lax.all_gather(query_weight, "dp", axis=0, tiled=True),
        lax.all_gather(query_bias, "dp", axis=0, tiled=True),
        lax.all_gather(key_weight, "dp", axis=0, tiled=True),
        lax.all_gather(value_weight, "dp", axis=0, tiled=True),
        lax.all_gather(value_bias, "dp", axis=0, tiled=True),
        lax.all_gather(output_weight, "dp", axis=0, tiled=True),
        lax.all_gather(output_bias, "dp", axis=0, tiled=True),
    )
    hidden = hidden_in.astype(jnp.float32)
    normed = layer_norm(hidden, gain_one, shift_one).astype(jnp.bfloat16)
    query_tokens = (
        jnp.dot(normed, weight_query, preferred_element_type=jnp.float32) + bias_query
    ).astype(jnp.bfloat16)
    key_tokens = jnp.dot(normed, weight_key, preferred_element_type=jnp.float32).astype(
        jnp.bfloat16
    )
    value_tokens = (
        jnp.dot(normed, weight_value, preferred_element_type=jnp.float32) + bias_value
    ).astype(jnp.bfloat16)
    query_heads, key_heads, value_heads = (
        lax.all_to_all(query_tokens, "seq", split_axis=2, concat_axis=1, tiled=True),
        lax.all_to_all(key_tokens, "seq", split_axis=2, concat_axis=1, tiled=True),
        lax.all_to_all(value_tokens, "seq", split_axis=2, concat_axis=1, tiled=True),
    )
    head_shape = (clips_here, slots, heads_here, head_dim)
    query_heads = query_heads.reshape(head_shape)
    key_heads = key_heads.reshape(head_shape)
    value_heads = value_heads.reshape(head_shape)

    def clip_forward(clip_item):
        return attention_forward(clip_item[0], clip_item[1], clip_item[2], clip_item[3])

    mixture_heads, log_total = lax.map(
        clip_forward, (query_heads, key_heads, value_heads, lengths_here)
    )
    mixture = lax.all_to_all(
        mixture_heads.reshape(clips_here, slots, heads_here * head_dim),
        "seq",
        split_axis=1,
        concat_axis=2,
        tiled=True,
    )
    middle = hidden + (jnp.dot(mixture, weight_out, preferred_element_type=jnp.float32) + bias_out)
    gain_two, shift_two, weight_expand, bias_expand, weight_reduce, bias_reduce = (
        lax.all_gather(second_gain, "dp", axis=0, tiled=True),
        lax.all_gather(second_shift, "dp", axis=0, tiled=True),
        lax.all_gather(expand_weight, "dp", axis=0, tiled=True),
        lax.all_gather(expand_bias, "dp", axis=0, tiled=True),
        lax.all_gather(reduce_weight, "dp", axis=0, tiled=True),
        lax.all_gather(reduce_bias, "dp", axis=0, tiled=True),
    )
    second = layer_norm(middle, gain_two, shift_two).astype(jnp.bfloat16)
    expanded = jnp.dot(second, weight_expand, preferred_element_type=jnp.float32) + bias_expand
    activated = gelu_exact(expanded).astype(jnp.bfloat16)
    output = middle + (
        jnp.dot(activated, weight_reduce, preferred_element_type=jnp.float32) + bias_reduce
    )
    layer_output = output.astype(jnp.bfloat16)
    grad_out = cotangent.astype(jnp.float32) * row_valid[:, :, None]
    grad_branch_two = grad_out.astype(jnp.bfloat16)
    reduce_weight_grad = jnp.einsum(
        "ctf,ctd->fd", activated, grad_branch_two, preferred_element_type=jnp.float32
    )
    reduce_bias_grad = jnp.sum(grad_branch_two, axis=(0, 1), dtype=jnp.float32)
    grad_activated = jnp.einsum(
        "ctd,fd->ctf", grad_branch_two, weight_reduce, preferred_element_type=jnp.float32
    )
    expanded_value, gelu_pull = jax.vjp(gelu_exact, expanded)
    grad_expanded = gelu_pull(grad_activated)[0].astype(jnp.bfloat16)
    expand_weight_grad = jnp.einsum(
        "ctd,ctf->df", second, grad_expanded, preferred_element_type=jnp.float32
    )
    expand_bias_grad = jnp.sum(grad_expanded, axis=(0, 1), dtype=jnp.float32)
    grad_second = jnp.einsum(
        "ctf,df->ctd", grad_expanded, weight_expand, preferred_element_type=jnp.float32
    )
    second_value, second_pull = jax.vjp(layer_norm, middle, gain_two, shift_two)
    grad_middle_part, second_gain_grad, second_shift_grad = second_pull(grad_second)
    grad_middle = grad_out + grad_middle_part
    feed_shards = (
        lax.psum_scatter(second_gain_grad, "dp", scatter_dimension=0, tiled=True).astype(
            jnp.float32
        ),
        lax.psum_scatter(second_shift_grad, "dp", scatter_dimension=0, tiled=True).astype(
            jnp.float32
        ),
        lax.psum_scatter(
            expand_weight_grad.astype(jnp.bfloat16), "dp", scatter_dimension=0, tiled=True
        ).astype(jnp.float32),
        lax.psum_scatter(
            expand_bias_grad.astype(jnp.bfloat16), "dp", scatter_dimension=0, tiled=True
        ).astype(jnp.float32),
        lax.psum_scatter(
            reduce_weight_grad.astype(jnp.bfloat16), "dp", scatter_dimension=0, tiled=True
        ).astype(jnp.float32),
        lax.psum_scatter(
            reduce_bias_grad.astype(jnp.bfloat16), "dp", scatter_dimension=0, tiled=True
        ).astype(jnp.float32),
    )
    grad_branch = grad_middle.astype(jnp.bfloat16)
    output_weight_grad = jnp.einsum(
        "ctd,cte->de", mixture, grad_branch, preferred_element_type=jnp.float32
    )
    output_bias_grad = jnp.sum(grad_branch, axis=(0, 1), dtype=jnp.float32)
    grad_mixture = jnp.einsum(
        "cte,de->ctd", grad_branch, weight_out, preferred_element_type=jnp.float32
    ).astype(jnp.bfloat16)
    grad_mixture_heads = lax.all_to_all(
        grad_mixture, "seq", split_axis=2, concat_axis=1, tiled=True
    ).reshape(head_shape)

    def clip_backward(clip_item):
        return attention_backward(
            clip_item[0], clip_item[1], clip_item[2], clip_item[3], clip_item[4], clip_item[5]
        )

    grad_query_heads, grad_key_heads, grad_value_heads = lax.map(
        clip_backward,
        (query_heads, key_heads, value_heads, lengths_here, grad_mixture_heads, log_total),
    )
    flat_shape = (clips_here, slots, heads_here * head_dim)
    grad_queries, grad_keys, grad_values = (
        lax.all_to_all(
            grad_query_heads.reshape(flat_shape), "seq", split_axis=1, concat_axis=2, tiled=True
        ),
        lax.all_to_all(
            grad_key_heads.reshape(flat_shape), "seq", split_axis=1, concat_axis=2, tiled=True
        ),
        lax.all_to_all(
            grad_value_heads.reshape(flat_shape), "seq", split_axis=1, concat_axis=2, tiled=True
        ),
    )
    query_weight_grad = jnp.einsum(
        "ctd,cte->de", normed, grad_queries, preferred_element_type=jnp.float32
    )
    query_bias_grad = jnp.sum(grad_queries, axis=(0, 1), dtype=jnp.float32)
    key_weight_grad = jnp.einsum(
        "ctd,cte->de", normed, grad_keys, preferred_element_type=jnp.float32
    )
    value_weight_grad = jnp.einsum(
        "ctd,cte->de", normed, grad_values, preferred_element_type=jnp.float32
    )
    value_bias_grad = jnp.sum(grad_values, axis=(0, 1), dtype=jnp.float32)
    grad_normed = jnp.einsum(
        "cte,de->ctd", grad_queries, weight_query, preferred_element_type=jnp.float32
    )
    grad_normed = grad_normed + jnp.einsum(
        "cte,de->ctd", grad_keys, weight_key, preferred_element_type=jnp.float32
    )
    grad_normed = grad_normed + jnp.einsum(
        "cte,de->ctd", grad_values, weight_value, preferred_element_type=jnp.float32
    )
    first_value, first_pull = jax.vjp(layer_norm, hidden, gain_one, shift_one)
    grad_front_part, first_gain_grad, first_shift_grad = first_pull(grad_normed)
    input_grad = (grad_middle + grad_front_part).astype(jnp.bfloat16)
    attention_shards = (
        lax.psum_scatter(first_gain_grad, "dp", scatter_dimension=0, tiled=True).astype(
            jnp.float32
        ),
        lax.psum_scatter(first_shift_grad, "dp", scatter_dimension=0, tiled=True).astype(
            jnp.float32
        ),
        lax.psum_scatter(
            query_weight_grad.astype(jnp.bfloat16), "dp", scatter_dimension=0, tiled=True
        ).astype(jnp.float32),
        lax.psum_scatter(
            query_bias_grad.astype(jnp.bfloat16), "dp", scatter_dimension=0, tiled=True
        ).astype(jnp.float32),
        lax.psum_scatter(
            key_weight_grad.astype(jnp.bfloat16), "dp", scatter_dimension=0, tiled=True
        ).astype(jnp.float32),
        lax.psum_scatter(
            value_weight_grad.astype(jnp.bfloat16), "dp", scatter_dimension=0, tiled=True
        ).astype(jnp.float32),
        lax.psum_scatter(
            value_bias_grad.astype(jnp.bfloat16), "dp", scatter_dimension=0, tiled=True
        ).astype(jnp.float32),
        lax.psum_scatter(
            output_weight_grad.astype(jnp.bfloat16), "dp", scatter_dimension=0, tiled=True
        ).astype(jnp.float32),
        lax.psum_scatter(
            output_bias_grad.astype(jnp.bfloat16), "dp", scatter_dimension=0, tiled=True
        ).astype(jnp.float32),
    )
    summed = (
        lax.psum(attention_shards[0].astype(jnp.bfloat16), "seq").astype(jnp.float32),
        lax.psum(attention_shards[1].astype(jnp.bfloat16), "seq").astype(jnp.float32),
        lax.psum(attention_shards[2].astype(jnp.bfloat16), "seq").astype(jnp.float32),
        lax.psum(attention_shards[3].astype(jnp.bfloat16), "seq").astype(jnp.float32),
        lax.psum(attention_shards[4].astype(jnp.bfloat16), "seq").astype(jnp.float32),
        lax.psum(attention_shards[5].astype(jnp.bfloat16), "seq").astype(jnp.float32),
        lax.psum(attention_shards[6].astype(jnp.bfloat16), "seq").astype(jnp.float32),
        lax.psum(attention_shards[7].astype(jnp.bfloat16), "seq").astype(jnp.float32),
        lax.psum(attention_shards[8].astype(jnp.bfloat16), "seq").astype(jnp.float32),
        lax.psum(feed_shards[0].astype(jnp.bfloat16), "seq").astype(jnp.float32),
        lax.psum(feed_shards[1].astype(jnp.bfloat16), "seq").astype(jnp.float32),
        lax.psum(feed_shards[2].astype(jnp.bfloat16), "seq").astype(jnp.float32),
        lax.psum(feed_shards[3].astype(jnp.bfloat16), "seq").astype(jnp.float32),
        lax.psum(feed_shards[4].astype(jnp.bfloat16), "seq").astype(jnp.float32),
        lax.psum(feed_shards[5].astype(jnp.bfloat16), "seq").astype(jnp.float32),
    )
    return (
        layer_output,
        input_grad,
        summed[0],
        summed[1],
        summed[2],
        summed[3],
        summed[4],
        summed[5],
        summed[6],
        summed[7],
        summed[8],
        summed[9],
        summed[10],
        summed[11],
        summed[12],
        summed[13],
        summed[14],
    )


def solution(mesh):
    return jax.shard_map(
        per_device,
        mesh=mesh,
        in_specs=(
            P("dp", "seq", None),
            P("dp", "seq", None),
            P(),
            P("dp"),
            P("dp"),
            P("dp"),
            P("dp", None),
            P("dp"),
            P("dp", None),
            P("dp", None),
            P("dp"),
            P("dp", None),
            P("dp"),
            P("dp"),
            P("dp"),
            P("dp", None),
            P("dp"),
            P("dp", None),
            P("dp"),
        ),
        out_specs=(
            P("dp", "seq", None),
            P("dp", "seq", None),
            P("dp"),
            P("dp"),
            P("dp", None),
            P("dp"),
            P("dp", None),
            P("dp", None),
            P("dp"),
            P("dp", None),
            P("dp"),
            P("dp"),
            P("dp"),
            P("dp", None),
            P("dp"),
            P("dp", None),
            P("dp"),
        ),
        check_vma=False,
    )
```

profile of v0, /device:TPU:0, one launch (start us, length us, event | category | flops | bytes accessed | tf_op | source)
XLA Modules:
  0.0 1642.0 jit_solution(3411974804848993153)
XLA Ops:
  14.3 41.0 %all-reduce.18 = (bf16[1280]{0:T(1024)(128)(2,1)S(1)}, bf16[1280]{0:T(1024)(128)(2,1)S(1)}, bf16[1280]{0:T(1024)(128)(2,1)S(1)}, bf16[1280]{0:T(1024)(128)(2,1)S...) all-reduce(bf16[1280]{0:T(1024)(128)(2,1)S(1)} %dynamic-update-slic, ...), channel_id=1, replica_groups=mesh['dp'=8,'seq'=4] {'dp'}, use_global_device_ids=true, to_apply=%add.2 | all-reduce | flops 8960 | bytes 35840
  56.0 19.0 %all-gather.8.cloned.1.call-done = bf16[1280,1280]{1,0:T(8,128)(2,1)} async-done(((bf16[160,1280]{1,0:T(8,128)(2,1)}), bf16[1280,1280]{1,0:T(8,128)(2,1)}) %all-gather.8.cloned.1.call-update) | async-done | bytes 3276816 | tf_op jit(solution)/shard_map/all_gather | solution.py:151
  100.6 36.8 %all-gather.12.cloned.1.call-done = bf16[1280,1280]{1,0:T(8,128)(2,1)} async-done(((bf16[160,1280]{1,0:T(8,128)(2,1)}), bf16[1280,1280]{1,0:T(8,128)(2,1)}) %all-gather.12.cloned.1.call-update) | async-done | bytes 3276816 | tf_op jit(solution)/shard_map/all_gather | solution.py:154
  162.1 37.7 %all-gather.10.cloned.1.call-done = bf16[1280,1280]{1,0:T(8,128)(2,1)} async-done(((bf16[160,1280]{1,0:T(8,128)(2,1)}), bf16[1280,1280]{1,0:T(8,128)(2,1)}) %all-gather.10.cloned.1.call-update) | async-done | bytes 3276816 | tf_op jit(solution)/shard_map/all_gather | solution.py:153
  247.8 29.8 %while.48 = (s32[]{:T(128)}, bf16[3,512,4,80]{1,3,2,0:T(8,128)(2,1)}, f32[3,4,512]{2,1,0:T(4,128)S(1)}, bf16[3,512,4,80]{1,3,2,0:T(8,128)(2,1)S(1)}, bf16[1536,4...) while((s32[]{:T(128)}, ...), condition=%wide.region_6.7_spmd.clone, body=%wide.region_3.6_spmd.clone.sunk | while | flops 1044545024 | bytes 40442976 | solution.py:56
  281.1 19.0 %reshape.502 = bf16[1,1536,320]{2,0,1:T(2,128)(2,1)} reshape(bf16[3,512,4,80]{3,2,1,0:T(4,128)(2,1)} %copy.168) | data formatting | bytes 1966080 | tf_op jit(solution)/shard_map/reshape | solution.py:187
  300.2 10.4 reduce.27
  318.9 31.4 %all-gather = bf16[8,1,640]{2,1,0:T(2,128)(2,1)S(1)} all-gather(bf16[1,1,640]{2,1,0:T(2,128)(2,1)S(1)} %reshape.483), channel_id=1, replica_groups=mesh['dp'=8,'seq'=4] {'dp'}, dimensions={0}, use_global_device_ids=true | all-gather | bytes 11520 | tf_op jit(solution)/shard_map/all_gather | solution.py:198
  369.8 75.7 %all-gather.16.cloned.1.call-done = bf16[1280,5120]{1,0:T(8,128)(2,1)} async-done(((bf16[160,5120]{1,0:T(8,128)(2,1)}), bf16[1280,5120]{1,0:T(8,128)(2,1)}) %all-gather.16.cloned.1.call-update) | async-done | bytes 13107216 | tf_op jit(solution)/shard_map/all_gather | solution.py:197
  445.4 26.5 %multiply_convert_fusion.1 = (bf16[384,5120]{1,0:T(8,128)(2,1)}, f32[384,5120]{1,0:T(8,128)}, f32[384,5120]{1,0:T(8,128)}) fusion(f32[5120]{0:T(1024)S(1)} %bitcast.270, bf16[1280,5120]{1,0:T(8,128)(2,1)} %all-gather.16.cloned.1.call-done, f32[1,384,1280]{2,1,0:T(8,128)} %copy-done.10, f32[1280]{0:T(1024)S(1)} %convert_element_type.260, ...), kind=kOutput, calls=%fused_computation.52 | convolution fusion | flops 5165383680 | bytes 34767872 | tf_op jit(solution)/shard_map/dot_general | solution.py:203
  471.9 156.3 %all-gather.18.cloned.1.call-done = bf16[5120,1280]{1,0:T(8,128)(2,1)} async-done(((bf16[640,1280]{1,0:T(8,128)(2,1)}), bf16[5120,1280]{1,0:T(8,128)(2,1)}) %all-gather.18.cloned.1.call-update) | async-done | bytes 13107216 | tf_op jit(solution)/shard_map/all_gather | solution.py:199
  628.2 16.3 fusion.104
  644.5 12.7 fusion.69
  713.6 95.8 %while.49 = (s32[]{:T(128)}, f32[1536,4,80]{0,2,1:T(8,128)}, f32[1536,4,80]{0,2,1:T(8,128)}, bf16[3,512,4,80]{1,3,2,0:T(8,128)(2,1)}, bf16[3,512,4,80]{1,3,2,0:T...) while((s32[]{:T(128)}, f32[1536,4,80]{0,2,1:T(8,128)}, ...), condition=%wide.region_13.14_spmd.clone, body=%wide.region_11.13_spmd.clone.sunk | while | flops 2547514880 | bytes 207860944 | solution.py:98
  830.9 16.1 all_to_all.120
  877.7 17.2 %all_to_all.121 = bf16[4,2,61440]{2,1,0:T(2,128)(2,1)S(1)} all-to-all(bf16[4,2,61440]{2,1,0:T(2,128)(2,1)} %reshape.531), channel_id=1, replica_groups=mesh['dp'=8,'seq'=4] {'seq'}, dimensions={0} | all-to-all | bytes 1966080 | tf_op jit(solution)/shard_map/all_to_all | solution.py:279
  929.6 17.2 %all_to_all.122 = bf16[4,2,61440]{2,1,0:T(2,128)(2,1)S(1)} all-to-all(bf16[4,2,61440]{2,1,0:T(2,128)(2,1)} %reshape.529), channel_id=1, replica_groups=mesh['dp'=8,'seq'=4] {'seq'}, dimensions={0} | all-to-all | bytes 1966080 | tf_op jit(solution)/shard_map/all_to_all | solution.py:276
  961.4 12.3 convolution_convert_fusion.1
  974.9 13.0 convolution_convert_fusion
  1003.5 36.2 %all-reduce.17 = (bf16[1280]{0:T(1024)(128)(2,1)S(1)}, bf16[1280]{0:T(1024)(128)(2,1)S(1)}, bf16[1280]{0:T(1024)(128)(2,1)S(1)}, bf16[1280]{0:T(1024)(128)(2,1)S...) all-reduce(bf16[1280]{0:T(1024)(128)(2,1)S(1)} %dynamic-update-slic, ...), channel_id=1, replica_groups=mesh['dp'=8,'seq'=4] {'dp'}, use_global_device_ids=true, to_apply=%add.7 | all-reduce | flops 16640 | bytes 66560
  1051.7 40.1 %reduce-scatter.9.cloned.1.call-done = bf16[160,1280]{1,0:T(8,128)(2,1)} async-done(((bf16[1280,1280]{1,0:T(8,128)(2,1)}), bf16[160,1280]{1,0:T(8,128)(2,1)}) %reduce-scatter.9.cloned.1.call-update) | async-done | bytes 409616 | tf_op jit(solution)/shard_map/reduce_scatter | solution.py:319
  1091.8 217.4 %reduce-scatter.15.cloned.1.call-done = bf16[160,5120]{1,0:T(8,128)(2,1)} async-done(((bf16[1280,5120]{1,0:T(8,128)(2,1)}), bf16[160,5120]{1,0:T(8,128)(2,1)}) %reduce-scatter.15.cloned.1.call-update) | async-done | bytes 1638416 | tf_op jit(solution)/shard_map/reduce_scatter | solution.py:237
  1309.2 217.4 %reduce-scatter.17.cloned.1.call-done = bf16[640,1280]{1,0:T(8,128)(2,1)} async-done(((bf16[5120,1280]{1,0:T(8,128)(2,1)}), bf16[640,1280]{1,0:T(8,128)(2,1)}) %reduce-scatter.17.cloned.1.call-update) | async-done | bytes 1638416 | tf_op jit(solution)/shard_map/reduce_scatter | solution.py:243
  1540.2 85.7 %all-reduce.23.cloned.1.call-done = (bf16[160,1280]{1,0:T(8,128)(2,1)}, bf16[160,1280]{1,0:T(8,128)(2,1)}, bf16[160,1280]{1,0:T(8,128)(2,1)}, bf16[160,1280]{1,0...) async-done(((bf16[160,1280]{1,0:T(8,128)(2,1)}, bf16[160,1280]{1,0:T(8,128)(2,1)}, bf16[160,1280]{1,0:T(8,128)(2,1)}, bf16[160,1280]{1,0:T(8,128)(2,1)}, ...) | async-done | bytes 4915216 | tf_op jit(solution)/shard_map/psum | solution.py:338
  (391 shorter events, 468.5 us)
Async XLA Ops:
  7.3 67.6 %all-gather.8.cloned.1.call-start = ((), (), s32[]{:S(2)}) async-start(), calls=%async_computation.14 | async-start | bytes 3686400 | tf_op jit(solution)/shard_map/all_gather | solution.py:151
  8.0 129.4 %all-gather.12.cloned.1.call-start = ((), (), s32[]{:S(2)}) async-start(), calls=%async_computation.16 | async-start | bytes 3686400 | tf_op jit(solution)/shard_map/all_gather | solution.py:154
  8.8 191.0 %all-gather.10.cloned.1.call-start = ((), (), s32[]{:S(2)}) async-start(), calls=%async_computation.15 | async-start | bytes 3686400 | tf_op jit(solution)/shard_map/all_gather | solution.py:153
  9.5 354.5 %all-gather.14.cloned.1.call-start = ((), (), s32[]{:S(2)}) async-start(), calls=%async_computation.17 | async-start | bytes 3686400 | tf_op jit(solution)/shard_map/all_gather | solution.py:156
  10.1 435.3 %all-gather.16.cloned.1.call-start = ((), (), s32[]{:S(2)}) async-start(), calls=%async_computation.18 | async-start | bytes 14745600 | tf_op jit(solution)/shard_map/all_gather | solution.py:197
  10.7 617.5 %all-gather.18.cloned.1.call-start = ((), (), s32[]{:S(2)}) async-start(), calls=%async_computation.19 | async-start | bytes 14745600 | tf_op jit(solution)/shard_map/all_gather | solution.py:199
  96.3 61.9 %all-to-all-start = ((bf16[4,2,61440]{2,1,0:T(2,128)(2,1)}), bf16[4,2,61440]{2,1,0:T(2,128)(2,1)}, u32[]{:S(2)}, u32[]{:S(2)}) async-start(bf16[4,2,61440]{2,1,0:T(2,128)(2,1)} %reshape.517), calls=%async_computation | async-start | bytes 1966080 | tf_op jit(solution)/shard_map/all_to_all | solution.py:171
  158.3 62.4 %all-to-all-start.2 = ((bf16[4,2,61440]{2,1,0:T(2,128)(2,1)}), bf16[4,2,61440]{2,1,0:T(2,128)(2,1)S(1)}, u32[]{:S(2)}, u32[]{:S(2)}) async-start(bf16[4,2,61440]{2,1,0:T(2,128)(2,1)} %reshape.521), calls=%async_computation.2 | async-start | bytes 1966080 | tf_op jit(solution)/shard_map/all_to_all | solution.py:173
  220.7 18.0 %all-to-all-start.1 = ((bf16[4,2,61440]{2,1,0:T(2,128)(2,1)}), bf16[4,2,61440]{2,1,0:T(2,128)(2,1)}, u32[]{:S(2)}, u32[]{:S(2)}) async-start(bf16[4,2,61440]{2,1,0:T(2,128)(2,1)} %reshape.519), calls=%async_computation.1 | async-start | bytes 1966080 | tf_op jit(solution)/shard_map/all_to_all | solution.py:172
  314.6 36.4 %all-to-all-start.3 = ((bf16[4,2,61440]{2,1,0:T(2,128)(2,1)}), bf16[4,2,61440]{2,1,0:T(2,128)(2,1)}, u32[]{:S(2)}, u32[]{:S(2)}) async-start(bf16[4,2,61440]{2,1,0:T(2,128)(2,1)} %reshape.523), calls=%async_computation.3 | async-start | bytes 1966080 | tf_op jit(solution)/shard_map/all_to_all | solution.py:186
  318.9 338.4 %copy-start.36 = (f32[1280]{0:T(1024)}, f32[1280]{0:T(1024)S(1)}, u32[]{:S(2)}) copy-start(f32[1280]{0:T(1024)S(1)} %convert_element_type.259) | copy-start | bytes 15364
  351.0 306.9 %copy-start.38 = (f32[384]{0:T(512)}, f32[384]{0:T(512)S(1)}, u32[]{:S(2)}) copy-start(f32[384]{0:T(512)S(1)} %fusion.82) | copy-start | bytes 4612
  368.2 289.1 %copy-start.44 = (f32[384]{0:T(512)}, f32[384]{0:T(512)S(1)}, u32[]{:S(2)}) copy-start(f32[384]{0:T(512)S(1)} %broadcast_multiply_fusion) | copy-start | bytes 4612
  369.8 287.5 %copy-start.49 = (f32[384]{0:T(512)}, f32[384]{0:T(512)S(1)}, u32[]{:S(2)}) copy-start(f32[384]{0:T(512)S(1)} %fusion.84) | copy-start | bytes 4612
  681.7 18.0 %all-to-all-start.4 = ((bf16[4,2,61440]{2,1,0:T(2,128)(2,1)}), bf16[4,2,61440]{2,1,0:T(2,128)(2,1)}, u32[]{:S(2)}, u32[]{:S(2)}) async-start(bf16[4,2,61440]{2,1,0:T(2,128)(2,1)} %reshape.525), calls=%async_computation.4 | async-start | bytes 1966080 | tf_op jit(solution)/shard_map/all_to_all | solution.py:258
  686.0 365.7 %reduce-scatter.13.cloned.1.call-start = ((), (), s32[]{:S(2)}) async-start(), calls=%async_computation.23 | async-start | bytes 3686400 | tf_op jit(solution)/shard_map/reduce_scatter | solution.py:328
  691.1 360.5 %reduce-scatter.7.cloned.1.call-start = ((), (), s32[]{:S(2)}) async-start(), calls=%async_computation.20 | async-start | bytes 3686400 | tf_op jit(solution)/shard_map/reduce_scatter | solution.py:313
  859.7 191.9 %reduce-scatter.11.cloned.1.call-start = ((), (), s32[]{:S(2)}) async-start(), calls=%async_computation.22 | async-start | bytes 3686400 | tf_op jit(solution)/shard_map/reduce_scatter | solution.py:322
  908.7 183.0 %reduce-scatter.9.cloned.1.call-start = ((), (), s32[]{:S(2)}) async-start(), calls=%async_computation.21 | async-start | bytes 3686400 | tf_op jit(solution)/shard_map/reduce_scatter | solution.py:319
  959.8 349.3 %reduce-scatter.15.cloned.1.call-start = ((), (), s32[]{:S(2)}) async-start(), calls=%async_computation.24 | async-start | bytes 14745600 | tf_op jit(solution)/shard_map/reduce_scatter | solution.py:237
  973.8 552.8 %reduce-scatter.17.cloned.1.call-start = ((), (), s32[]{:S(2)}) async-start(), calls=%async_computation.25 | async-start | bytes 14745600 | tf_op jit(solution)/shard_map/reduce_scatter | solution.py:243
  988.0 637.9 %all-reduce.23.cloned.1.call-start = ((), (), s32[]{:S(2)}) async-start(), calls=%async_computation.26 | async-start | bytes 9830400 | tf_op jit(solution)/shard_map/psum | solution.py:338
  1003.4 523.2 %copy-start.4 = (f32[1,384,1280]{2,1,0:T(8,128)S(1)}, f32[1,384,1280]{2,1,0:T(8,128)}, u32[]{:S(2)}) copy-start(f32[1,384,1280]{2,1,0:T(8,128)} %copy-done.3) | copy-start | bytes 5898244
  1003.4 523.2 %copy-start.41 = (f32[384]{0:T(512)S(1)}, f32[384]{0:T(512)}, u32[]{:S(2)}) copy-start(f32[384]{0:T(512)} %copy-done.40) | copy-start | bytes 4612
  (72 other events, 1119.8 us)
Sparse Core Ops, SparseCore 0:
  10.3 64.5 all-gather.7
  77.1 60.2 all-gather.11
  139.6 60.1 all-gather.9
  201.8 60.1 all-gather.13
  264.0 181.3 all-gather.15
  447.5 180.7 all-gather.17
  691.2 74.6 reduce-scatter.12
  859.9 73.5 reduce-scatter.6
  937.0 74.9 reduce-scatter.10
  1016.1 75.6 reduce-scatter.8
  1095.4 213.7 reduce-scatter.14
  1312.7 213.8 reduce-scatter.16
  1529.4 96.4 all-reduce.22
where the time goes:
time: 1650 us; the launch traced here: 1640 us
  waiting for transfers between devices  903 us (55%)
  matrix products  223 us (14%)
  local copies, waits for them, and re-layouts  185 us (11%)
  blocking collectives  165 us (10%)
  other arithmetic  126 us (8%)
  starting transfers between devices  21.8 us (1%)
  between operations  18 us (1%)
    reduce_scatter x1, waiting for transfers between devices, per_device(): lax.psum_scatter(expand_weight_grad.astype(jnp.bfloat16), 'dp', scatter_d...  217 us
    reduce_scatter x1, waiting for transfers between devices, per_device(): lax.psum_scatter(reduce_weight_grad.astype(jnp.bfloat16), 'dp', scatter_d...  217 us
    all_gather x1, waiting for transfers between devices, per_device(): lax.all_gather(reduce_weight, 'dp', axis=0, tiled=True)  156 us
    psum x1, waiting for transfers between devices, per_device(): lax.psum(attention_shards[2].astype(jnp.bfloat16), 'seq')  85.7 us
    unnamed x198, local copies, waits for them, and re-layouts  82.3 us
    unnamed x2, blocking collectives  77.2 us
    all_gather x1, waiting for transfers between devices, per_device(): lax.all_gather(expand_weight, 'dp', axis=0, tiled=True)  75.7 us
    unnamed x10, other arithmetic  73 us
  transfers between devices with their start and end apart: 18, of which 11 were waited for; matrix products, arithmetic and copies ran while one was open for 27% of the time, Pallas kernels for 0%

commit v1 on v0

v1 whole, which is shorter than its diff:
```python
import functools

import jax
import jax.numpy as jnp
from jax import lax
from jax.experimental import pallas as pl
from jax.experimental.pallas import tpu as pltpu
from jax.sharding import PartitionSpec as P

D = 1280
FF = 5120
HEADS = 16
HEAD_DIM = D // HEADS
EPSILON = 1e-05
SCALE = HEAD_DIM ** (-0.5)
F32 = jnp.float32
BF16 = jnp.bfloat16
VMEM_LIMIT = 60 * 1024 * 1024


def dot(left, right, contract=((1,), (0,))):
    return lax.dot_general(left, right, (contract, ((), ())), preferred_element_type=F32)


def normalize(values):
    average = jnp.mean(values, axis=-1, keepdims=True)
    centered = values - average
    variance = jnp.mean(centered * centered, axis=-1, keepdims=True)
    spread = lax.rsqrt(variance + EPSILON)
    return centered * spread, spread


def norm_backward(unit, spread, grad_unit):
    inner = jnp.mean(grad_unit * unit, axis=-1, keepdims=True)
    return spread * (grad_unit - jnp.mean(grad_unit, axis=-1, keepdims=True) - unit * inner)


def params(**extra):
    return pltpu.CompilerParams(vmem_limit_bytes=VMEM_LIMIT, **extra)


def whole(shape):
    return pl.BlockSpec(shape, lambda *_: (0,) * len(shape), pipeline_mode=pl.Buffered(1))


def project_kernel(heads, x_ref, w_ref, gain_ref, shift_ref, bias_ref, normed_ref, qkv_ref):
    unit, _ = normalize(x_ref[...].astype(F32))
    normed = (unit * gain_ref[...] + shift_ref[...]).astype(BF16)
    normed_ref[...] = normed
    tokens = (dot(normed, w_ref[...]) + bias_ref[...]).astype(BF16)
    for item in range(3 * heads):
        qkv_ref[item] = tokens[:, item * HEAD_DIM : (item + 1) * HEAD_DIM]


def project(x, w, gain, shift, bias):
    slots = x.shape[0]
    items = w.shape[1] // HEAD_DIM
    block = 256
    return pl.pallas_call(
        functools.partial(project_kernel, items // 3),
        grid=(slots // block,),
        in_specs=[
            pl.BlockSpec((block, D), lambda i: (i, 0)),
            whole(w.shape),
            whole((1, D)),
            whole((1, D)),
            whole((1, w.shape[1])),
        ],
        out_specs=[
            pl.BlockSpec((block, D), lambda i: (i, 0)),
            pl.BlockSpec((items, block, HEAD_DIM), lambda i: (0, i, 0)),
        ],
        out_shape=[
            jax.ShapeDtypeStruct((slots, D), BF16),
            jax.ShapeDtypeStruct((items, slots, HEAD_DIM), BF16),
        ],
        compiler_params=params(),
        name="project",
    )(x, w, gain, shift, bias)


def attend_kernel(heads, slots, length_ref, q_ref, k_ref, v_ref, mix_ref, lse_ref, own_ref):
    length = length_ref[0]
    block = q_ref.shape[1]
    invalid = lax.broadcasted_iota(jnp.int32, (1, slots), 1) >= length

    def one_head(head, _):
        scores = dot(q_ref[head], k_ref[head], ((1,), (1,))) * SCALE
        scores = jnp.where(invalid, -1e30, scores)
        top = jnp.max(scores, axis=-1, keepdims=True)
        exponent = jnp.exp(scores - top)
        total = jnp.sum(exponent, axis=-1, keepdims=True)
        mixed = dot(exponent.astype(BF16), v_ref[head])
        own_ref[head] = mixed / total
        lse_ref[head] = jnp.transpose(top + jnp.log(total))
        return 0

    lax.fori_loop(0, heads, one_head, 0)
    for head in range(heads):
        mix_ref[:, head * HEAD_DIM : (head + 1) * HEAD_DIM] = own_ref[head].astype(BF16)


def attend(qkv, length):
    items, slots, _ = qkv.shape
    heads = items // 3
    block = 256
    return pl.pallas_call(
        functools.partial(attend_kernel, heads, slots),
        grid_spec=pltpu.PrefetchScalarGridSpec(
            num_scalar_prefetch=1,
            grid=(slots // block,),
            in_specs=[
                pl.BlockSpec((heads, block, HEAD_DIM), lambda i, n: (0, i, 0)),
                pl.BlockSpec((heads, slots, HEAD_DIM), lambda i, n: (1, 0, 0)),
                pl.BlockSpec((heads, slots, HEAD_DIM), lambda i, n: (2, 0, 0)),
            ],
            out_specs=[
                pl.BlockSpec((block, heads * HEAD_DIM), lambda i, n: (i, 0)),
                pl.BlockSpec((heads, 1, block), lambda i, n: (0, 0, i)),
            ],
            scratch_shapes=[pltpu.VMEM((heads, block, HEAD_DIM), F32)],
        ),
        out_shape=[
            jax.ShapeDtypeStruct((slots, heads * HEAD_DIM), BF16),
            jax.ShapeDtypeStruct((heads, 1, slots), F32),
        ],
        compiler_params=params(),
        name="attend",
    )(length, qkv, qkv, qkv)


def attend_back_kernel(
    slots, length_ref, q_ref, k_ref, v_ref, go_ref, mix_ref, lse_ref,
    dq_ref, dk_ref, dv_ref, turned_ref, dk_sum, dv_sum,
):
    step = pl.program_id(1)
    length = length_ref[0]

    @pl.when(step == 0)
    def _():
        turned_ref[...] = jnp.transpose(k_ref[0])
        dk_sum[...] = jnp.zeros_like(dk_sum)
        dv_sum[...] = jnp.zeros_like(dv_sum)

    invalid = lax.broadcasted_iota(jnp.int32, (slots, 1), 0) >= length
    query = q_ref[0]
    grad = go_ref[0]
    delta = jnp.sum(
        jnp.transpose(grad.astype(F32) * mix_ref[0].astype(F32)), axis=0, keepdims=True
    )
    scores = dot(k_ref[0], query, ((1,), (1,))) * SCALE
    probs = jnp.where(invalid, 0.0, jnp.exp(scores - lse_ref[0]))
    grad_probs = dot(v_ref[0], grad, ((1,), (1,)))
    grad_scores = (probs * (grad_probs - delta)).astype(BF16)
    dv_sum[...] += dot(probs.astype(BF16), grad)
    dk_sum[...] += dot(grad_scores, query)
    dq_ref[0] = (jnp.transpose(dot(turned_ref[...], grad_scores)) * SCALE).astype(BF16)

    @pl.when(step == pl.num_programs(1) - 1)
    def _():
        dk_ref[0] = (dk_sum[...] * SCALE).astype(BF16)
        dv_ref[0] = dv_sum[...].astype(BF16)


def attend_back(qkv, length, grad_mix, mix, lse):
    items, slots, _ = qkv.shape
    heads = items // 3
    block = 256
    part = jax.ShapeDtypeStruct((heads, slots, HEAD_DIM), BF16)
    per_block = pl.BlockSpec((1, block, HEAD_DIM), lambda h, i, n: (h, i, 0))
    per_head = pl.BlockSpec((1, slots, HEAD_DIM), lambda h, i, n: (h, 0, 0))
    return pl.pallas_call(
        functools.partial(attend_back_kernel, slots),
        grid_spec=pltpu.PrefetchScalarGridSpec(
            num_scalar_prefetch=1,
            grid=(heads, slots // block),
            in_specs=[
                per_block,
                pl.BlockSpec((1, slots, HEAD_DIM), lambda h, i, n: (heads + h, 0, 0)),
                pl.BlockSpec((1, slots, HEAD_DIM), lambda h, i, n: (2 * heads + h, 0, 0)),
                per_block,
                per_block,
                pl.BlockSpec((1, 1, block), lambda h, i, n: (h, 0, i)),
            ],
            out_specs=[per_block, per_head, per_head],
            scratch_shapes=[
                pltpu.VMEM((HEAD_DIM, slots), BF16),
                pltpu.VMEM((slots, HEAD_DIM), F32),
                pltpu.VMEM((slots, HEAD_DIM), F32),
            ],
        ),
        out_shape=[part, part, part],
        compiler_params=params(),
        name="attend_back",
    )(length, qkv, qkv, qkv, grad_mix, mix, lse)


def feed_kernel(
    place_ref, x_ref, mix_ref, cot_ref, wo_ref, w1_ref, w2_ref, bo_ref, gain_ref, shift_ref, b1_ref,
    out_ref, ds_ref, second_ref, act_ref, de_ref, middle_ref, gain_sum, shift_sum, b1_sum,
):
    step = pl.program_id(0)
    count = pl.num_programs(0)
    block = x_ref.shape[0]
    owner = lax.rem(place_ref[0] + 1 + step, count)

    @pl.when(step == 0)
    def _():
        gain_sum[...] = jnp.zeros_like(gain_sum)
        shift_sum[...] = jnp.zeros_like(shift_sum)
        b1_sum[...] = jnp.zeros_like(b1_sum)

    middle = x_ref[...].astype(F32) + (dot(mix_ref[...], wo_ref[...]) + bo_ref[...])
    middle_ref[...] = middle
    unit, _ = normalize(middle)
    second = (unit * gain_ref[...] + shift_ref[...]).astype(BF16)
    second_ref[...] = second
    valid = owner * block + lax.broadcasted_iota(jnp.int32, (block, 1), 0) < place_ref[1]
    grad_two = jnp.where(valid, cot_ref[...].astype(F32), 0.0).astype(BF16)
    expanded = dot(second, w1_ref[...]) + b1_ref[...]
    phi = 0.5 * (1.0 + lax.erf(expanded * (0.5**0.5)))
    activated = (expanded * phi).astype(BF16)
    act_ref[...] = activated
    slope = phi + expanded * (jnp.exp(-0.5 * expanded * expanded) * 0.3989422804014327)
    out_ref[...] = dot(activated, w2_ref[...]).astype(BF16)
    grad_act = dot(grad_two, w2_ref[...], ((1,), (1,)))
    grad_expanded = (grad_act * slope).astype(BF16)
    de_ref[...] = grad_expanded
    b1_sum[...] += jnp.sum(grad_expanded.astype(F32), axis=0, keepdims=True)
    grad_second = dot(grad_expanded, w1_ref[...], ((1,), (1,)))
    ds_ref[...] = grad_second.astype(BF16)
    gain_sum[...] += jnp.sum(grad_second * unit, axis=0, keepdims=True)
    shift_sum[...] += jnp.sum(grad_second, axis=0, keepdims=True)


def feed(place, count, x, mix, cot, wo, w1, w2, bo, gain, shift, b1):
    slots = x.shape[0]
    block = slots // count
    width = w1.shape[1]

    def turn(i, place):
        return lax.rem(place[0] + 1 + i, count)

    rows = pl.BlockSpec((block, D), lambda i, p: (turn(i, p), 0))
    wide = pl.BlockSpec((block, width), lambda i, p: (turn(i, p), 0))
    return pl.pallas_call(
        feed_kernel,
        grid_spec=pltpu.PrefetchScalarGridSpec(
            num_scalar_prefetch=1,
            grid=(count,),
            in_specs=[rows, rows, rows, whole(wo.shape), whole(w1.shape), whole(w2.shape)]
            + [whole((1, D))] * 3
            + [whole((1, width))],
            out_specs=[
                rows,
                rows,
                rows,
                wide,
                wide,
                pl.BlockSpec((block, D), lambda i, p: (0, 0)),
                pl.BlockSpec((1, D), lambda i, p: (0, 0)),
                pl.BlockSpec((1, D), lambda i, p: (0, 0)),
                pl.BlockSpec((1, width), lambda i, p: (0, 0)),
            ],
        ),
        out_shape=[
            jax.ShapeDtypeStruct((slots, D), BF16),
            jax.ShapeDtypeStruct((slots, D), BF16),
            jax.ShapeDtypeStruct((slots, D), BF16),
            jax.ShapeDtypeStruct((slots, width), BF16),
            jax.ShapeDtypeStruct((slots, width), BF16),
            jax.ShapeDtypeStruct((block, D), F32),
            jax.ShapeDtypeStruct((1, D), F32),
            jax.ShapeDtypeStruct((1, D), F32),
            jax.ShapeDtypeStruct((1, width), F32),
        ],
        compiler_params=params(),
        name="feed",
    )(place, x, mix, cot, wo, w1, w2, bo, gain, shift, b1)


def gather(value, axes, axis=0):
    return lax.all_gather(value, axes, axis=axis, tiled=True)


def scatter_sum(value, axes, axis=0):
    return lax.psum_scatter(value, axes, scatter_dimension=axis, tiled=True)


def per_device(
    hidden_in, cotangent, clip_lengths, clip_order, first_gain, first_shift, query_weight,
    query_bias, key_weight, value_weight, value_bias, output_weight, output_bias, second_gain,
    second_shift, expand_weight, expand_bias, reduce_weight, reduce_bias,
):
    dp = lax.axis_size("dp")
    seq = lax.axis_size("seq")
    me = lax.axis_index("seq")
    rows_here = hidden_in.shape[1]
    slots = rows_here * seq
    share = D // dp
    head_cols = D // seq
    heads = HEADS // seq
    units = FF // (dp * seq)
    quarter = dp * units

    hidden_own = hidden_in[0]
    matches = clip_order[0] == jnp.arange(clip_lengths.shape[0], dtype=jnp.int32)
    length = jnp.sum(jnp.where(matches, clip_lengths, 0)).reshape(1)

    def columns(weight):
        return lax.dynamic_slice_in_dim(weight, me * head_cols, head_cols, 1)

    small = jnp.concatenate(
        [first_gain, first_shift, query_bias, value_bias, output_bias, second_gain, second_shift,
         reduce_bias, expand_bias]
    )
    width = 3 * head_cols
    extra = -(-small.shape[0] // width)
    tall = -(-(share + extra) // 16) * 16
    small = jnp.pad(small, (0, (tall - share) * width - small.shape[0])).reshape(-1, width)
    qkv_share = jnp.concatenate(
        [columns(query_weight), columns(key_weight), columns(value_weight)], axis=1
    )
    packed = gather(jnp.concatenate([qkv_share, small], axis=0), "dp").reshape(dp, tall, width)
    w_qkv = packed[:, :share].reshape(D, width)
    flat = packed[:, share : share + extra].reshape(dp, extra * width)

    def vector(index, size=share):
        return flat[:, index * share : index * share + size].reshape(1, dp * size).astype(F32)

    gain_one, shift_one, bias_query, bias_value, bias_out, gain_two, shift_two, bias_reduce = (
        vector(i) for i in range(8)
    )
    expand_all = flat[:, 8 * share : 8 * share + FF // dp]
    bias_expand = lax.dynamic_slice_in_dim(expand_all, me * units, units, 1)
    bias_expand = bias_expand.reshape(1, quarter).astype(F32)
    bias_qkv = jnp.concatenate(
        [columns(bias_query), jnp.zeros((1, head_cols), F32), columns(bias_value)], axis=1
    )

    x = gather(hidden_own, "seq")
    cot = gather(cotangent[0], "seq")
    wo_share = lax.dynamic_slice_in_dim(output_weight, me * (share // seq), share // seq, 0)
    w_out = gather(wo_share, ("dp", "seq"))
    w1_share = jnp.concatenate(
        [
            lax.dynamic_slice_in_dim(expand_weight, d * (FF // dp) + me * units, units, 1)
            for d in range(dp)
        ],
        axis=1,
    )
    w2_share = lax.dynamic_slice_in_dim(reduce_weight, me * units, units, 0)
    w_expand = gather(w1_share, "dp")
    w_reduce = gather(w2_share, "dp")

    normed, qkv = project(x, w_qkv, gain_one, shift_one, bias_qkv)
    mix_own, lse = attend(qkv, length)
    mix = gather(mix_own, "seq", axis=1)
    place = jnp.stack([me.astype(jnp.int32), length[0]])
    (
        out_part, ds_part, second, act, grad_expanded, middle_own, gain_two_grad, shift_two_grad,
        bias_expand_grad,
    ) = feed(
        place, seq, x, mix, cot, w_out, w_expand, w_reduce, bias_out, gain_two, shift_two,
        bias_expand,
    )
    positions = jnp.arange(slots, dtype=jnp.int32)
    valid = (positions < length)[:, None]
    grad_two = jnp.where(valid, cot, 0).astype(BF16)
    grad_out = lax.dynamic_slice_in_dim(grad_two, me * rows_here, rows_here, 0).astype(F32)

    layer_output = (
        middle_own + (scatter_sum(out_part, "seq").astype(F32) + bias_reduce)
    ).astype(BF16)
    grad_second = scatter_sum(ds_part, "seq").astype(F32)
    unit_two, spread_two = normalize(middle_own)
    grad_middle = grad_out + norm_backward(unit_two, spread_two, grad_second * gain_two)
    grad_branch = grad_middle.astype(BF16)
    reduce_bias_grad = jnp.sum(grad_out, axis=0)
    output_bias_grad = jnp.sum(grad_branch.astype(F32), axis=0)

    w1_grad = dot(second, grad_expanded, ((0,), (0,))).astype(BF16)
    w2_grad = dot(act, grad_two, ((0,), (0,))).astype(BF16)
    w1_grad = scatter_sum(w1_grad, "dp")
    w2_grad = scatter_sum(w2_grad, "dp")

    grad_branch_all = gather(grad_branch, "seq")
    wo_grad = dot(mix, columns(grad_branch_all), ((0,), (0,))).astype(BF16)
    wo_rows = lax.dynamic_slice_in_dim(w_out, me * head_cols, head_cols, 0)
    grad_mix = dot(grad_branch_all, wo_rows, ((1,), (1,))).astype(BF16)

    def split_heads(value):
        return value.reshape(slots, heads, HEAD_DIM).transpose(1, 0, 2)

    dq, dk, dv = attend_back(qkv, length, split_heads(grad_mix), split_heads(mix_own), lse)
    dqkv = jnp.concatenate([dq, dk, dv], axis=0).transpose(1, 0, 2).reshape(slots, width)
    qkv_grad = dot(normed, dqkv, ((0,), (0,))).astype(BF16)
    bias_qkv_grad = jnp.sum(dqkv.astype(F32), axis=0)
    grad_normed = dot(dqkv, w_qkv, ((1,), (1,)))
    unit_all, _ = normalize(x.astype(F32))
    gain_one_grad = jnp.sum(grad_normed * unit_all, axis=0)
    shift_one_grad = jnp.sum(grad_normed, axis=0)
    grad_normed_own = scatter_sum(grad_normed.astype(BF16), "seq").astype(F32)
    unit_one, spread_one = normalize(hidden_own.astype(F32))
    grad_front = grad_middle + norm_backward(unit_one, spread_one, grad_normed_own * gain_one)
    input_grad = grad_front.astype(BF16)

    def mine(value):
        return lax.dynamic_update_slice_in_dim(
            jnp.zeros((D,), F32), value.reshape(-1), me * head_cols, 0
        )

    expand_vec = lax.dynamic_update_slice_in_dim(
        jnp.zeros((dp, FF // dp), F32), bias_expand_grad.reshape(dp, units), me * units, 1
    )
    vectors = [
        gain_one_grad, shift_one_grad, mine(bias_qkv_grad[:head_cols]),
        mine(bias_qkv_grad[2 * head_cols :]), output_bias_grad, gain_two_grad.reshape(-1),
        shift_two_grad.reshape(-1), reduce_bias_grad,
    ]
    small_grad = jnp.concatenate([v.reshape(dp, share) for v in vectors] + [expand_vec], axis=1)
    small_grad = jnp.pad(
        small_grad.astype(BF16), ((0, 0), (0, (tall - share) * width - small_grad.shape[1]))
    ).reshape(dp, tall - share, width)
    packed_grad = jnp.concatenate([qkv_grad.reshape(dp, share, width), small_grad], axis=1)
    packed_grad = scatter_sum(packed_grad, "dp")[0]
    wo_grad = scatter_sum(wo_grad, "dp")

    packed_grad = gather(packed_grad[None], "seq")
    wo_grad = gather(wo_grad[None], "seq")
    w1_grad = gather(w1_grad[None], "seq")
    w2_grad = gather(w2_grad, "seq").astype(F32)
    w1_grad = (
        w1_grad.reshape(seq, share, dp, units).transpose(1, 2, 0, 3).reshape(share, FF).astype(F32)
    )
    wo_grad = wo_grad.transpose(1, 0, 2).reshape(share, D).astype(F32)
    qkv_grad = packed_grad[:, :share].reshape(seq, share, 3, head_cols).astype(F32)
    qkv_grad = qkv_grad.transpose(2, 1, 0, 3).reshape(3, share, D)
    small_grad = jnp.sum(
        packed_grad[:, share : share + extra].reshape(seq, extra * width).astype(F32), axis=0
    )
    pieces = [small_grad[i * share : (i + 1) * share] for i in range(8)]
    expand_bias_grad = small_grad[8 * share : 8 * share + FF // dp]
    return (
        layer_output[None],
        input_grad[None],
        pieces[0],
        pieces[1],
        qkv_grad[0],
        pieces[2],
        qkv_grad[1],
        qkv_grad[2],
        pieces[3],
        wo_grad,
        pieces[4],
        pieces[5],
        pieces[6],
        w1_grad,
        expand_bias_grad,
        w2_grad,
        pieces[7],
    )


def solution(mesh):
    clip = P("dp", "seq", None)
    vec = P("dp")
    mat = P("dp", None)
    return jax.shard_map(
        per_device,
        mesh=mesh,
        in_specs=(
            clip, clip, P(), vec, vec, vec, mat, vec, mat, mat, vec, mat, vec, vec, vec, mat, vec,
            mat, vec,
        ),
        out_specs=(
            clip, clip, vec, vec, mat, vec, mat, mat, vec, mat, vec, vec, vec, mat, vec, mat, vec,
        ),
        check_vma=False,
    )
```

time: 1650 us -> 1000 us (0.61)
  waiting for transfers between devices: 903 us -> 664 us
  matrix products: 223 us -> 48.4 us
  blocking collectives: 165 us -> 7.16 us
  Pallas kernels: 0 us -> 110 us
  local copies, waits for them, and re-layouts: 185 us -> 98.2 us
  other arithmetic: 126 us -> 48 us
  starting transfers between devices: 21.8 us -> 1.34 us
    dot_general x39 -> x6, matrix products: 223 us -> 48.4 us  [dot(): lax.dot_general(left, right, (contract, ((), ())), preferred_element_type...]
    reduce_scatter x6 -> x7, waiting for transfers between devices: 475 us -> 301 us  [scatter_sum(): return lax.psum_scatter(value, axes, scatter_dimension=axis, tiled=True)]
    pallas_call x0 -> x4, Pallas kernels: none -> 110 us  [the longest x1 36.8 us: feed(): pl.pallas_call(feed_kernel, grid_spec=pltpu.PrefetchScalarGridSpec(num_sc...]
    psum x1 -> x0, waiting for transfers between devices: 85.7 us -> none  [per_device(): lax.psum(attention_shards[2].astype(jnp.bfloat16), 'seq')]
    unnamed x198 -> x20, local copies, waits for them, and re-layouts: 82.3 us -> 1.23 us
    unnamed x2 -> x0, blocking collectives: 77.2 us -> none
    unnamed x10 -> x0, other arithmetic: 73 us -> none
    all_to_all x3 -> x0, blocking collectives: 50.6 us -> none  [the longest x1 17.2 us: per_device(): lax.all_to_all(grad_value_heads.reshape(flat_shape), 'seq', split_axis=1,...]
  transfers between devices with their start and end apart: 18 -> 18, of which waited for: 11 -> 16; matrix products, arithmetic and copies ran while one was open for 27% -> 17% of each run, Pallas kernels for 0% -> 4%
where the time goes in v1:
time: 1000 us; the launch traced here: 993 us
  waiting for transfers between devices  664 us (66%)
  Pallas kernels  110 us (11%)
  local copies, waits for them, and re-layouts  98.2 us (10%)
  matrix products  48.4 us (5%)
  other arithmetic  48 us (5%)
  between operations  15.7 us (2%)
    all_gather x11, waiting for transfers between devices, gather(): return lax.all_gather(value, axes, axis=axis, tiled=True)  360 us
    reduce_scatter x7, waiting for transfers between devices, scatter_sum(): return lax.psum_scatter(value, axes, scatter_dimension=axis, tiled=True)  301 us
    dot_general x6, matrix products, dot(): lax.dot_general(left, right, (contract, ((), ())), preferred_element_type...  48.4 us
    pallas_call x1, Pallas kernels, feed(): pl.pallas_call(feed_kernel, grid_spec=pltpu.PrefetchScalarGridSpec(num_sc...  36.8 us
    pallas_call x1, Pallas kernels, attend_back(): pl.pallas_call(functools.partial(attend_back_kernel, slots), grid_spec=pl...  36.6 us
    pallas_call x1, Pallas kernels, attend(): pl.pallas_call(functools.partial(attend_kernel, heads, slots), grid_spec=...  25.5 us
    convert_element_type x3, local copies, waits for them, and re-layouts, per_device(): w1_grad.reshape(seq, share, dp, units).transpose(1, 2, 0, 3)  22.2 us
  transfers between devices with their start and end apart: 18, of which 16 were waited for; matrix products, arithmetic and copies ran while one was open for 17% of the time, Pallas kernels for 4%

profile of v1, /device:TPU:0, one launch (start us, length us, event | category | flops | bytes accessed | tf_op | source)
XLA Modules:
  0.0 992.8 jit_solution(14501467054794672167)
XLA Ops:
  19.7 58.0 %all-gather.16.cloned.1.call-done = bf16[1408,960]{1,0:T(8,128)(2,1)} async-done(((bf16[176,960]{1,0:T(8,128)(2,1)}), bf16[1408,960]{1,0:T(8,128)(2,1)}) %all-gather.16.cloned.1.call-update) | async-done | bytes 2703376 | tf_op jit(solution)/shard_map/all_gather | solution.py:283
  84.5 26.4 %all-gather.32.cloned.1.call-done = bf16[1,1536,1280]{2,1,0:T(8,128)(2,1)} async-done(((bf16[1,384,1280]{2,1,0:T(8,128)(2,1)}), bf16[1,1536,1280]{2,1,0:T(8,128)(2,1)}) %all-gather.32.cloned.1.call-update) | async-done | bytes 3932176 | tf_op jit(solution)/shard_map/all_gather | solution.py:283
  110.9 11.3 %project.1 = (bf16[1536,1280]{1,0:T(8,128)(2,1)}, bf16[12,1536,80]{2,1,0:T(8,128)(2,1)}) custom-call(bf16[1536,1280]{1,0:T(8,128)(2,1)} %bitcast.68, bf16[1280,960]{1,0:T(8,128)(2,1)} %bitcast.73, f32[1,1280]{1,0:T(1,128)} %reshape.322.gain_ref, f32[1,1280]{1,0:T(1,128)} %reshape.323.shift_ref, f32[1,960]{1,0:T(1,128)} %pad_maximum_fusion.2.bias_ref), custom_call_target="tpu_custom_call" | custom-call | tf_op jit(solution)/shard_map/project/pallas_call | solution.py:59
  122.3 25.5 %attend.1 = (bf16[1536,320]{1,0:T(8,128)(2,1)}, f32[4,1,1536]{2,1,0:T(1,128)}) custom-call(s32[1]{0:T(128)} %bitcast.2.length_ref, bf16[12,1536,80]{2,1,0:T(8,128)(2,1)} %get-tuple-element.33.q_ref.k_ref.v_ref, bf16[12,1536,80]{2,1,0:T(8,128)(2,1)} %get-tuple-element.33.q_ref.k_ref.v_ref, bf16[12,1536,80]{2,1,0:T(8,128)(2,1)} %get-tuple-element.33.q_ref.k_ref.v_ref), custom_call_target="tpu_custom_call" | custom-call | tf_op jit(solution)/shard_map/attend/pallas_call | solution.py:107
  160.1 23.2 %all-gather.18.cloned.1.call-done = bf16[1536,1280]{0,1:T(8,128)(2,1)} async-done(((bf16[1536,320]{0,1:T(8,128)(2,1)}), bf16[1536,1280]{0,1:T(8,128)(2,1)}) %all-gather.18.cloned.1.call-update) | async-done | bytes 3932176 | tf_op jit(solution)/shard_map/all_gather | solution.py:283
  189.6 57.8 %all-gather.22.cloned.1.call-done.w1_ref = bf16[1280,1280]{1,0:T(8,128)(2,1)} async-done(((bf16[160,1280]{1,0:T(8,128)(2,1)}), bf16[1280,1280]{1,0:T(8,128)(2,1)}) %all-gather.22.cloned.1.call-update) | async-done | bytes 3276816 | tf_op jit(solution)/shard_map/all_gather | solution.py:283
  247.3 62.8 %all-gather.24.cloned.1.call-done.w2_ref = bf16[1280,1280]{1,0:T(8,128)(2,1)} async-done(((bf16[160,1280]{1,0:T(8,128)(2,1)}), bf16[1280,1280]{1,0:T(8,128)(2,1)}) %all-gather.24.cloned.1.call-update) | async-done | bytes 3276816 | tf_op jit(solution)/shard_map/all_gather | solution.py:283
  310.1 33.1 %all-gather.34.cloned.1.call-done = bf16[1,1536,1280]{2,1,0:T(8,128)(2,1)} async-done(((bf16[1,384,1280]{2,1,0:T(8,128)(2,1)}), bf16[1,1536,1280]{2,1,0:T(8,128)(2,1)}) %all-gather.34.cloned.1.call-update) | async-done | bytes 3932176 | tf_op jit(solution)/shard_map/all_gather | solution.py:283
  343.2 63.0 %all-gather.20.cloned.1.call-done.wo_ref = bf16[1280,1280]{1,0:T(8,128)(2,1)} async-done(((bf16[40,1280]{1,0:T(8,128)(2,1)}), bf16[1280,1280]{1,0:T(8,128)(2,1)}) %all-gather.20.cloned.1.call-update) | async-done | bytes 3276816 | tf_op jit(solution)/shard_map/all_gather | solution.py:283
  406.2 36.8 %feed.1 = (bf16[1536,1280]{1,0:T(8,128)(2,1)}, bf16[1536,1280]{1,0:T(8,128)(2,1)}, bf16[1536,1280]{1,0:T(8,128)(2,1)}, bf16[1536,1280]{1,0:T(8,128)(2,1)}, bf16[...) custom-call(s32[2]{0:T(128)} %pad_add_fusion.place_ref, ...), custom_call_target="tpu_custom_call" | custom-call | tf_op jit(solution)/shard_map/feed/pallas_call | solution.py:246
  453.0 31.7 %reduce-scatter.10.cloned.1.call-done = bf16[384,1280]{1,0:T(8,128)(2,1)} async-done(((bf16[1536,1280]{1,0:T(8,128)(2,1)}), bf16[384,1280]{1,0:T(8,128)(2,1)}) %reduce-scatter.10.cloned.1.call-update) | async-done | bytes 983056 | tf_op jit(solution)/shard_map/reduce_scatter | solution.py:287
  484.7 45.5 %reduce-scatter.8.cloned.1.call-done = bf16[384,1280]{1,0:T(8,128)(2,1)} async-done(((bf16[1536,1280]{1,0:T(8,128)(2,1)}), bf16[384,1280]{1,0:T(8,128)(2,1)}) %reduce-scatter.8.cloned.1.call-update) | async-done | bytes 983056 | tf_op jit(solution)/shard_map/reduce_scatter | solution.py:287
  538.4 9.4 convolution_convert_fusion.1
  548.0 9.4 convolution_convert_fusion
  576.8 36.6 %attend_back.1 = (bf16[4,1536,80]{2,1,0:T(8,128)(2,1)}, bf16[4,1536,80]{2,1,0:T(8,128)(2,1)}, bf16[4,1536,80]{2,1,0:T(8,128)(2,1)}) custom-call(s32[1]{0:T(128)} %bitcast.2.length_ref, bf16[12,1536,80]{2,1,0:T(8,128)(2,1)} %get-tuple-element.33.q_ref.k_ref.v_ref, bf16[12,1536,80]{2,1,0:T(8,128)(2,1)} %get-tuple-element.33.q_ref.k_ref.v_ref, ...), custom_call_target="tpu_custom_call" | custom-call | tf_op jit(solution)/shard_map/attend_back/pallas_call | solution.py:172
  625.8 8.6 convolution_convert_fusion.2
  639.0 11.3 %fusion.26 = (bf16[1280]{0:T(1024)(128)(2,1)S(1)}, bf16[1280]{0:T(1024)(128)(2,1)S(1)}, bf16[1536,1280]{1,0:T(8,128)(2,1)}) fusion(f32[1536]{0:T(1024)S(1)} %add_rsqrt_fusion, f32[1536]{0:T(1024)S(1)} %broadcast_multiply_fusion, bf16[1,1536,1280]{2,1,0:T(8,128)(2,1)} %all-gather.32.cloned.1.call-done, bf16[1536,960]{0,1:T(8,128)(2,1)} %bitcast.80, ...), kind=kOutput, calls=%fused_computation.90 | convolution fusion | flops 3788633600 | bytes 13288448 | tf_op jit(solution)/shard_map/dot_general | solution.py:22
  656.2 74.4 %reduce-scatter.20.cloned.1.call-done = bf16[160,1280]{1,0:T(8,128)(2,1)} async-done(((bf16[1280,1280]{1,0:T(8,128)(2,1)}), bf16[160,1280]{1,0:T(8,128)(2,1)}) %reduce-scatter.20.cloned.1.call-update) | async-done | bytes 409616 | tf_op jit(solution)/shard_map/reduce_scatter | solution.py:287
  736.7 68.8 %reduce-scatter.14.cloned.1.call-done = bf16[1,176,960]{2,1,0:T(8,128)(2,1)} async-done(((bf16[8,176,960]{2,1,0:T(8,128)(2,1)}), bf16[1,176,960]{2,1,0:T(8,128)(2,1)}) %reduce-scatter.14.cloned.1.call-update) | async-done | bytes 337936 | tf_op jit(solution)/shard_map/reduce_scatter | solution.py:287
  806.8 19.4 %all-gather.36.cloned.1.call-done = bf16[640,1280]{1,0:T(8,128)(2,1)} async-done(((bf16[160,1280]{1,0:T(8,128)(2,1)}), bf16[640,1280]{1,0:T(8,128)(2,1)}) %all-gather.36.cloned.1.call-update) | async-done | bytes 1638416 | tf_op jit(solution)/shard_map/all_gather | solution.py:283
  832.3 8.5 copy.77
  851.8 63.7 %reduce-scatter.16.cloned.1.call-done = bf16[160,320]{1,0:T(8,128)(2,1)} async-done(((bf16[1280,320]{1,0:T(8,128)(2,1)}), bf16[160,320]{1,0:T(8,128)(2,1)}) %reduce-scatter.16.cloned.1.call-update) | async-done | bytes 102416 | tf_op jit(solution)/shard_map/reduce_scatter | solution.py:287
  924.8 9.9 all-gather.28.cloned.1.call-done
  963.1 16.9 %reduce-scatter.12.cloned.1.call-done = bf16[384,1280]{1,0:T(8,128)(2,1)} async-done(((bf16[1536,1280]{1,0:T(8,128)(2,1)}), bf16[384,1280]{1,0:T(8,128)(2,1)}) %reduce-scatter.12.cloned.1.call-update) | async-done | bytes 983056 | tf_op jit(solution)/shard_map/reduce_scatter | solution.py:287
  (169 shorter events, 165.0 us)
Async XLA Ops:
  7.2 145.8 %copy-start = (bf16[640,1280]{1,0:T(8,128)(2,1)S(1)}, bf16[640,1280]{1,0:T(8,128)(2,1)}, u32[]{:S(2)}) copy-start(bf16[640,1280]{1,0:T(8,128)(2,1)} %param.36) | copy-start | bytes 4915204
  7.2 11.9 %copy-start.9 = (s32[8]{0:T(128)S(1)}, s32[8]{0:T(128)}, u32[]{:S(2)}) copy-start(s32[8]{0:T(128)} %param.21) | copy-start | bytes 100
  7.2 70.5 %all-gather.16.cloned.1.call-start = ((), (), s32[]{:S(2)}) async-start(), calls=%async_computation.7 | async-start | bytes 3244032 | tf_op jit(solution)/shard_map/all_gather | solution.py:283
  17.6 93.4 %all-gather.32.cloned.1.call-start = ((), (), s32[]{:S(2)}) async-start(), calls=%async_computation.22 | async-start | bytes 4915200 | tf_op jit(solution)/shard_map/all_gather | solution.py:283
  18.3 164.9 %all-gather.18.cloned.1.call-start = ((), (), s32[]{:S(2)}) async-start(), calls=%async_computation.8 | async-start | bytes 4915200 | tf_op jit(solution)/shard_map/all_gather | solution.py:283
  150.1 97.2 %all-gather.22.cloned.1.call-start = ((), (), s32[]{:S(2)}) async-start(), calls=%async_computation.10 | async-start | bytes 3686400 | tf_op jit(solution)/shard_map/all_gather | solution.py:283
  152.9 157.2 %all-gather.24.cloned.1.call-start = ((), (), s32[]{:S(2)}) async-start(), calls=%async_computation.11 | async-start | bytes 3686400 | tf_op jit(solution)/shard_map/all_gather | solution.py:283
  153.8 189.5 %all-gather.34.cloned.1.call-start = ((), (), s32[]{:S(2)}) async-start(), calls=%async_computation.23 | async-start | bytes 4915200 | tf_op jit(solution)/shard_map/all_gather | solution.py:283
  154.4 251.9 %all-gather.20.cloned.1.call-start = ((), (), s32[]{:S(2)}) async-start(), calls=%async_computation.9 | async-start | bytes 3379200 | tf_op jit(solution)/shard_map/all_gather | solution.py:283
  156.0 328.7 %reduce-scatter.10.cloned.1.call-start = ((), (), s32[]{:S(2)}) async-start(), calls=%async_computation.13 | async-start | bytes 4915200 | tf_op jit(solution)/shard_map/reduce_scatter | solution.py:287
  443.0 87.2 %reduce-scatter.8.cloned.1.call-start = ((), (), s32[]{:S(2)}) async-start(), calls=%async_computation.12 | async-start | bytes 4915200 | tf_op jit(solution)/shard_map/reduce_scatter | solution.py:287
  443.7 127.8 %all-gather.26.cloned.1.call-start = ((), (), s32[]{:S(2)}) async-start(), calls=%async_computation.14 | async-start | bytes 4915200 | tf_op jit(solution)/shard_map/all_gather | solution.py:283
  484.7 49.3 %copy-start.5 = (bf16[384,1280]{1,0:T(8,128)(2,1)S(1)}, bf16[384,1280]{1,0:T(8,128)(2,1)}, u32[]{:S(2)}) copy-start(bf16[384,1280]{1,0:T(8,128)(2,1)} %reduce-scatter.10.cloned.1.call-done) | copy-start | bytes 2949124
  538.4 117.3 %reduce-scatter.18.cloned.1.call-start = ((), (), s32[]{:S(2)}) async-start(), calls=%async_computation.19 | async-start | bytes 3686400 | tf_op jit(solution)/shard_map/reduce_scatter | solution.py:287
  547.9 182.8 %reduce-scatter.20.cloned.1.call-start = ((), (), s32[]{:S(2)}) async-start(), calls=%async_computation.20 | async-start | bytes 3686400 | tf_op jit(solution)/shard_map/reduce_scatter | solution.py:287
  557.4 248.1 %reduce-scatter.14.cloned.1.call-start = ((), (), s32[]{:S(2)}) async-start(), calls=%async_computation.16 | async-start | bytes 3244032 | tf_op jit(solution)/shard_map/reduce_scatter | solution.py:287
  560.2 3.3 copy-start.2
  655.6 170.6 %all-gather.36.cloned.1.call-start = ((), (), s32[]{:S(2)}) async-start(), calls=%async_computation.24 | async-start | bytes 2048000 | tf_op jit(solution)/shard_map/all_gather | solution.py:283
  656.2 192.2 %all-gather.30.cloned.1.call-start = ((), (), s32[]{:S(2)}) async-start(), calls=%async_computation.21 | async-start | bytes 2048000 | tf_op jit(solution)/shard_map/all_gather | solution.py:283
  730.7 184.8 %reduce-scatter.16.cloned.1.call-start = ((), (), s32[]{:S(2)}) async-start(), calls=%async_computation.18 | async-start | bytes 1105920 | tf_op jit(solution)/shard_map/reduce_scatter | solution.py:287
  736.6 69.5 %copy-start.3 = (bf16[1,384,1280]{2,1,0:T(8,128)(2,1)S(1)}, bf16[1,384,1280]{2,1,0:T(8,128)(2,1)}, u32[]{:S(2)}) copy-start(bf16[1,384,1280]{2,1,0:T(8,128)(2,1)} %param.19) | copy-start | bytes 2949124
  736.6 198.1 %all-gather.28.cloned.1.call-start = ((), (), s32[]{:S(2)}) async-start(), calls=%async_computation.17 | async-start | bytes 1802240 | tf_op jit(solution)/shard_map/all_gather | solution.py:283
  805.5 174.5 %reduce-scatter.12.cloned.1.call-start = ((), (), s32[]{:S(2)}) async-start(), calls=%async_computation.15 | async-start | bytes 4915200 | tf_op jit(solution)/shard_map/reduce_scatter | solution.py:287
  980.1 5.5 copy-start.1
  (4 other events, 6.5 us)
Sparse Core Ops, SparseCore 0:
  17.7 60.0 all-gather.15
  79.3 31.5 all-gather.31
  150.3 32.9 all-gather.17
  185.9 61.4 all-gather.21
  249.9 60.1 all-gather.23
  311.5 31.6 all-gather.33
  346.6 59.5 all-gather.19
  443.1 41.4 reduce-scatter.9
  487.2 42.9 reduce-scatter.7
  538.5 32.9 all-gather.25
  575.7 76.1 reduce-scatter.17
  655.9 74.6 reduce-scatter.19
  734.2 71.2 reduce-scatter.13
  806.9 19.2 all-gather.35
  827.6 19.9 all-gather.29
  851.4 64.0 reduce-scatter.15
  916.9 17.8 all-gather.27
  937.1 42.8 reduce-scatter.11

commit v2 on v1

v2 whole, which is shorter than its diff:
```python
import functools

import jax
import jax.numpy as jnp
from jax import lax
from jax.experimental import pallas as pl
from jax.experimental.pallas import tpu as pltpu
from jax.sharding import PartitionSpec as P

D = 1280
FF = 5120
HEADS = 16
HEAD_DIM = D // HEADS
EPSILON = 1e-05
SCALE = HEAD_DIM ** (-0.5)
F32 = jnp.float32
BF16 = jnp.bfloat16
VMEM_LIMIT = 60 * 1024 * 1024
MESH = pl.DeviceIdType.MESH


def dot(left, right, contract=((1,), (0,))):
    return lax.dot_general(left, right, (contract, ((), ())), preferred_element_type=F32)


def normalize(values):
    average = jnp.mean(values, axis=-1, keepdims=True)
    centered = values - average
    variance = jnp.mean(centered * centered, axis=-1, keepdims=True)
    spread = lax.rsqrt(variance + EPSILON)
    return centered * spread, spread


def norm_backward(unit, spread, grad_unit):
    inner = jnp.mean(grad_unit * unit, axis=-1, keepdims=True)
    return spread * (grad_unit - jnp.mean(grad_unit, axis=-1, keepdims=True) - unit * inner)


def params(**extra):
    return pltpu.CompilerParams(vmem_limit_bytes=VMEM_LIMIT, **extra)


def whole(shape):
    return pl.BlockSpec(shape, lambda *_: (0,) * len(shape), pipeline_mode=pl.Buffered(1))


def chunk_of(slots):
    return slots // 4 if slots % 512 == 0 else slots


class Place:
    def __init__(self, dp, seq):
        self.dp, self.seq = dp, seq
        self.xs = 1 << ((dp.bit_length() - 1) // 2)
        self.zs = dp // self.xs
        self.ys = seq // 2

    def locate(self):
        self.d, self.s = lax.axis_index("dp"), lax.axis_index("seq")
        self.z, self.x = self.d // self.xs, lax.rem(self.d, self.xs)
        self.y, self.c = self.s // 2, lax.rem(self.s, 2)
        self.partner = self.y * 2 + 1 - self.c

    def at_z(self, k):
        return lax.rem(self.z + k + self.zs, self.zs) * self.xs + self.x

    def block(self, k, j):
        return lax.rem(self.z - k + self.zs, self.zs) * self.xs + lax.rem(
            self.x - j + self.xs, self.xs
        )

    def at_x(self, j):
        return self.z * self.xs + lax.rem(self.x + j, self.xs)

    def at_y(self, j, core):
        return lax.rem(self.y + j + self.ys, self.ys) * 2 + core

    def peers(self, over_dp=True, over_seq=True):
        found = []
        if over_dp:
            found += [(self.at_z(k), self.s) for k in range(1, self.zs)]
            found += [(self.at_x(j), self.s) for j in range(1, self.xs)]
        if over_seq:
            found += [(self.d, self.partner)]
            found += [(self.d, self.at_y(j, self.c)) for j in range(1, self.ys)]
        return found

    def barrier(self, **which):
        semaphore = pltpu.get_barrier_semaphore()
        peers = self.peers(**which)
        for peer in peers:
            pl.semaphore_signal(semaphore, inc=1, device_id=peer, device_id_type=MESH)
        pl.semaphore_wait(semaphore, len(peers))


def send(src, dst, send_sem, recv_sem, device):
    return pltpu.make_async_remote_copy(
        src_ref=src, dst_ref=dst, send_sem=send_sem, recv_sem=recv_sem, device_id=device,
        device_id_type=MESH,
    )


def dp_semaphores(place, groups):
    return [
        pltpu.SemaphoreType.DMA((groups, place.zs)),
        pltpu.SemaphoreType.DMA((groups, place.zs)),
        pltpu.SemaphoreType.DMA((groups, place.zs, place.xs)),
        pltpu.SemaphoreType.DMA((groups, place.zs, place.xs)),
    ]


def seq_semaphores(place, groups):
    return [pltpu.SemaphoreType.DMA((groups, 2, place.ys))] * 2


class GatherDp:
    def __init__(self, place, group, sems, own, slab):
        self.p, self.g, self.own, self.slab = place, group, own, slab
        self.zsend, self.zrecv, self.xsend, self.xrecv = sems

    def z_copy(self, k):
        src = self.own
        return send(src, self.slab(self.p.d), self.zsend.at[self.g, k], self.zrecv.at[self.g, k],
                    (self.p.at_z(k), self.p.s))

    def x_copy(self, k, j):
        block = self.p.block(k, 0)
        src = self.own if k == 0 else self.slab(block)
        return send(src, self.slab(block), self.xsend.at[self.g, k, j],
                    self.xrecv.at[self.g, k, j], (self.p.at_x(j), self.p.s))

    def start(self):
        for j in range(1, self.p.xs):
            self.x_copy(0, j).start()
        for k in range(self.p.zs - 1, 0, -1):
            self.z_copy(k).start()

    def forward(self, k):
        place = self.p
        send(self.own, self.slab(place.block(k, 0)), self.zsend.at[self.g, k],
             self.zrecv.at[self.g, k], (place.at_z(k), place.s)).wait_recv()
        for j in range(1, place.xs):
            self.x_copy(k, j).start()

    def forward_all(self):
        for k in range(1, self.p.zs):
            self.forward(k)

    def arrive(self):
        place = self.p
        for k in range(place.zs):
            for j in range(1, place.xs):
                send(self.own, self.slab(place.block(k, j)), self.xsend.at[self.g, k, j],
                     self.xrecv.at[self.g, k, j], (place.at_x(j), place.s)).wait_recv()

    def drain(self):
        place = self.p
        for k in range(1, place.zs):
            self.z_copy(k).wait_send()
        for k in range(place.zs):
            for j in range(1, place.xs):
                self.x_copy(k, j).wait_send()


class GatherSeq:
    def __init__(self, place, group, sems, own, slab):
        self.p, self.g, self.own, self.slab = place, group, own, slab
        self.sends, self.recvs = sems

    def y_copy(self, j):
        place = self.p
        return send(self.own, self.slab(place.s), self.sends.at[self.g, 0, j],
                    self.recvs.at[self.g, 0, j], (place.d, place.at_y(j, place.c)))

    def core_copy(self, j):
        place = self.p
        block = place.at_y(-j, place.c)
        src = self.own if j == 0 else self.slab(block)
        return send(src, self.slab(block), self.sends.at[self.g, 1, j],
                    self.recvs.at[self.g, 1, j], (place.d, place.partner))

    def start(self):
        for j in range(1, self.p.ys):
            self.y_copy(j).start()
        self.core_copy(0).start()

    def arrive_y(self, j):
        place = self.p
        block = place.at_y(-j, place.c)
        send(self.own, self.slab(block), self.sends.at[self.g, 0, j], self.recvs.at[self.g, 0, j],
             (place.d, place.at_y(j, place.c))).wait_recv()
        self.core_copy(j).start()
        return block

    def arrive_core(self, j):
        place = self.p
        block = place.at_y(-j, 1 - place.c)
        send(self.own, self.slab(block), self.sends.at[self.g, 1, j], self.recvs.at[self.g, 1, j],
             (place.d, place.partner)).wait_recv()
        return block

    def drain(self):
        for j in range(1, self.p.ys):
            self.y_copy(j).wait_send()
        for j in range(self.p.ys):
            self.core_copy(j).wait_send()


LOG2E = 1.4426950408889634
QSCALE = SCALE * LOG2E


def front_kernel(
    place, length_ref, x_in, cot_in, sm_in, wq_in, wo_in, w1_in, w2_in,
    x_out, cot_out, sm_out, wq_out, wo_out, w1_out, w2_out, normed_out, qt_out, kt_out, k_out,
    v_out, mix_out, lse_ref,
    xs, nr, sm, wq, wt, qt, kt, vt, kn, vn, mix,
    zsend, zrecv, xsend, xrecv, ssend, srecv, local,
):
    place.locate()
    seq, rows = x_out.shape[0], x_out.shape[1]
    slots = seq * rows
    heads = k_out.shape[0]
    wide = heads * HEAD_DIM
    place.barrier()
    dp_sems = (zsend, zrecv, xsend, xrecv)
    seq_sems = (ssend, srecv)

    def over_dp(group, own, buffer):
        return GatherDp(place, group, dp_sems, own, lambda d: buffer.at[d])

    def over_seq(group, own, buffer):
        return GatherSeq(place, group, seq_sems, own, lambda s: buffer.at[s])

    g_sm = over_dp(0, sm_in, sm)
    g_wq = over_dp(1, wq_in, wq)
    g_wo = over_dp(2, wo_in, wo_out)
    g_w1 = over_dp(3, w1_in, w1_out)
    g_w2 = over_dp(4, w2_in, w2_out)
    g_x = over_seq(0, x_in, xs)
    g_cot = over_seq(1, cot_in, cot_out)

    locals_in = [
        pltpu.make_async_copy(x_in, xs.at[place.s], local.at[0]),
        pltpu.make_async_copy(sm_in, sm.at[place.d], local.at[1]),
        pltpu.make_async_copy(wq_in, wq.at[place.d], local.at[2]),
    ]
    own_blocks = [
        pltpu.make_async_copy(cot_in, cot_out.at[place.s], local.at[3]),
        pltpu.make_async_copy(wo_in, wo_out.at[place.d], local.at[4]),
        pltpu.make_async_copy(w1_in, w1_out.at[place.d], local.at[5]),
        pltpu.make_async_copy(w2_in, w2_out.at[place.d], local.at[6]),
    ]
    for copy in locals_in:
        copy.start()
    g_sm.start()
    g_x.start()
    g_wq.start()
    for copy in own_blocks:
        copy.start()

    column = lax.broadcasted_iota(jnp.int32, (slots, 1), 0)
    penalty = jnp.where(column >= length_ref[0], -1e30, 0.0).astype(BF16)
    ones_row = jnp.where(
        lax.broadcasted_iota(jnp.int32, (128 - HEAD_DIM, slots), 0) == 0, 1.0, 0.0
    ).astype(BF16)
    for head in range(heads):
        kn[head] = jnp.zeros((slots, 128), BF16)
        kn[head, :, HEAD_DIM : HEAD_DIM + 1] = penalty
        qt[head, HEAD_DIM:, :] = ones_row

    for copy in locals_in:
        copy.wait()
    g_sm.forward_all()
    g_wq.forward_all()
    g_wo.start()
    g_w1.start()
    g_cot.start()
    g_sm.arrive()
    vectors = jnp.sum(sm[...].astype(F32), axis=0)
    gain, shift = vectors[0:1], vectors[1:2]

    def norm_block(block):
        unit, _ = normalize(xs[block].astype(F32))
        lines = pl.ds(pl.multiple_of(block * rows, 16), rows)
        nr[lines, :] = (unit * gain + shift).astype(BF16)

    norm_block(place.s)
    norm_block(g_x.arrive_core(0))
    for j in range(1, place.ys):
        norm_block(g_x.arrive_y(j))
        norm_block(g_x.arrive_core(j))
    g_wq.arrive()
    share = wq.shape[1]
    wt[...] = jnp.transpose(wq[...].reshape(place.dp * share, 3 * wide))
    bias = jnp.transpose(vectors[8:16])

    chunk = chunk_of(slots)

    def project_block(block, _):
        cols = pl.ds(pl.multiple_of(block * chunk, 128), chunk)
        lines = pl.ds(pl.multiple_of(block * chunk, 128), chunk)
        tokens = dot(wt[...], nr[lines, :], ((1,), (1,)))
        query = (tokens[:wide] + bias[:wide, 0:1]).astype(BF16)
        key = tokens[wide : 2 * wide].astype(BF16)
        value = (tokens[2 * wide :] + bias[:wide, 1:2]).astype(BF16)
        for head in range(heads):
            part = slice(head * HEAD_DIM, (head + 1) * HEAD_DIM)
            qt[head, :HEAD_DIM, cols] = query[part]
            kt[head, :, cols] = key[part]
            vt[head, :, cols] = value[part]
            kn[head, lines, :HEAD_DIM] = jnp.transpose(key[part])
            vn[head, lines, :] = jnp.transpose(value[part])
        return 0

    lax.fori_loop(0, slots // chunk, project_block, 0)
    results = [
        pltpu.make_async_copy(src, dst, local.at[7 + i])
        for i, (src, dst) in enumerate(
            [(xs, x_out), (sm, sm_out), (wq, wq_out), (nr, normed_out), (qt, qt_out), (kt, kt_out),
             (kn, k_out), (vn, v_out)]
        )
    ]
    for copy in results:
        copy.start()

    block = 256

    def attend(head):
        def one(i, _):
            cols = pl.ds(pl.multiple_of(i * block, 128), block)
            scores = dot(kn[head], qt[head, :, cols])
            top = jnp.max(scores, axis=0, keepdims=True)
            exponent = jnp.exp2((scores - top) * QSCALE)
            total = jnp.sum(exponent, axis=0, keepdims=True)
            mixed = dot(vt[head], exponent.astype(BF16)) / total
            mix[place.s, head, :, cols] = mixed.astype(BF16)
            lse_ref[head, :, cols] = top * QSCALE + jnp.log2(total)
            return 0

        lax.fori_loop(0, slots // block, one, 0)

    g_mix = [
        GatherSeq(place, 2 + head, seq_sems, mix.at[place.s, head],
                  lambda s, head=head: mix.at[s, head])
        for head in range(heads)
    ]
    for head in range(heads):
        attend(head)
        g_mix[head].start()
        if head == 0:
            g_wo.forward_all()
            for j in range(1, place.ys):
                g_cot.arrive_y(j)
        if head == 1:
            g_w1.forward_all()
            g_w2.start()
    for head in range(heads):
        for j in range(1, place.ys):
            g_mix[head].arrive_y(j)
    for head in range(heads):
        for j in range(place.ys):
            g_mix[head].arrive_core(j)
    mix_copy = pltpu.make_async_copy(mix, mix_out, local.at[15])
    mix_copy.start()
    g_w2.forward_all()
    for j in range(place.ys):
        g_cot.arrive_core(j)
    for group in (g_wo, g_w1, g_w2):
        group.arrive()
    for group in (g_sm, g_wq, g_wo, g_w1, g_w2, g_x, g_cot, *g_mix):
        group.drain()
    for copy in (*own_blocks, *results, mix_copy):
        copy.wait()


def front(place, length, x, cot, small, wqkv, wo, w1, w2):
    dp, seq = place.dp, place.seq
    rows = x.shape[0]
    slots = rows * seq
    heads = HEADS // seq
    share, width = wqkv.shape
    anyspace = pl.BlockSpec(memory_space=pl.ANY)
    shapes = [
        (seq, rows, D),
        (seq, rows, D),
        (dp, *small.shape),
        (dp, share, width),
        (dp, *wo.shape),
        (dp, *w1.shape),
        (dp, *w2.shape),
        (slots, D),
        (heads, 128, slots),
        (heads, HEAD_DIM, slots),
        (heads, slots, 128),
        (heads, slots, HEAD_DIM),
        (seq, heads, HEAD_DIM, slots),
    ]
    vm = lambda *shape: pltpu.VMEM(shape, BF16)
    return pl.pallas_call(
        functools.partial(front_kernel, place),
        in_specs=[pl.BlockSpec(memory_space=pltpu.SMEM)] + [anyspace] * 7,
        out_specs=[anyspace] * len(shapes) + [pl.BlockSpec(memory_space=pltpu.VMEM)],
        out_shape=[jax.ShapeDtypeStruct(shape, BF16) for shape in shapes]
        + [jax.ShapeDtypeStruct((heads, 1, slots), F32)],
        scratch_shapes=[
            vm(seq, rows, D),
            vm(slots, D),
            vm(dp, *small.shape),
            vm(dp, share, width),
            vm(width, D),
            vm(heads, 128, slots),
            vm(heads, HEAD_DIM, slots),
            vm(heads, HEAD_DIM, slots),
            vm(heads, slots, 128),
            vm(heads, slots, HEAD_DIM),
            vm(seq, heads, HEAD_DIM, slots),
        ]
        + dp_semaphores(place, 5)
        + seq_semaphores(place, 2 + heads)
        + [pltpu.SemaphoreType.DMA((16,))],
        compiler_params=params(collective_id=0, has_side_effects=True),
        name="front",
    )(length, x, cot, small, wqkv, wo, w1, w2)


def attend_back_kernel(
    qt_ref, kt_ref, k_ref, v_ref, got_ref, mix_ref, lse_ref,
    dqt_ref, dk_ref, dv_ref, dk_sum, dv_sum,
):
    step = pl.program_id(1)

    @pl.when(step == 0)
    def _():
        dk_sum[...] = jnp.zeros_like(dk_sum)
        dv_sum[...] = jnp.zeros_like(dv_sum)

    grad = got_ref[0]
    delta = jnp.sum(grad.astype(F32) * mix_ref[0].astype(F32), axis=0, keepdims=True)
    probs = jnp.exp2(dot(k_ref[0], qt_ref[0]) * QSCALE - lse_ref[0])
    grad_probs = dot(v_ref[0], grad)
    grad_scores = (probs * (grad_probs - delta)).astype(BF16)
    dv_sum[...] += dot(probs.astype(BF16), grad, ((1,), (1,)))
    dk_sum[...] += dot(grad_scores, qt_ref[0, :HEAD_DIM], ((1,), (1,)))
    dqt_ref[0] = (dot(kt_ref[0], grad_scores) * SCALE).astype(BF16)

    @pl.when(step == pl.num_programs(1) - 1)
    def _():
        dk_ref[0] = (dk_sum[...] * SCALE).astype(BF16)
        dv_ref[0] = dv_sum[...].astype(BF16)


def attend_back(qt, kt, k, v, grad_mix, mix, lse):
    heads, _, slots = qt.shape
    block = 256
    turned = jax.ShapeDtypeStruct((heads, HEAD_DIM, slots), BF16)
    part = jax.ShapeDtypeStruct((heads, slots, HEAD_DIM), BF16)
    cols = pl.BlockSpec((1, HEAD_DIM, block), lambda h, i: (h, 0, i))
    rows = pl.BlockSpec((1, slots, HEAD_DIM), lambda h, i: (h, 0, 0))
    return pl.pallas_call(
        attend_back_kernel,
        grid=(heads, slots // block),
        in_specs=[
            pl.BlockSpec((1, 128, block), lambda h, i: (h, 0, i)),
            pl.BlockSpec((1, HEAD_DIM, slots), lambda h, i: (h, 0, 0)),
            pl.BlockSpec((1, slots, 128), lambda h, i: (h, 0, 0)),
            rows,
            cols,
            cols,
            pl.BlockSpec((1, 1, block), lambda h, i: (h, 0, i)),
        ],
        out_specs=[cols, rows, rows],
        scratch_shapes=[pltpu.VMEM((slots, HEAD_DIM), F32), pltpu.VMEM((slots, HEAD_DIM), F32)],
        out_shape=[turned, part, part],
        compiler_params=params(),
        name="attend_back",
    )(qt, kt, k, v, grad_mix, mix, lse)


def feed_kernel(
    place_ref, x_ref, mix_ref, cot_ref, wo_ref, w1_ref, w2_ref, bo_ref, gain_ref, shift_ref, b1_ref,
    out_ref, ds_ref, second_ref, act_ref, de_ref, middle_ref, gain_sum, shift_sum, b1_sum,
):
    step = pl.program_id(0)
    count = pl.num_programs(0)
    block = x_ref.shape[0]
    owner = lax.rem(place_ref[0] + 1 + step, count)

    @pl.when(step == 0)
    def _():
        gain_sum[...] = jnp.zeros_like(gain_sum)
        shift_sum[...] = jnp.zeros_like(shift_sum)
        b1_sum[...] = jnp.zeros_like(b1_sum)

    middle = x_ref[...].astype(F32) + (dot(mix_ref[...], wo_ref[...], ((0,), (0,))) + bo_ref[...])
    middle_ref[...] = middle
    unit, _ = normalize(middle)
    second = (unit * gain_ref[...] + shift_ref[...]).astype(BF16)
    second_ref[...] = second
    valid = owner * block + lax.broadcasted_iota(jnp.int32, (block, 1), 0) < place_ref[1]
    grad_two = jnp.where(valid, cot_ref[...].astype(F32), 0.0).astype(BF16)
    expanded = dot(second, w1_ref[...]) + b1_ref[...]
    phi = 0.5 * (1.0 + lax.erf(expanded * (0.5**0.5)))
    activated = (expanded * phi).astype(BF16)
    act_ref[...] = activated
    slope = phi + expanded * (jnp.exp(-0.5 * expanded * expanded) * 0.3989422804014327)
    out_ref[...] = dot(activated, w2_ref[...]).astype(BF16)
    grad_act = dot(grad_two, w2_ref[...], ((1,), (1,)))
    grad_expanded = (grad_act * slope).astype(BF16)
    de_ref[...] = grad_expanded
    b1_sum[...] += jnp.sum(grad_expanded.astype(F32), axis=0, keepdims=True)
    grad_second = dot(grad_expanded, w1_ref[...], ((1,), (1,)))
    ds_ref[...] = grad_second.astype(BF16)
    gain_sum[...] += jnp.sum(grad_second * unit, axis=0, keepdims=True)
    shift_sum[...] += jnp.sum(grad_second, axis=0, keepdims=True)


def feed(place, x, mix, cot, wo, w1, w2, bo, gain, shift, b1):
    slots = x.shape[0]
    block = chunk_of(slots)
    count = slots // block
    width = w1.shape[1]

    def turn(i, place):
        return lax.rem(place[0] + 1 + i, count)

    rows = pl.BlockSpec((block, D), lambda i, p: (turn(i, p), 0))
    wide = pl.BlockSpec((block, width), lambda i, p: (turn(i, p), 0))
    return pl.pallas_call(
        feed_kernel,
        grid_spec=pltpu.PrefetchScalarGridSpec(
            num_scalar_prefetch=1,
            grid=(count,),
            in_specs=[
                rows,
                pl.BlockSpec((D, block), lambda i, p: (0, turn(i, p))),
                rows,
                whole(wo.shape), whole(w1.shape), whole(w2.shape)]
            + [whole((1, D))] * 3
            + [whole((1, width))],
            out_specs=[
                rows,
                rows,
                rows,
                wide,
                wide,
                pl.BlockSpec((block, D), lambda i, p: (0, 0)),
                pl.BlockSpec((1, D), lambda i, p: (0, 0)),
                pl.BlockSpec((1, D), lambda i, p: (0, 0)),
                pl.BlockSpec((1, width), lambda i, p: (0, 0)),
            ],
        ),
        out_shape=[
            jax.ShapeDtypeStruct((slots, D), BF16),
            jax.ShapeDtypeStruct((slots, D), BF16),
            jax.ShapeDtypeStruct((slots, D), BF16),
            jax.ShapeDtypeStruct((slots, width), BF16),
            jax.ShapeDtypeStruct((slots, width), BF16),
            jax.ShapeDtypeStruct((block, D), F32),
            jax.ShapeDtypeStruct((1, D), F32),
            jax.ShapeDtypeStruct((1, D), F32),
            jax.ShapeDtypeStruct((1, width), F32),
        ],
        compiler_params=params(),
        name="feed",
    )(place, x, mix, cot, wo, w1, w2, bo, gain, shift, b1)


def gather(value, axes, axis=0):
    return lax.all_gather(value, axes, axis=axis, tiled=True)


def scatter_sum(value, axes, axis=0):
    return lax.psum_scatter(value, axes, scatter_dimension=axis, tiled=True)


def per_device(
    hidden_in, cotangent, clip_lengths, clip_order, first_gain, first_shift, query_weight,
    query_bias, key_weight, value_weight, value_bias, output_weight, output_bias, second_gain,
    second_shift, expand_weight, expand_bias, reduce_weight, reduce_bias,
):
    dp = lax.axis_size("dp")
    seq = lax.axis_size("seq")
    me = lax.axis_index("seq")
    rows_here = hidden_in.shape[1]
    slots = rows_here * seq
    share = D // dp
    head_cols = D // seq
    heads = HEADS // seq
    units = FF // (dp * seq)
    quarter = dp * units

    hidden_own = hidden_in[0]
    matches = clip_order[0] == jnp.arange(clip_lengths.shape[0], dtype=jnp.int32)
    length = jnp.sum(jnp.where(matches, clip_lengths, 0)).reshape(1)

    spot = Place(dp, seq)
    mine_dp = lax.axis_index("dp")

    def columns(weight):
        return lax.dynamic_slice_in_dim(weight, me * head_cols, head_cols, 1)

    width = 3 * head_cols
    extra = -(-(8 * share + FF // dp) // width)
    tall = -(-(share + extra) // 16) * 16

    def spread(vector):
        return lax.dynamic_update_slice_in_dim(jnp.zeros((D,), BF16), vector, mine_dp * share, 0)

    def head_part(vector):
        part = lax.dynamic_slice_in_dim(spread(vector), me * head_cols, head_cols, 0)
        return jnp.pad(part, (0, D - head_cols))

    expand_own = lax.dynamic_slice_in_dim(expand_bias, me * units, units, 0)
    expand_row = lax.dynamic_update_slice_in_dim(
        jnp.zeros((quarter,), BF16), expand_own, mine_dp * units, 0
    )
    blank = jnp.zeros((D,), BF16)
    small = jnp.stack(
        [spread(first_gain), spread(first_shift), spread(output_bias), spread(second_gain),
         spread(second_shift), spread(reduce_bias), jnp.pad(expand_row, (0, D - quarter)), blank,
         head_part(query_bias), head_part(value_bias)] + [blank] * 6
    )
    wqkv_share = jnp.concatenate(
        [columns(query_weight), columns(key_weight), columns(value_weight)], axis=1
    )
    w1_share = jnp.concatenate(
        [
            lax.dynamic_slice_in_dim(expand_weight, d * (FF // dp) + me * units, units, 1)
            for d in range(dp)
        ],
        axis=1,
    )
    w2_share = lax.dynamic_slice_in_dim(reduce_weight, me * units, units, 0)
    (
        x, cot, small, w_qkv, w_out, w_expand, w_reduce, normed, qt, kt, keys, values, mix, lse,
    ) = front(spot, length, hidden_own, cotangent[0], small, wqkv_share, output_weight, w1_share, w2_share)
    x, cot = (value.reshape(slots, D) for value in (x, cot))
    w_qkv = w_qkv.reshape(D, width)
    w_out = w_out.reshape(D, D)
    w_expand = w_expand.reshape(D, quarter)
    w_reduce = w_reduce.reshape(quarter, D)
    vectors = jnp.sum(small.astype(F32), axis=0)
    gain_one, shift_one, bias_out, gain_two, shift_two, bias_reduce = (
        vectors[i : i + 1] for i in range(6)
    )
    bias_expand = vectors[6:7, :quarter]
    mix_own = lax.dynamic_index_in_dim(mix, me, 0, keepdims=False)
    mix = mix.reshape(D, slots)
    joined = chunk_of(slots) // rows_here
    place = jnp.stack([me.astype(jnp.int32) // joined, length[0]])
    (
        out_part, ds_part, second, act, grad_expanded, middle_own, gain_two_grad, shift_two_grad,
        bias_expand_grad,
    ) = feed(
        place, x, mix, cot, w_out, w_expand, w_reduce, bias_out, gain_two, shift_two,
        bias_expand,
    )
    middle_own = lax.dynamic_slice_in_dim(
        middle_own, lax.rem(me.astype(jnp.int32), joined) * rows_here, rows_here, 0
    )
    positions = jnp.arange(slots, dtype=jnp.int32)
    valid = (positions < length)[:, None]
    grad_two = jnp.where(valid, cot, 0).astype(BF16)
    grad_out = lax.dynamic_slice_in_dim(grad_two, me * rows_here, rows_here, 0).astype(F32)

    layer_output = (
        middle_own + (scatter_sum(out_part, "seq").astype(F32) + bias_reduce)
    ).astype(BF16)
    grad_second = scatter_sum(ds_part, "seq").astype(F32)
    unit_two, spread_two = normalize(middle_own)
    grad_middle = grad_out + norm_backward(unit_two, spread_two, grad_second * gain_two)
    grad_branch = grad_middle.astype(BF16)
    reduce_bias_grad = jnp.sum(grad_out, axis=0)
    output_bias_grad = jnp.sum(grad_branch.astype(F32), axis=0)

    w1_grad = dot(second, grad_expanded, ((0,), (0,))).astype(BF16)
    w2_grad = dot(act, grad_two, ((0,), (0,))).astype(BF16)
    w1_grad = scatter_sum(w1_grad, "dp")
    w2_grad = scatter_sum(w2_grad, "dp")

    grad_branch_all = gather(grad_branch, "seq")
    wo_grad = dot(mix, columns(grad_branch_all)).astype(BF16)
    wo_rows = lax.dynamic_slice_in_dim(w_out, me * head_cols, head_cols, 0)
    grad_mix = dot(wo_rows, grad_branch_all, ((1,), (1,))).astype(BF16)
    dqt, dk, dv = attend_back(
        qt, kt, keys, values, grad_mix.reshape(heads, HEAD_DIM, slots), mix_own, lse
    )
    dqkv = jnp.concatenate(
        [
            dqt.reshape(head_cols, slots).T,
            jnp.concatenate([dk, dv], axis=0).transpose(1, 0, 2).reshape(slots, 2 * head_cols),
        ],
        axis=1,
    )
    qkv_grad = dot(normed, dqkv, ((0,), (0,))).astype(BF16)
    bias_qkv_grad = jnp.sum(dqkv.astype(F32), axis=0)
    grad_normed = dot(dqkv, w_qkv, ((1,), (1,)))
    unit_all, _ = normalize(x.astype(F32))
    gain_one_grad = jnp.sum(grad_normed * unit_all, axis=0)
    shift_one_grad = jnp.sum(grad_normed, axis=0)
    grad_normed_own = scatter_sum(grad_normed.astype(BF16), "seq").astype(F32)
    unit_one, spread_one = normalize(hidden_own.astype(F32))
    grad_front = grad_middle + norm_backward(unit_one, spread_one, grad_normed_own * gain_one)
    input_grad = grad_front.astype(BF16)

    def mine(value):
        return lax.dynamic_update_slice_in_dim(
            jnp.zeros((D,), F32), value.reshape(-1), me * head_cols, 0
        )

    expand_vec = lax.dynamic_update_slice_in_dim(
        jnp.zeros((dp, FF // dp), F32), bias_expand_grad.reshape(dp, units), me * units, 1
    )
    vectors = [
        gain_one_grad, shift_one_grad, mine(bias_qkv_grad[:head_cols]),
        mine(bias_qkv_grad[2 * head_cols :]), output_bias_grad, gain_two_grad.reshape(-1),
        shift_two_grad.reshape(-1), reduce_bias_grad,
    ]
    small_grad = jnp.concatenate([v.reshape(dp, share) for v in vectors] + [expand_vec], axis=1)
    small_grad = jnp.pad(
        small_grad.astype(BF16), ((0, 0), (0, (tall - share) * width - small_grad.shape[1]))
    ).reshape(dp, tall - share, width)
    packed_grad = jnp.concatenate([qkv_grad.reshape(dp, share, width), small_grad], axis=1)
    packed_grad = scatter_sum(packed_grad, "dp")[0]
    wo_grad = scatter_sum(wo_grad, "dp")

    packed_grad = gather(packed_grad[None], "seq")
    wo_grad = gather(wo_grad[None], "seq")
    w1_grad = gather(w1_grad[None], "seq")
    w2_grad = gather(w2_grad, "seq").astype(F32)
    w1_grad = (
        w1_grad.reshape(seq, share, dp, units).transpose(1, 2, 0, 3).reshape(share, FF).astype(F32)
    )
    wo_grad = wo_grad.transpose(1, 0, 2).reshape(share, D).astype(F32)
    qkv_grad = packed_grad[:, :share].reshape(seq, share, 3, head_cols).astype(F32)
    qkv_grad = qkv_grad.transpose(2, 1, 0, 3).reshape(3, share, D)
    small_grad = jnp.sum(
        packed_grad[:, share : share + extra].reshape(seq, extra * width).astype(F32), axis=0
    )
    pieces = [small_grad[i * share : (i + 1) * share] for i in range(8)]
    expand_bias_grad = small_grad[8 * share : 8 * share + FF // dp]
    return (
        layer_output[None],
        input_grad[None],
        pieces[0],
        pieces[1],
        qkv_grad[0],
        pieces[2],
        qkv_grad[1],
        qkv_grad[2],
        pieces[3],
        wo_grad,
        pieces[4],
        pieces[5],
        pieces[6],
        w1_grad,
        expand_bias_grad,
        w2_grad,
        pieces[7],
    )


def solution(mesh):
    clip = P("dp", "seq", None)
    vec = P("dp")
    mat = P("dp", None)
    return jax.shard_map(
        per_device,
        mesh=mesh,
        in_specs=(
            clip, clip, P(), vec, vec, vec, mat, vec, mat, mat, vec, mat, vec, vec, vec, mat, vec,
            mat, vec,
        ),
        out_specs=(
            clip, clip, vec, vec, mat, vec, mat, mat, vec, mat, vec, vec, vec, mat, vec, mat, vec,
        ),
        check_vma=False,
    )
```

time: 1000 us -> 720 us (0.72)
  waiting for transfers between devices: 664 us -> 265 us
  Pallas kernels: 110 us -> 245 us
  local copies, waits for them, and re-layouts: 98.2 us -> 76.8 us
    all_gather x11 -> x4, waiting for transfers between devices: 360 us -> 4.28 us  [gather(): return lax.all_gather(value, axes, axis=axis, tiled=True)]
    pallas_call x3 -> x2, Pallas kernels: 73.5 us -> 208 us  [the longest x1 177 us: front(): pl.pallas_call(functools.partial(front_kernel, place), in_specs=[pl.Block...]
    reduce_scatter x7, waiting for transfers between devices: 301 us -> 258 us  [scatter_sum(): return lax.psum_scatter(value, axes, scatter_dimension=axis, tiled=True)]
  transfers between devices with their start and end apart: 18 -> 11, of which waited for: 16 -> 7; matrix products, arithmetic and copies ran while one was open for 17% -> 20% of each run, Pallas kernels for 4% -> 4%
where the time goes in v2:
time: 720 us; the launch traced here: 711 us
  waiting for transfers between devices  265 us (37%)
  Pallas kernels  245 us (34%)
  local copies, waits for them, and re-layouts  76.8 us (11%)
  other arithmetic  50.7 us (7%)
  matrix products  47.9 us (7%)
  between operations  17.3 us (2%)
  blocking collectives  7.46 us (1%)
    reduce_scatter x7, waiting for transfers between devices, scatter_sum(): return lax.psum_scatter(value, axes, scatter_dimension=axis, tiled=True)  258 us
    pallas_call x1, Pallas kernels, front(): pl.pallas_call(functools.partial(front_kernel, place), in_specs=[pl.Block...  177 us
    dot_general x6, matrix products, dot(): lax.dot_general(left, right, (contract, ((), ())), preferred_element_type...  47.9 us
    pallas_call x1, Pallas kernels, feed(): pl.pallas_call(feed_kernel, grid_spec=pltpu.PrefetchScalarGridSpec(num_sc...  36.9 us
    pallas_call x1, Pallas kernels, attend_back(): pl.pallas_call(attend_back_kernel, grid=(heads, slots // block), in_specs...  31.5 us
    convert_element_type x3, local copies, waits for them, and re-layouts, per_device(): w1_grad.reshape(seq, share, dp, units).transpose(1, 2, 0, 3)  21.8 us
  transfers between devices with their start and end apart: 11, of which 7 were waited for; matrix products, arithmetic and copies ran while one was open for 20% of the time, Pallas kernels for 4%

profile of v2, /device:TPU:0, one launch (start us, length us, event | category | flops | bytes accessed | tf_op | source)
XLA Modules:
  0.0 710.7 jit_solution(14766083838358690417)
XLA Ops:
  25.9 176.8 %front.1 = (bf16[4,384,1280]{2,1,0:T(8,128)(2,1)}, bf16[4,384,1280]{2,1,0:T(8,128)(2,1)}, bf16[8,16,1280]{2,1,0:T(8,128)(2,1)}, bf16[8,160,960]{2,1,0:T(8,128)(2...) custom-call(s32[1]{0:T(128)} %bitcast.2.length_ref, ...), custom_call_target="tpu_custom_call" | custom-call | tf_op jit(solution)/shard_map/front/pallas_call | solution.py:400
  205.6 36.9 %feed.1 = (bf16[1536,1280]{1,0:T(8,128)(2,1)}, bf16[1536,1280]{1,0:T(8,128)(2,1)}, bf16[1536,1280]{1,0:T(8,128)(2,1)}, bf16[1536,1280]{1,0:T(8,128)(2,1)}, bf16[...) custom-call(s32[2]{0:T(128)} %pad_add_fusion.place_ref, ...), custom_call_target="tpu_custom_call" | custom-call | tf_op jit(solution)/shard_map/feed/pallas_call | solution.py:529
  251.5 39.8 %reduce-scatter.10.cloned.1.call-done = bf16[384,1280]{1,0:T(8,128)(2,1)} async-done(((bf16[1536,1280]{1,0:T(8,128)(2,1)}), bf16[384,1280]{1,0:T(8,128)(2,1)}) %reduce-scatter.10.cloned.1.call-update) | async-done | bytes 983056 | tf_op jit(solution)/shard_map/reduce_scatter | solution.py:574
  291.3 45.5 %reduce-scatter.8.cloned.1.call-done = bf16[384,1280]{1,0:T(8,128)(2,1)} async-done(((bf16[1536,1280]{1,0:T(8,128)(2,1)}), bf16[384,1280]{1,0:T(8,128)(2,1)}) %reduce-scatter.8.cloned.1.call-update) | async-done | bytes 983056 | tf_op jit(solution)/shard_map/reduce_scatter | solution.py:574
  340.5 4.4 fusion.25
  345.0 9.9 %convolution_convert_fusion.1 = bf16[1280,1280]{1,0:T(8,128)(2,1)} fusion(bf16[1536,1280]{1,0:T(8,128)(2,1)} %get-tuple-element.66, bf16[1536,1280]{1,0:T(8,128)(2,1)} %get-tuple-element.67), kind=kOutput, calls=%fused_computation.6 | convolution fusion | flops 5034803200 | bytes 11141120 | tf_op jit(solution)/shard_map/dot_general | solution.py:23
  354.9 9.4 %convolution_convert_fusion = bf16[1280,1280]{1,0:T(8,128)(2,1)} fusion(bf16[1536,1280]{1,0:T(8,128)(2,1)} %get-tuple-element.68, bf16[1536,1280]{1,0:T(8,128)(2,1)} %broadcast_select_fusion), kind=kOutput, calls=%fused_computation.5 | convolution fusion | flops 5034803200 | bytes 11141120 | tf_op jit(solution)/shard_map/dot_general | solution.py:23
  378.1 4.9 convolution_convert_fusion.4
  383.0 31.5 %attend_back.1 = (bf16[4,80,1536]{2,1,0:T(8,128)(2,1)}, bf16[4,1536,80]{2,1,0:T(8,128)(2,1)}, bf16[4,1536,80]{2,1,0:T(8,128)(2,1)}) custom-call(bf16[4,128,1536]{2,1,0:T(8,128)(2,1)} %get-tuple-element.53.qt_ref, bf16[4,80,1536]{2,1,0:T(8,128)(2,1)} %get-tuple-element.54.kt_ref, bf16[4,1536,128]{2,1,0:T(8,128)(2,1)} %get-tuple-element.55.k_ref, ...), custom_call_target="tpu_custom_call" | custom-call | tf_op jit(solution)/shard_map/attend_back/pallas_call | solution.py:460
  418.7 4.5 copy.58
  423.2 8.2 %convolution_convert_fusion.2 = bf16[1280,960]{0,1:T(8,128)(2,1)} fusion(bf16[1536,1280]{1,0:T(8,128)(2,1)} %get-tuple-element.62, bf16[1536,640]{0,1:T(8,128)(2,1)} %bitcast.53, bf16[1536,320]{0,1:T(8,128)(2,1)S(1)} %bitcast.63), kind=kOutput, calls=%fused_computation.9 | convolution fusion | flops 3782000640 | bytes 9338880 | tf_op jit(solution)/shard_map/dot_general | solution.py:23
  431.4 4.5 copy.59
  438.2 9.7 %fusion.24 = (bf16[1280]{0:T(1024)(128)(2,1)S(1)}, bf16[1280]{0:T(1024)(128)(2,1)S(1)}, bf16[1536,1280]{1,0:T(8,128)(2,1)}) fusion(f32[1536]{0:T(1024)S(1)} %rsqrt.30, f32[1536]{0:T(1024)S(1)} %div.43, bf16[4,384,1280]{2,1,0:T(8,128)(2,1)} %get-tuple-element.43, bf16[1280,960]{1,0:T(8,128)(2,1)} %bitcast.68, bf16[1536,640]{0,1:T(8,128)(2,1)} %bitcast.55, ...), kind=kOutput, calls=%fused_computation.84 | convolution fusion | flops 3794531840 | bytes 13288448 | tf_op jit(solution)/shard_map/dot_general | solution.py:23
  453.1 57.5 %reduce-scatter.20.cloned.1.call-done = bf16[160,1280]{1,0:T(8,128)(2,1)} async-done(((bf16[1280,1280]{1,0:T(8,128)(2,1)}), bf16[160,1280]{1,0:T(8,128)(2,1)}) %reduce-scatter.20.cloned.1.call-update) | async-done | bytes 409616 | tf_op jit(solution)/shard_map/reduce_scatter | solution.py:574
  510.8 5.8 convolution_convert_fusion.3
  516.7 68.7 %reduce-scatter.14.cloned.1.call-done = bf16[1,176,960]{2,1,0:T(8,128)(2,1)} async-done(((bf16[8,176,960]{2,1,0:T(8,128)(2,1)}), bf16[1,176,960]{2,1,0:T(8,128)(2,1)}) %reduce-scatter.14.cloned.1.call-update) | async-done | bytes 337936 | tf_op jit(solution)/shard_map/reduce_scatter | solution.py:574
  586.9 6.0 reshape.232
  592.8 8.2 %copy.64 = f32[160,8,4,160]{3,2,1,0:T(4,128)} copy(f32[160,8,4,160]{3,1,0,2:T(8,128)} %bitcast.49) | data formatting | bytes 6553600 | tf_op jit(solution)/shard_map/convert_element_type | solution.py:733
  601.0 7.7 %reshape.230 = f32[160,5120]{1,0:T(8,128)} reshape(f32[160,8,4,160]{3,2,1,0:T(4,128)} %copy.64) | data formatting | bytes 6553600 | tf_op jit(solution)/shard_map/convert_element_type | solution.py:733
  612.1 40.7 %reduce-scatter.16.cloned.1.call-done = bf16[160,320]{1,0:T(8,128)(2,1)} async-done(((bf16[1280,320]{1,0:T(8,128)(2,1)}), bf16[160,320]{1,0:T(8,128)(2,1)}) %reduce-scatter.16.cloned.1.call-update) | async-done | bytes 102416 | tf_op jit(solution)/shard_map/reduce_scatter | solution.py:574
  652.8 7.5 %all-gather = bf16[640,320]{1,0:T(8,128)(2,1)S(1)} all-gather(bf16[160,320]{1,0:T(8,128)(2,1)} %reduce-scatter.16.cloned.1.call-done), channel_id=2, replica_groups=mesh['dp'=8,'seq'=4] {'seq'}, dimensions={0}, use_global_device_ids=true | all-gather | bytes 512000 | tf_op jit(solution)/shard_map/all_gather | solution.py:570
  665.9 5.6 reshape.231
  671.5 8.4 %fusion.26 = (f32[1,160,4,320]{3,0,1,2:T(1,128)}, f32[1,160,4,320]{3,0,1,2:T(1,128)}, f32[1,160,4,320]{3,0,1,2:T(1,128)S(1)}) fusion(f32[3,160,4,320]{3,0,1,2:T(4,128)} %bitcast.51), kind=kLoop, calls=%fused_computation.86 | loop fusion | bytes 4915200 | tf_op jit(solution)/shard_map/slice | solution.py:751
  690.9 6.2 reduce-scatter.12.cloned.1.call-done
  (154 shorter events, 85.2 us)
Async XLA Ops:
  8.0 7.8 %copy-start = (bf16[640,1280]{1,0:T(8,128)(2,1)S(1)}, bf16[640,1280]{1,0:T(8,128)(2,1)}, u32[]{:S(2)}) copy-start(bf16[640,1280]{1,0:T(8,128)(2,1)} %param.36) | copy-start | bytes 4915204
  8.0 283.3 %reduce-scatter.10.cloned.1.call-start = ((), (), s32[]{:S(2)}) async-start(), calls=%async_computation.8 | async-start | bytes 4915200 | tf_op jit(solution)/shard_map/reduce_scatter | solution.py:574
  242.5 94.3 %reduce-scatter.8.cloned.1.call-start = ((), (), s32[]{:S(2)}) async-start(), calls=%async_computation.7 | async-start | bytes 4915200 | tf_op jit(solution)/shard_map/reduce_scatter | solution.py:574
  243.3 134.8 %all-gather.7.cloned.1.call-start = ((), (), s32[]{:S(2)}) async-start(), calls=%async_computation.9 | async-start | bytes 4915200 | tf_op jit(solution)/shard_map/all_gather | solution.py:570
  291.3 49.2 %copy-start.3 = (bf16[384,1280]{1,0:T(8,128)(2,1)S(1)}, bf16[384,1280]{1,0:T(8,128)(2,1)}, u32[]{:S(2)}) copy-start(bf16[384,1280]{1,0:T(8,128)(2,1)} %reduce-scatter.10.cloned.1.call-done) | copy-start | bytes 2949124
  345.0 107.5 %reduce-scatter.18.cloned.1.call-start = ((), (), s32[]{:S(2)}) async-start(), calls=%async_computation.14 | async-start | bytes 3686400 | tf_op jit(solution)/shard_map/reduce_scatter | solution.py:574
  354.9 155.6 %reduce-scatter.20.cloned.1.call-start = ((), (), s32[]{:S(2)}) async-start(), calls=%async_computation.15 | async-start | bytes 3686400 | tf_op jit(solution)/shard_map/reduce_scatter | solution.py:574
  364.4 221.0 %reduce-scatter.14.cloned.1.call-start = ((), (), s32[]{:S(2)}) async-start(), calls=%async_computation.11 | async-start | bytes 3244032 | tf_op jit(solution)/shard_map/reduce_scatter | solution.py:574
  367.2 3.4 copy-start.7
  367.2 3.5 copy-start.6
  367.2 3.6 copy-start.5
  418.7 4.5 copy-start.4
  452.4 134.4 %all-gather.13.cloned.1.call-start = ((), (), s32[]{:S(2)}) async-start(), calls=%async_computation.17 | async-start | bytes 2048000 | tf_op jit(solution)/shard_map/all_gather | solution.py:570
  453.0 155.7 %all-gather.11.cloned.1.call-start = ((), (), s32[]{:S(2)}) async-start(), calls=%async_computation.16 | async-start | bytes 2048000 | tf_op jit(solution)/shard_map/all_gather | solution.py:570
  510.5 142.3 %reduce-scatter.16.cloned.1.call-start = ((), (), s32[]{:S(2)}) async-start(), calls=%async_computation.13 | async-start | bytes 1105920 | tf_op jit(solution)/shard_map/reduce_scatter | solution.py:574
  516.6 69.6 %copy-start.2 = (bf16[1,384,1280]{2,1,0:T(8,128)(2,1)S(1)}, bf16[1,384,1280]{2,1,0:T(8,128)(2,1)}, u32[]{:S(2)}) copy-start(bf16[1,384,1280]{2,1,0:T(8,128)(2,1)} %param.19) | copy-start | bytes 2949124
  516.7 145.8 %all-gather.9.cloned.1.call-start = ((), (), s32[]{:S(2)}) async-start(), calls=%async_computation.12 | async-start | bytes 1802240 | tf_op jit(solution)/shard_map/all_gather | solution.py:570
  585.4 111.7 %reduce-scatter.12.cloned.1.call-start = ((), (), s32[]{:S(2)}) async-start(), calls=%async_computation.10 | async-start | bytes 4915200 | tf_op jit(solution)/shard_map/reduce_scatter | solution.py:574
  697.2 5.5 copy-start.1
Sparse Core Ops, SparseCore 0:
  242.6 48.6 reduce-scatter.9
  293.8 42.8 reduce-scatter.7
  345.1 32.9 all-gather.6
  454.5 20.2 all-gather.12
  510.7 19.0 all-gather.10
  585.6 18.1 all-gather.8
Sparse Core Ops, SparseCore 1:
  355.0 76.2 reduce-scatter.17
  435.2 75.2 reduce-scatter.19
  513.9 71.4 reduce-scatter.13
  589.4 63.4 reduce-scatter.15
  655.4 41.7 reduce-scatter.11

commit v3 on v2

--- a/solution.py
+++ b/solution.py
@@ -15,7 +15,7 @@
 SCALE = HEAD_DIM ** (-0.5)
 F32 = jnp.float32
 BF16 = jnp.bfloat16
-VMEM_LIMIT = 60 * 1024 * 1024
+VMEM_LIMIT = 66_000_000
 MESH = pl.DeviceIdType.MESH
 
 
@@ -211,8 +211,8 @@
 
 
 def front_kernel(
-    place, length_ref, x_in, cot_in, sm_in, wq_in, wo_in, w1_in, w2_in,
-    x_out, cot_out, sm_out, wq_out, wo_out, w1_out, w2_out, normed_out, qt_out, kt_out, k_out,
+    place, length_ref, x_in, cot_in, sm_in, wq_in, wo_in, w1_in,
+    x_out, cot_out, sm_out, wq_out, wo_out, w1_out, normed_out, qt_out, kt_out, k_out,
     v_out, mix_out, lse_ref,
     xs, nr, sm, wq, wt, qt, kt, vt, kn, vn, mix,
     zsend, zrecv, xsend, xrecv, ssend, srecv, local,
@@ -236,7 +236,6 @@
     g_wq = over_dp(1, wq_in, wq)
     g_wo = over_dp(2, wo_in, wo_out)
     g_w1 = over_dp(3, w1_in, w1_out)
-    g_w2 = over_dp(4, w2_in, w2_out)
     g_x = over_seq(0, x_in, xs)
     g_cot = over_seq(1, cot_in, cot_out)
 
@@ -249,7 +248,6 @@
         pltpu.make_async_copy(cot_in, cot_out.at[place.s], local.at[3]),
         pltpu.make_async_copy(wo_in, wo_out.at[place.d], local.at[4]),
         pltpu.make_async_copy(w1_in, w1_out.at[place.d], local.at[5]),
-        pltpu.make_async_copy(w2_in, w2_out.at[place.d], local.at[6]),
     ]
     for copy in locals_in:
         copy.start()
@@ -354,7 +352,6 @@
                 g_cot.arrive_y(j)
         if head == 1:
             g_w1.forward_all()
-            g_w2.start()
     for head in range(heads):
         for j in range(1, place.ys):
             g_mix[head].arrive_y(j)
@@ -363,18 +360,17 @@
             g_mix[head].arrive_core(j)
     mix_copy = pltpu.make_async_copy(mix, mix_out, local.at[15])
     mix_copy.start()
-    g_w2.forward_all()
     for j in range(place.ys):
         g_cot.arrive_core(j)
-    for group in (g_wo, g_w1, g_w2):
+    for group in (g_wo, g_w1):
         group.arrive()
-    for group in (g_sm, g_wq, g_wo, g_w1, g_w2, g_x, g_cot, *g_mix):
+    for group in (g_sm, g_wq, g_wo, g_w1, g_x, g_cot, *g_mix):
         group.drain()
     for copy in (*own_blocks, *results, mix_copy):
         copy.wait()
 
 
-def front(place, length, x, cot, small, wqkv, wo, w1, w2):
+def front(place, length, x, cot, small, wqkv, wo, w1):
     dp, seq = place.dp, place.seq
     rows = x.shape[0]
     slots = rows * seq
@@ -388,7 +384,6 @@
         (dp, share, width),
         (dp, *wo.shape),
         (dp, *w1.shape),
-        (dp, *w2.shape),
         (slots, D),
         (heads, 128, slots),
         (heads, HEAD_DIM, slots),
@@ -399,7 +394,7 @@
     vm = lambda *shape: pltpu.VMEM(shape, BF16)
     return pl.pallas_call(
         functools.partial(front_kernel, place),
-        in_specs=[pl.BlockSpec(memory_space=pltpu.SMEM)] + [anyspace] * 7,
+        in_specs=[pl.BlockSpec(memory_space=pltpu.SMEM)] + [anyspace] * 6,
         out_specs=[anyspace] * len(shapes) + [pl.BlockSpec(memory_space=pltpu.VMEM)],
         out_shape=[jax.ShapeDtypeStruct(shape, BF16) for shape in shapes]
         + [jax.ShapeDtypeStruct((heads, 1, slots), F32)],
@@ -416,154 +411,729 @@
             vm(heads, slots, HEAD_DIM),
             vm(seq, heads, HEAD_DIM, slots),
         ]
-        + dp_semaphores(place, 5)
+        + dp_semaphores(place, 4)
         + seq_semaphores(place, 2 + heads)
         + [pltpu.SemaphoreType.DMA((16,))],
         compiler_params=params(collective_id=0, has_side_effects=True),
         name="front",
-    )(length, x, cot, small, wqkv, wo, w1, w2)
-
-
-def attend_back_kernel(
-    qt_ref, kt_ref, k_ref, v_ref, got_ref, mix_ref, lse_ref,
-    dqt_ref, dk_ref, dv_ref, dk_sum, dv_sum,
+    )(length, x, cot, small, wqkv, wo, w1)
+
+
+class ScatterSeq:
+    def __init__(self, place, group, sems, part, from_core, from_y):
+        self.p, self.g, self.part, self.from_core, self.from_y = place, group, part, from_core, from_y
+        self.sends, self.recvs = sems
+
+    def core_copy(self, j):
+        place = self.p
+        return send(self.part(place.at_y(j, 1 - place.c)), self.from_core(j),
+                    self.sends.at[self.g, 1, j], self.recvs.at[self.g, 1, j],
+                    (place.d, place.partner))
+
+    def y_copy(self, j, src):
+        place = self.p
+        return send(src, self.from_y(j), self.sends.at[self.g, 0, j], self.recvs.at[self.g, 0, j],
+                    (place.d, place.at_y(j, place.c)))
+
+
+class ScatterDp:
+    def __init__(self, place, group, sems, part, from_x, total, from_z):
+        self.p, self.g = place, group
+        self.part, self.from_x, self.total, self.from_z = part, from_x, total, from_z
+        self.zsend, self.zrecv, self.xsend, self.xrecv = sems
+
+    def x_copy(self, j, zi):
+        place = self.p
+        target = lax.rem(place.x + j, place.xs)
+        return send(self.part(zi * place.xs + target), self.from_x(j, zi),
+                    self.xsend.at[self.g, zi, j], self.xrecv.at[self.g, zi, j],
+                    (place.at_x(j), place.s))
+
+    def start_x(self):
+        for zi in range(self.p.zs):
+            for j in range(1, self.p.xs):
+                self.x_copy(j, zi).start()
+
+    def fold(self, zi):
+        place = self.p
+        value = self.part(zi * place.xs + place.x)[...].astype(F32)
+        for j in range(1, place.xs):
+            self.x_copy(j, zi).wait_recv()
+            value = value + self.from_x(j, zi)[...].astype(F32)
+        self.total(zi)[...] = value.astype(BF16)
+
+    def fold_all(self):
+        for zi in range(self.p.zs):
+            self.fold(zi)
+
+    def z_copy(self, k):
+        place = self.p
+        return send(self.total(lax.rem(place.z + k, place.zs)), self.from_z(k),
+                    self.zsend.at[self.g, k], self.zrecv.at[self.g, k], (place.at_z(k), place.s))
+
+    def start_z(self):
+        for k in range(self.p.zs - 1, 0, -1):
+            self.z_copy(k).start()
+
+    def finish(self, own):
+        value = own[...].astype(F32)
+        for k in range(1, self.p.zs):
+            self.z_copy(k).wait_recv()
+            value = value + self.from_z(k)[...].astype(F32)
+        return value
+
+    def drain_x(self):
+        for zi in range(self.p.zs):
+            for j in range(1, self.p.xs):
+                self.x_copy(j, zi).wait_send()
+
+    def drain_z(self):
+        for k in range(1, self.p.zs):
+            self.z_copy(k).wait_send()
+
+
+def whole_tiles(*heights):
+    return all(height % 16 == 0 for height in heights)
+
+
+def feed_kernel(
+    place, length_ref, x_in, mix_in, cot_in, wo_in, w1_in, w2_in, vec_ref,
+    gb_out, middle_out, grad_out, part_out, s1_out, s2_out, sums_ref,
+    xa, mixv, gv, wo, w1, w2, second, act, slope, unit, ds, own, from_core, from_y,
+    from_x1, from_x2, *rest,
 ):
-    step = pl.program_id(1)
-
-    @pl.when(step == 0)
-    def _():
+    zsend, zrecv, xsend, xrecv, ssend, srecv, local = rest[-7:]
+    gb = xa
+    place.locate()
+    seq, rows, _ = x_in.shape
+    slots = seq * rows
+    chunk = chunk_of(slots)
+    joined = chunk // rows
+    width = w1.shape[1]
+    share = D // place.dp
+    units = width // place.dp
+    place.barrier()
+    dp_sems = (zsend, zrecv, xsend, xrecv)
+    seq_sems = (ssend, srecv)
+    if whole_tiles(share, units):
+        w1_part = lambda d: w1.at[pl.ds(pl.multiple_of(d * share, 16), share), :]
+        w2_part = lambda d: w2.at[pl.ds(pl.multiple_of(d * units, 16), units), :]
+        total1 = lambda zi: wo.at[pl.ds(zi * share, share), pl.ds(0, width)]
+        total2 = lambda zi: wo.at[pl.ds(place.zs * share + zi * units, units), :]
+    else:
+        w1_split, w2_split, total1_split, total2_split = rest[:4]
+        w1_part, w2_part = (lambda d: w1_split.at[d]), (lambda d: w2_split.at[d])
+        total1, total2 = (lambda zi: total1_split.at[zi]), (lambda zi: total2_split.at[zi])
+    gather = GatherDp(place, 0, dp_sems, w2_in, w2_part)
+    gather.start()
+    loads = [
+        pltpu.make_async_copy(src, dst, local.at[i])
+        for i, (src, dst) in enumerate(
+            [(mix_in, mixv), (wo_in, wo), (w1_in, w1), (cot_in, gv), (x_in, xa)]
+        )
+    ]
+    w2_own = pltpu.make_async_copy(w2_in, w2_part(place.d), local.at[5])
+    for copy in (*loads, w2_own):
+        copy.start()
+    gain, shift, bias_out, bias1 = vec_ref[3:4], vec_ref[4:5], vec_ref[2:3], vec_ref[6:7, :width]
+    own_chunk = place.s // joined
+    sums_ref[...] = jnp.zeros_like(sums_ref)
+    for copy in loads:
+        copy.wait()
+
+    def lines_of(index, size, step=16):
+        return pl.ds(pl.multiple_of(index * size, step), size)
+
+    def forward(i, _):
+        lines = lines_of(i, chunk)
+        hidden = xa[pl.ds(i * joined, joined)].reshape(chunk, D).astype(F32)
+        cols = pl.ds(pl.multiple_of(i * chunk, 128), chunk)
+        middle = hidden + (dot(mixv[:, cols], wo[...], ((0,), (0,))) + bias_out)
+
+        @pl.when(i == own_chunk)
+        def _():
+            own[...] = middle
+
+        normal, _ = normalize(middle)
+        unit[lines, :] = normal.astype(BF16)
+        tokens = (normal * gain + shift).astype(BF16)
+        second[lines, :] = tokens
+        expanded = dot(tokens, w1[...]) + bias1
+        phi = 0.5 * (1.0 + lax.erf(expanded * (0.5**0.5)))
+        act[lines, :] = (expanded * phi).astype(BF16)
+        density = jnp.exp(-0.5 * expanded * expanded) * 0.3989422804014327
+        slope[lines, :] = (phi + expanded * density).astype(BF16)
+        valid = (
+            i * chunk + lax.broadcasted_iota(jnp.int32, (chunk, 1), 0) < length_ref[0]
+        )
+        cot = gv[pl.ds(i * joined, joined)].reshape(chunk, D)
+        gv[pl.ds(i * joined, joined)] = jnp.where(valid, cot.astype(F32), 0.0).astype(BF16).reshape(
+            joined, rows, D
+        )
+        return 0
+
+    lax.fori_loop(0, slots // chunk, forward, 0)
+    gather.forward_all()
+    w2_own.wait()
+    gather.arrive()
+    if not whole_tiles(share, units):
+        for d in range(place.dp):
+            w2[d * units : (d + 1) * units, :] = w2_split[d]
+
+    scatter = ScatterSeq(place, 0, seq_sems, lambda s: ds.at[s], lambda j: from_core.at[j],
+                         lambda j: from_y.at[j - 1])
+    def backward(i):
+        lines = lines_of(i, chunk)
+        grad_two = gv[pl.ds(i * joined, joined)].reshape(chunk, D)
+        grad_act = dot(grad_two, w2[...], ((1,), (1,)))
+        grad_expanded = (grad_act * slope[lines, :].astype(F32)).astype(BF16)
+        slope[lines, :] = grad_expanded
+        grad_second = dot(grad_expanded, w1[...], ((1,), (1,)))
+        ds[pl.ds(i * joined, joined)] = grad_second.astype(BF16).reshape(joined, rows, D)
+        sums_ref[3:4] += jnp.sum(grad_second * unit[lines, :].astype(F32), axis=0, keepdims=True)
+        sums_ref[4:5] += jnp.sum(grad_second, axis=0, keepdims=True)
+        sums_ref[7:8, :width] += jnp.sum(grad_expanded.astype(F32), axis=0, keepdims=True)
+
+    def fold_y(j):
+        block = place.at_y(j, place.c)
+        scatter.core_copy(j).wait_recv()
+        ds[block] = (ds[block].astype(F32) + from_core[j].astype(F32)).astype(BF16)
+        scatter.y_copy(j, ds.at[block]).start()
+
+    for j in list(range(1, place.ys)) + [0]:
+        if joined == 1:
+            backward(place.at_y(j, 1 - place.c))
+            scatter.core_copy(j).start()
+            backward(place.at_y(j, place.c))
+        else:
+            backward(lax.rem(place.y + j, place.ys))
+            scatter.core_copy(j).start()
+        if j:
+            fold_y(j)
+
+    gather.drain()
+
+    def emit(i, _):
+        lines = lines_of(i, chunk)
+        unit[lines, :] = dot(act[lines, :], w2[...]).astype(BF16)
+        return 0
+
+    lax.fori_loop(0, slots // chunk, emit, 0)
+    keep_parts = [
+        pltpu.make_async_copy(
+            unit.at[pl.ds(i * rows, rows), :], part_out.at[i], local.at[9 + i]
+        )
+        for i in range(seq)
+    ]
+    for copy in keep_parts:
+        copy.start()
+
+    step = 256 if width % 256 == 0 else 128
+
+    def w2_grad(i, _):
+        cols = pl.ds(pl.multiple_of(i * step, 128), step)
+        value = dot(act[:, cols], gv[...].reshape(slots, D), ((0,), (0,)))
+        w2[pl.ds(pl.multiple_of(i * step, 128), step), :] = value.astype(BF16)
+        return 0
+
+    def w1_grad(i, _):
+        cols = pl.ds(pl.multiple_of(i * 256, 128), 256)
+        value = dot(second[:, cols], slope[...], ((0,), (0,)))
+        w1[pl.ds(pl.multiple_of(i * 256, 128), 256), :] = value.astype(BF16)
+        return 0
+
+    lax.fori_loop(0, width // step, w2_grad, 0)
+    if not whole_tiles(share, units):
+        for d in range(place.dp):
+            w2_split[d] = w2[d * units : (d + 1) * units, :]
+    r2 = ScatterDp(place, 1, dp_sems, w2_part, lambda j, zi: from_x2.at[j - 1, zi], total2, None)
+    r1 = ScatterDp(place, 2, dp_sems, w1_part, lambda j, zi: from_x1.at[j - 1, zi], total1, None)
+    r2.start_x()
+
+    scatter.core_copy(0).wait_recv()
+    value = ds[place.s].astype(F32) + from_core[0].astype(F32)
+    for j in range(1, place.ys):
+        scatter.y_copy(j, ds.at[place.s]).wait_recv()
+        value = value + from_y[j - 1].astype(F32)
+    mine = pl.ds(pl.multiple_of(lax.rem(place.s, joined) * rows, 8), rows)
+    middle = own[mine, :]
+    normal, spread = normalize(middle)
+    grad_two = gv[place.s].astype(F32)
+    grad_middle = grad_two + norm_backward(normal, spread, value * gain)
+    branch = grad_middle.astype(BF16)
+    gb[place.s] = branch
+    sums_ref[5:6] = jnp.sum(grad_two, axis=0, keepdims=True)
+    sums_ref[2:3] = jnp.sum(branch.astype(F32), axis=0, keepdims=True)
+    spread_out = GatherSeq(place, 1, seq_sems, gb.at[place.s], lambda s: gb.at[s])
+    spread_out.start()
+    middle_out[...] = middle
+    grad_out[...] = grad_middle
+
+    lax.fori_loop(0, D // 256, w1_grad, 0)
+    if not whole_tiles(share, units):
+        for d in range(place.dp):
+            w1_split[d] = w1[d * share : (d + 1) * share, :]
+    r1.start_x()
+    r2.fold_all()
+    keep = [
+        pltpu.make_async_copy(total2(zi), s2_out.at[zi], local.at[9 + seq + zi])
+        for zi in range(place.zs)
+    ] + [
+        pltpu.make_async_copy(total1(zi), s1_out.at[zi], local.at[9 + seq + place.zs + zi])
+        for zi in range(place.zs)
+    ]
+    for copy in keep[: place.zs]:
+        copy.start()
+    for j in range(1, place.ys):
+        spread_out.arrive_y(j)
+    r1.fold_all()
+    for copy in keep[place.zs :]:
+        copy.start()
+    for j in range(place.ys):
+        spread_out.arrive_core(j)
+    save = pltpu.make_async_copy(gb, gb_out, local.at[8])
+    save.start()
+    for j in range(place.ys):
+        scatter.core_copy(j).wait_send()
+    for j in range(1, place.ys):
+        scatter.y_copy(j, ds.at[place.s]).wait_send()
+    spread_out.drain()
+    r2.drain_x()
+    r1.drain_x()
+    for copy in (*keep_parts, *keep, save):
+        copy.wait()
+
+
+def feed(place, length, x, mix, cot, wo, w1, w2, vectors):
+    seq, rows, _ = x.shape
+    slots = seq * rows
+    chunk = chunk_of(slots)
+    width = w1.shape[1]
+    share, units = D // place.dp, width // place.dp
+    split = []
+    anyspace = pl.BlockSpec(memory_space=pl.ANY)
+    inside = pl.BlockSpec(memory_space=pltpu.VMEM)
+    vm = lambda *shape: pltpu.VMEM(shape, BF16)
+    if not whole_tiles(share, units):
+        split = [
+            vm(place.dp, share, width), vm(place.dp, units, D), vm(place.zs, share, width),
+            vm(place.zs, units, D),
+        ]
+    outs = [
+        ((seq, rows, D), BF16, anyspace),
+        ((rows, D), F32, inside),
+        ((rows, D), F32, inside),
+        ((seq, rows, D), BF16, anyspace),
+        ((place.zs, share, width), BF16, anyspace),
+        ((place.zs, units, D), BF16, anyspace),
+        ((8, D), F32, inside),
+    ]
+    return pl.pallas_call(
+        functools.partial(feed_kernel, place),
+        in_specs=[pl.BlockSpec(memory_space=pltpu.SMEM)] + [anyspace] * 6 + [inside],
+        out_specs=[spec for _, _, spec in outs],
+        out_shape=[jax.ShapeDtypeStruct(shape, kind) for shape, kind, _ in outs],
+        scratch_shapes=[
+            vm(seq, rows, D),
+            vm(D, slots),
+            vm(seq, rows, D),
+            vm(D, D),
+            vm(D, width),
+            vm(width, D),
+            vm(slots, D),
+            vm(slots, width),
+            vm(slots, width),
+            vm(slots, D),
+            vm(seq, rows, D),
+            pltpu.VMEM((chunk, D), F32),
+            vm(place.ys, rows, D),
+            vm(max(place.ys - 1, 1), rows, D),
+            vm(max(place.xs - 1, 1), place.zs, share, width),
+            vm(max(place.xs - 1, 1), place.zs, units, D),
+        ]
+        + split
+        + dp_semaphores(place, 3)
+        + seq_semaphores(place, 2)
+        + [pltpu.SemaphoreType.DMA((9 + seq + 2 * place.zs,))],
+        compiler_params=params(collective_id=1, has_side_effects=True),
+        name="feed",
+    )(length, x, mix, cot, wo, w1, w2, vectors)
+
+
+class SumSmall:
+    def __init__(self, place, values, landing, sems):
+        self.p, self.values, self.landing = place, values, landing
+        self.sends, self.recvs = sems
+        self.hops = [
+            [((place.d, place.partner))],
+            [(place.d, place.at_y(j, place.c)) for j in range(1, place.ys)],
+            [(place.at_x(j), place.s) for j in range(1, place.xs)],
+            [(place.at_z(k), place.s) for k in range(1, place.zs)],
+        ]
+
+    def copies(self, hop):
+        first = sum(len(peers) for peers in self.hops[:hop])
+        return [
+            (first + i, send(self.values.at[hop], self.landing.at[first + i],
+                             self.sends.at[first + i], self.recvs.at[first + i], peer))
+            for i, peer in enumerate(self.hops[hop])
+        ]
+
+    def start(self, hop):
+        for _, copy in self.copies(hop):
+            copy.start()
+
+    def fold(self, hop):
+        value = self.values[hop]
+        for i, copy in self.copies(hop):
+            copy.wait_recv()
+            value = value + self.landing[i]
+        return value
+
+    def drain(self):
+        for hop in range(4):
+            for _, copy in self.copies(hop):
+                copy.wait_send()
+
+
+def small_hops(place):
+    return 1 + (place.ys - 1) + (place.xs - 1) + (place.zs - 1)
+
+
+def tail_kernel(
+    place, vec_ref, sums_ref, lse_ref, middle_ref, gmid_ref,
+    qt_in, kt_in, k_in, v_in, gb_in, mix_in, wo_in, wq_in, normed_in, x_in, part_in, s1_in, s2_in,
+    layer_ref, input_ref, total_ref, w1_out, w2_out, wq_out, wo_out,
+    qt, kt, kn, vn, got, gbv, mixv, normed, wq, dqkv, wo_rows, gbs, dk_sum, dv_sum, xbuf, outp,
+    core_a, y_a, core_b, y_b, pq, po, xq, xo, tq, to, zq, zo, z1, z2, r1, r2, rq, ro, own1, own2,
+    values, landing, *rest,
+):
+    zsend, zrecv, xsend, xrecv, ssend, srecv, vsend, vrecv, local = rest[-9:]
+    place.locate()
+    seq, rows, _ = x_in.shape
+    slots = seq * rows
+    chunk = chunk_of(slots)
+    joined = chunk // rows
+    count = slots // chunk
+    heads = kt.shape[0]
+    wide = heads * HEAD_DIM
+    share = D // place.dp
+    place.barrier()
+    dp_sems, seq_sems = (zsend, zrecv, xsend, xrecv), (ssend, srecv)
+    e1 = gbv
+    if whole_tiles(share):
+        q_part = lambda d: pq.at[pl.ds(pl.multiple_of(d * share, 16), share), :]
+        o_part = lambda d: po.at[pl.ds(pl.multiple_of(d * share, 16), share), :]
+    else:
+        pq_split, po_split = rest[:2]
+        q_part, o_part = (lambda d: pq_split.at[d]), (lambda d: po_split.at[d])
+    g1 = ScatterDp(place, 0, dp_sems, None, None, lambda zi: s1_in.at[zi], lambda k: z1.at[k - 1])
+    g2 = ScatterDp(place, 1, dp_sems, None, None, lambda zi: s2_in.at[zi], lambda k: z2.at[k - 1])
+    gq = ScatterDp(place, 2, dp_sems, q_part, lambda j, zi: xq.at[j - 1, zi],
+                   lambda zi: tq.at[zi], lambda k: zq.at[k - 1])
+    go = ScatterDp(place, 3, dp_sems, o_part, lambda j, zi: xo.at[j - 1, zi],
+                   lambda zi: to.at[zi], lambda k: zo.at[k - 1])
+    out_sum = ScatterSeq(place, 0, seq_sems, lambda s: part_in.at[s], lambda j: core_a.at[j],
+                         lambda j: y_a.at[j - 1])
+    e1_sum = ScatterSeq(place, 1, seq_sems, lambda s: e1.at[s], lambda j: core_b.at[j],
+                        lambda j: y_b.at[j - 1])
+    final2 = GatherSeq(place, 2, seq_sems, r2, lambda s: w2_out.at[s])
+    final1 = GatherSeq(place, 3, seq_sems, r1, lambda s: w1_out.at[s])
+    final_o = GatherSeq(place, 4, seq_sems, ro, lambda s: wo_out.at[s])
+    final_q = GatherSeq(place, 5, seq_sems, rq, lambda s: wq_out.at[s])
+
+    first = [(gb_in, gbv), (wo_in.at[pl.ds(pl.multiple_of(place.s * wide, 16), wide), :], wo_rows),
+             (mix_in, mixv), (qt_in, qt), (kt_in, kt), (k_in, kn), (v_in, vn)]
+    later = [(normed_in, normed), (wq_in, wq), (s1_in.at[place.z], own1), (s2_in.at[place.z], own2)]
+    later += [(part_in.at[place.at_y(j, place.c)], outp.at[j]) for j in range(place.ys)]
+    loads = [
+        pltpu.make_async_copy(src, dst, local.at[i]) for i, (src, dst) in enumerate(first + later)
+    ]
+    free = len(loads)
+    for copy in loads:
+        copy.start()
+    g2.start_z()
+    g1.start_z()
+    for j in list(range(1, place.ys)) + [0]:
+        out_sum.core_copy(j).start()
+    for copy in loads[: len(first)]:
+        copy.wait()
+
+    def lines_of(index, size, step=16):
+        return pl.ds(pl.multiple_of(index * size, step), size)
+
+    def turn(i, _):
+        cols = pl.ds(pl.multiple_of(i * chunk, 128), chunk)
+        branch = gbv[pl.ds(i * joined, joined)].reshape(chunk, D)
+        got[:, cols] = dot(wo_rows[...], branch, ((1,), (1,))).astype(BF16)
+        for s in range(seq):
+
+            @pl.when(place.s == s)
+            def _():
+                gbs[lines_of(i, chunk), :] = branch[:, s * wide : (s + 1) * wide]
+
+        return 0
+
+    lax.fori_loop(0, count, turn, 0)
+
+    def wo_grad(i, _):
+        lines = pl.ds(pl.multiple_of(i * 256, 128), 256)
+        po[lines, :] = dot(mixv[lines, :], gbs[...]).astype(BF16)
+        return 0
+
+    lax.fori_loop(0, D // 256, wo_grad, 0)
+    if not whole_tiles(share):
+        for d in range(place.dp):
+            po_split[d] = po[d * share : (d + 1) * share, :]
+    go.start_x()
+
+    block = 256
+
+    def head_back(head):
+        part = slice(head * HEAD_DIM, (head + 1) * HEAD_DIM)
         dk_sum[...] = jnp.zeros_like(dk_sum)
         dv_sum[...] = jnp.zeros_like(dv_sum)
 
-    grad = got_ref[0]
-    delta = jnp.sum(grad.astype(F32) * mix_ref[0].astype(F32), axis=0, keepdims=True)
-    probs = jnp.exp2(dot(k_ref[0], qt_ref[0]) * QSCALE - lse_ref[0])
-    grad_probs = dot(v_ref[0], grad)
-    grad_scores = (probs * (grad_probs - delta)).astype(BF16)
-    dv_sum[...] += dot(probs.astype(BF16), grad, ((1,), (1,)))
-    dk_sum[...] += dot(grad_scores, qt_ref[0, :HEAD_DIM], ((1,), (1,)))
-    dqt_ref[0] = (dot(kt_ref[0], grad_scores) * SCALE).astype(BF16)
-
-    @pl.when(step == pl.num_programs(1) - 1)
-    def _():
-        dk_ref[0] = (dk_sum[...] * SCALE).astype(BF16)
-        dv_ref[0] = dv_sum[...].astype(BF16)
-
-
-def attend_back(qt, kt, k, v, grad_mix, mix, lse):
-    heads, _, slots = qt.shape
-    block = 256
-    turned = jax.ShapeDtypeStruct((heads, HEAD_DIM, slots), BF16)
-    part = jax.ShapeDtypeStruct((heads, slots, HEAD_DIM), BF16)
-    cols = pl.BlockSpec((1, HEAD_DIM, block), lambda h, i: (h, 0, i))
-    rows = pl.BlockSpec((1, slots, HEAD_DIM), lambda h, i: (h, 0, 0))
+        def one(i, _):
+            cols = pl.ds(pl.multiple_of(i * block, 128), block)
+            grad = got[part, cols]
+            own_rows = pl.ds(pl.multiple_of(place.s * wide + head * HEAD_DIM, 16), HEAD_DIM)
+            mixed = mixv[own_rows, cols]
+            delta = jnp.sum(grad.astype(F32) * mixed.astype(F32), axis=0, keepdims=True)
+            probs = jnp.exp2(dot(kn[head], qt[head, :, cols]) * QSCALE - lse_ref[head, :, cols])
+            grad_scores = (probs * (dot(vn[head], grad) - delta)).astype(BF16)
+            dv_sum[...] += dot(probs.astype(BF16), grad, ((1,), (1,)))
+            dk_sum[...] += dot(grad_scores, qt[head, :HEAD_DIM, cols], ((1,), (1,)))
+            turned = dot(kt[head], grad_scores) * SCALE
+            dqkv[pl.ds(pl.multiple_of(i * block, 128), block), part] = jnp.transpose(turned).astype(BF16)
+            return 0
+
+        lax.fori_loop(0, slots // block, one, 0)
+        dqkv[:, wide + head * HEAD_DIM : wide + (head + 1) * HEAD_DIM] = (
+            dk_sum[...] * SCALE
+        ).astype(BF16)
+        dqkv[:, 2 * wide + head * HEAD_DIM : 2 * wide + (head + 1) * HEAD_DIM] = dv_sum[...].astype(
+            BF16
+        )
+
+    def out_fold():
+        for j in range(1, place.ys):
+            out_sum.core_copy(j).wait_recv()
+            outp[j] = (outp[j].astype(F32) + core_a[j].astype(F32)).astype(BF16)
+            out_sum.y_copy(j, outp.at[j]).start()
+
+    def publish(group, own, result, final):
+        result[...] = group.finish(own).astype(BF16)
+        final.start()
+
+    for head in range(heads):
+        head_back(head)
+        if head == 0:
+            for copy in loads[len(first) :]:
+                copy.wait()
+            out_fold()
+            go.fold_all()
+            go.start_z()
+        if head == min(1, heads - 1):
+            publish(g2, own2, r2, final2)
+        if head == min(2, heads - 1):
+            publish(g1, own1, r1, final1)
+            publish(go, to.at[place.z], ro, final_o)
+
+    def q_grad(i, _):
+        cols = pl.ds(pl.multiple_of(i * 256, 128), 256)
+        pq[cols, :] = dot(normed[:, cols], dqkv[...], ((0,), (0,))).astype(BF16)
+        return 0
+
+    lax.fori_loop(0, D // 256, q_grad, 0)
+    if not whole_tiles(share):
+        for d in range(place.dp):
+            pq_split[d] = pq[d * share : (d + 1) * share, :]
+    gq.start_x()
+    total = sums_ref[...]
+    bias_sum = jnp.sum(dqkv[...].astype(F32), axis=0, keepdims=True)
+    values[0] = jnp.zeros_like(values[0])
+    values[0, 0:8] = total
+    values[0, pl.ds(8 + place.s, 1), :wide] = bias_sum[:, :wide]
+    values[0, pl.ds(8 + place.s, 1), wide : 2 * wide] = bias_sum[:, 2 * wide :]
+    values[0, pl.ds(8 + seq + place.s, 1), :] = total[7:8]
+    values[0, 7:8] = jnp.zeros((1, D), F32)
+
+    order = []
+    for j in list(range(1, place.ys)) + [0]:
+        if joined == 1:
+            order += [(place.at_y(j, 1 - place.c), j, False), (place.at_y(j, place.c), j, True)]
+        else:
+            order += [(lax.rem(place.y + j, place.ys), j, True)]
+
+    def x_load(at, slot):
+        return pltpu.make_async_copy(
+            x_in.at[pl.ds(at * joined, joined)], xbuf.at[slot], local.at[free + slot]
+        )
+
+    x_load(order[0][0], 0).start()
+    for step, (at, j, both) in enumerate(order):
+        slot = step % 2
+        if step + 1 < len(order):
+            x_load(order[step + 1][0], 1 - slot).start()
+        x_load(at, slot).wait()
+        grad = dot(dqkv[lines_of(at, chunk), :], wq[...].reshape(D, 3 * wide), ((1,), (1,)))
+        normal, spread = normalize(xbuf[slot].reshape(chunk, D).astype(F32))
+        values[0, 0:1] += jnp.sum(grad * normal, axis=0, keepdims=True)
+        values[0, 1:2] += jnp.sum(grad, axis=0, keepdims=True)
+        e1[pl.ds(at * joined, joined)] = grad.astype(BF16).reshape(joined, rows, D)
+        if joined == 2 or not both:
+            e1_sum.core_copy(j).start()
+        if both and j:
+            target = place.at_y(j, place.c)
+            e1_sum.core_copy(j).wait_recv()
+            e1[target] = (e1[target].astype(F32) + core_b[j].astype(F32)).astype(BF16)
+            e1_sum.y_copy(j, e1.at[target]).start()
+    small = SumSmall(place, values, landing, (vsend, vrecv))
+    small.start(0)
+    gq.fold_all()
+    gq.start_z()
+    for hop in range(3):
+        values[hop + 1] = small.fold(hop)
+        small.start(hop + 1)
+    for final in (final2, final1, final_o):
+        for j in range(1, place.ys):
+            final.arrive_y(j)
+
+    value = outp[0].astype(F32)
+    out_sum.core_copy(0).wait_recv()
+    value = value + core_a[0].astype(F32)
+    for j in range(1, place.ys):
+        out_sum.y_copy(j, outp.at[j]).wait_recv()
+        value = value + y_a[j - 1].astype(F32)
+    layer_ref[...] = (middle_ref[...] + (value + vec_ref[5:6])).astype(BF16)
+
+    value = e1[place.s].astype(F32)
+    e1_sum.core_copy(0).wait_recv()
+    value = value + core_b[0].astype(F32)
+    for j in range(1, place.ys):
+        e1_sum.y_copy(j, e1.at[place.s]).wait_recv()
+        value = value + y_b[j - 1].astype(F32)
+    last = (len(order) - 1) % 2
+    hidden = xbuf[last, lax.rem(place.s, joined)].astype(F32)
+    normal, spread = normalize(hidden)
+    input_ref[...] = (gmid_ref[...] + norm_backward(normal, spread, value * vec_ref[0:1])).astype(
+        BF16
+    )
+    total_ref[...] = small.fold(3)
+    publish(gq, tq.at[place.z], rq, final_q)
+    keep = [
+        pltpu.make_async_copy(src, dst.at[place.s], local.at[free + 2 + i])
+        for i, (src, dst) in enumerate([(r1, w1_out), (r2, w2_out), (rq, wq_out), (ro, wo_out)])
+    ]
+    for copy in keep:
+        copy.start()
+    for final in (final2, final1, final_o):
+        for j in range(place.ys):
+            final.arrive_core(j)
+    for j in range(1, place.ys):
+        final_q.arrive_y(j)
+    for j in range(place.ys):
+        final_q.arrive_core(j)
+    for final in (final1, final2, final_o, final_q):
+        final.drain()
+    for group in (out_sum, e1_sum):
+        for j in range(place.ys):
+            group.core_copy(j).wait_send()
+        for j in range(1, place.ys):
+            group.y_copy(j, outp.at[j]).wait_send()
+    for group in (gq, go):
+        group.drain_x()
+    for group in (g1, g2, gq, go):
+        group.drain_z()
+    small.drain()
+    for copy in keep:
+        copy.wait()
+
+
+def tail(place, vectors, sums, lse, middle, gmid, qt, kt, kn, vn, gb, mix, wo, wq, normed, x, part, s1, s2):
+    seq, rows, _ = x.shape
+    slots = seq * rows
+    chunk = chunk_of(slots)
+    joined = chunk // rows
+    heads = kt.shape[0]
+    wide = heads * HEAD_DIM
+    share = D // place.dp
+    width, units = s1.shape[2], s2.shape[1]
+    ys, xs, zs = place.ys, max(place.xs - 1, 1), place.zs
+    anyspace = pl.BlockSpec(memory_space=pl.ANY)
+    inside = pl.BlockSpec(memory_space=pltpu.VMEM)
+    vm = lambda *shape: pltpu.VMEM(shape, BF16)
+    tall = 8 + 2 * seq
+    hops = small_hops(place)
+    outs = [
+        ((rows, D), BF16, inside),
+        ((rows, D), BF16, inside),
+        ((tall, D), F32, inside),
+        ((seq, share, width), BF16, anyspace),
+        ((seq, units, D), BF16, anyspace),
+        ((seq, share, 3 * wide), BF16, anyspace),
+        ((seq, share, wide), BF16, anyspace),
+    ]
+    split = []
+    if not whole_tiles(share):
+        split = [vm(place.dp, share, 3 * wide), vm(place.dp, share, wide)]
     return pl.pallas_call(
-        attend_back_kernel,
-        grid=(heads, slots // block),
-        in_specs=[
-            pl.BlockSpec((1, 128, block), lambda h, i: (h, 0, i)),
-            pl.BlockSpec((1, HEAD_DIM, slots), lambda h, i: (h, 0, 0)),
-            pl.BlockSpec((1, slots, 128), lambda h, i: (h, 0, 0)),
-            rows,
-            cols,
-            cols,
-            pl.BlockSpec((1, 1, block), lambda h, i: (h, 0, i)),
+        functools.partial(tail_kernel, place),
+        in_specs=[inside] * 5 + [anyspace] * 13,
+        out_specs=[spec for _, _, spec in outs],
+        out_shape=[jax.ShapeDtypeStruct(shape, kind) for shape, kind, _ in outs],
+        scratch_shapes=[
+            vm(heads, 128, slots),
+            vm(heads, HEAD_DIM, slots),
+            vm(heads, slots, 128),
+            vm(heads, slots, HEAD_DIM),
+            vm(wide, slots),
+            vm(seq, rows, D),
+            vm(D, slots),
+            vm(slots, D),
+            vm(place.dp, share, 3 * wide),
+            vm(slots, 3 * wide),
+            vm(wide, D),
+            vm(slots, wide),
+            pltpu.VMEM((slots, HEAD_DIM), F32),
+            pltpu.VMEM((slots, HEAD_DIM), F32),
+            vm(2, joined, rows, D),
+            vm(ys, rows, D),
+            vm(ys, rows, D),
+            vm(max(ys - 1, 1), rows, D),
+            vm(ys, rows, D),
+            vm(max(ys - 1, 1), rows, D),
+            vm(D, 3 * wide),
+            vm(D, wide),
+            vm(xs, zs, share, 3 * wide),
+            vm(xs, zs, share, wide),
+            vm(zs, share, 3 * wide),
+            vm(zs, share, wide),
+            vm(zs - 1, share, 3 * wide),
+            vm(zs - 1, share, wide),
+            vm(zs - 1, share, width),
+            vm(zs - 1, units, D),
+            vm(share, width),
+            vm(units, D),
+            vm(share, 3 * wide),
+            vm(share, wide),
+            vm(share, width),
+            vm(units, D),
+            pltpu.VMEM((4, tall, D), F32),
+            pltpu.VMEM((hops, tall, D), F32),
+        ]
+        + split
+        + dp_semaphores(place, 4)
+        + seq_semaphores(place, 6)
+        + [
+            pltpu.SemaphoreType.DMA((hops,)),
+            pltpu.SemaphoreType.DMA((hops,)),
+            pltpu.SemaphoreType.DMA((24 + ys,)),
         ],
-        out_specs=[cols, rows, rows],
-        scratch_shapes=[pltpu.VMEM((slots, HEAD_DIM), F32), pltpu.VMEM((slots, HEAD_DIM), F32)],
-        out_shape=[turned, part, part],
-        compiler_params=params(),
-        name="attend_back",
-    )(qt, kt, k, v, grad_mix, mix, lse)
-
-
-def feed_kernel(
-    place_ref, x_ref, mix_ref, cot_ref, wo_ref, w1_ref, w2_ref, bo_ref, gain_ref, shift_ref, b1_ref,
-    out_ref, ds_ref, second_ref, act_ref, de_ref, middle_ref, gain_sum, shift_sum, b1_sum,
-):
-    step = pl.program_id(0)
-    count = pl.num_programs(0)
-    block = x_ref.shape[0]
-    owner = lax.rem(place_ref[0] + 1 + step, count)
-
-    @pl.when(step == 0)
-    def _():
-        gain_sum[...] = jnp.zeros_like(gain_sum)
-        shift_sum[...] = jnp.zeros_like(shift_sum)
-        b1_sum[...] = jnp.zeros_like(b1_sum)
-
-    middle = x_ref[...].astype(F32) + (dot(mix_ref[...], wo_ref[...], ((0,), (0,))) + bo_ref[...])
-    middle_ref[...] = middle
-    unit, _ = normalize(middle)
-    second = (unit * gain_ref[...] + shift_ref[...]).astype(BF16)
-    second_ref[...] = second
-    valid = owner * block + lax.broadcasted_iota(jnp.int32, (block, 1), 0) < place_ref[1]
-    grad_two = jnp.where(valid, cot_ref[...].astype(F32), 0.0).astype(BF16)
-    expanded = dot(second, w1_ref[...]) + b1_ref[...]
-    phi = 0.5 * (1.0 + lax.erf(expanded * (0.5**0.5)))
-    activated = (expanded * phi).astype(BF16)
-    act_ref[...] = activated
-    slope = phi + expanded * (jnp.exp(-0.5 * expanded * expanded) * 0.3989422804014327)
-    out_ref[...] = dot(activated, w2_ref[...]).astype(BF16)
-    grad_act = dot(grad_two, w2_ref[...], ((1,), (1,)))
-    grad_expanded = (grad_act * slope).astype(BF16)
-    de_ref[...] = grad_expanded
-    b1_sum[...] += jnp.sum(grad_expanded.astype(F32), axis=0, keepdims=True)
-    grad_second = dot(grad_expanded, w1_ref[...], ((1,), (1,)))
-    ds_ref[...] = grad_second.astype(BF16)
-    gain_sum[...] += jnp.sum(grad_second * unit, axis=0, keepdims=True)
-    shift_sum[...] += jnp.sum(grad_second, axis=0, keepdims=True)
-
-
-def feed(place, x, mix, cot, wo, w1, w2, bo, gain, shift, b1):
-    slots = x.shape[0]
-    block = chunk_of(slots)
-    count = slots // block
-    width = w1.shape[1]
-
-    def turn(i, place):
-        return lax.rem(place[0] + 1 + i, count)
-
-    rows = pl.BlockSpec((block, D), lambda i, p: (turn(i, p), 0))
-    wide = pl.BlockSpec((block, width), lambda i, p: (turn(i, p), 0))
-    return pl.pallas_call(
-        feed_kernel,
-        grid_spec=pltpu.PrefetchScalarGridSpec(
-            num_scalar_prefetch=1,
-            grid=(count,),
-            in_specs=[
-                rows,
-                pl.BlockSpec((D, block), lambda i, p: (0, turn(i, p))),
-                rows,
-                whole(wo.shape), whole(w1.shape), whole(w2.shape)]
-            + [whole((1, D))] * 3
-            + [whole((1, width))],
-            out_specs=[
-                rows,
-                rows,
-                rows,
-                wide,
-                wide,
-                pl.BlockSpec((block, D), lambda i, p: (0, 0)),
-                pl.BlockSpec((1, D), lambda i, p: (0, 0)),
-                pl.BlockSpec((1, D), lambda i, p: (0, 0)),
-                pl.BlockSpec((1, width), lambda i, p: (0, 0)),
-            ],
-        ),
-        out_shape=[
-            jax.ShapeDtypeStruct((slots, D), BF16),
-            jax.ShapeDtypeStruct((slots, D), BF16),
-            jax.ShapeDtypeStruct((slots, D), BF16),
-            jax.ShapeDtypeStruct((slots, width), BF16),
-            jax.ShapeDtypeStruct((slots, width), BF16),
-            jax.ShapeDtypeStruct((block, D), F32),
-            jax.ShapeDtypeStruct((1, D), F32),
-            jax.ShapeDtypeStruct((1, D), F32),
-            jax.ShapeDtypeStruct((1, width), F32),
-        ],
-        compiler_params=params(),
-        name="feed",
-    )(place, x, mix, cot, wo, w1, w2, bo, gain, shift, b1)
+        compiler_params=params(collective_id=2, has_side_effects=True),
+        name="tail",
+    )(vectors, sums, lse, middle, gmid, qt, kt, kn, vn, gb, mix, wo, wq, normed, x, part, s1, s2)
 
 
 def gather(value, axes, axis=0):
@@ -633,131 +1203,52 @@
     )
     w2_share = lax.dynamic_slice_in_dim(reduce_weight, me * units, units, 0)
     (
-        x, cot, small, w_qkv, w_out, w_expand, w_reduce, normed, qt, kt, keys, values, mix, lse,
-    ) = front(spot, length, hidden_own, cotangent[0], small, wqkv_share, output_weight, w1_share, w2_share)
-    x, cot = (value.reshape(slots, D) for value in (x, cot))
-    w_qkv = w_qkv.reshape(D, width)
+        x, cot, small, w_qkv, w_out, w_expand, normed, qt, kt, keys, values, mix, lse,
+    ) = front(spot, length, hidden_own, cotangent[0], small, wqkv_share, output_weight, w1_share)
     w_out = w_out.reshape(D, D)
     w_expand = w_expand.reshape(D, quarter)
-    w_reduce = w_reduce.reshape(quarter, D)
     vectors = jnp.sum(small.astype(F32), axis=0)
-    gain_one, shift_one, bias_out, gain_two, shift_two, bias_reduce = (
-        vectors[i : i + 1] for i in range(6)
+    mix = mix.reshape(D, slots)
+    grad_branch, middle, grad_middle, out_part, s1, s2, sums = feed(
+        spot, length, x, mix, cot, w_out, w_expand, w2_share, vectors
     )
-    bias_expand = vectors[6:7, :quarter]
-    mix_own = lax.dynamic_index_in_dim(mix, me, 0, keepdims=False)
-    mix = mix.reshape(D, slots)
-    joined = chunk_of(slots) // rows_here
-    place = jnp.stack([me.astype(jnp.int32) // joined, length[0]])
-    (
-        out_part, ds_part, second, act, grad_expanded, middle_own, gain_two_grad, shift_two_grad,
-        bias_expand_grad,
-    ) = feed(
-        place, x, mix, cot, w_out, w_expand, w_reduce, bias_out, gain_two, shift_two,
-        bias_expand,
+    layer_output, input_grad, totals, w1_grad, w2_grad, qkv_grad, wo_grad = tail(
+        spot, vectors, sums, lse, middle, grad_middle, qt, kt, keys, values, grad_branch, mix,
+        w_out, w_qkv, normed, x, out_part, s1, s2,
     )
-    middle_own = lax.dynamic_slice_in_dim(
-        middle_own, lax.rem(me.astype(jnp.int32), joined) * rows_here, rows_here, 0
-    )
-    positions = jnp.arange(slots, dtype=jnp.int32)
-    valid = (positions < length)[:, None]
-    grad_two = jnp.where(valid, cot, 0).astype(BF16)
-    grad_out = lax.dynamic_slice_in_dim(grad_two, me * rows_here, rows_here, 0).astype(F32)
-
-    layer_output = (
-        middle_own + (scatter_sum(out_part, "seq").astype(F32) + bias_reduce)
-    ).astype(BF16)
-    grad_second = scatter_sum(ds_part, "seq").astype(F32)
-    unit_two, spread_two = normalize(middle_own)
-    grad_middle = grad_out + norm_backward(unit_two, spread_two, grad_second * gain_two)
-    grad_branch = grad_middle.astype(BF16)
-    reduce_bias_grad = jnp.sum(grad_out, axis=0)
-    output_bias_grad = jnp.sum(grad_branch.astype(F32), axis=0)
-
-    w1_grad = dot(second, grad_expanded, ((0,), (0,))).astype(BF16)
-    w2_grad = dot(act, grad_two, ((0,), (0,))).astype(BF16)
-    w1_grad = scatter_sum(w1_grad, "dp")
-    w2_grad = scatter_sum(w2_grad, "dp")
-
-    grad_branch_all = gather(grad_branch, "seq")
-    wo_grad = dot(mix, columns(grad_branch_all)).astype(BF16)
-    wo_rows = lax.dynamic_slice_in_dim(w_out, me * head_cols, head_cols, 0)
-    grad_mix = dot(wo_rows, grad_branch_all, ((1,), (1,))).astype(BF16)
-    dqt, dk, dv = attend_back(
-        qt, kt, keys, values, grad_mix.reshape(heads, HEAD_DIM, slots), mix_own, lse
-    )
-    dqkv = jnp.concatenate(
-        [
-            dqt.reshape(head_cols, slots).T,
-            jnp.concatenate([dk, dv], axis=0).transpose(1, 0, 2).reshape(slots, 2 * head_cols),
-        ],
-        axis=1,
-    )
-    qkv_grad = dot(normed, dqkv, ((0,), (0,))).astype(BF16)
-    bias_qkv_grad = jnp.sum(dqkv.astype(F32), axis=0)
-    grad_normed = dot(dqkv, w_qkv, ((1,), (1,)))
-    unit_all, _ = normalize(x.astype(F32))
-    gain_one_grad = jnp.sum(grad_normed * unit_all, axis=0)
-    shift_one_grad = jnp.sum(grad_normed, axis=0)
-    grad_normed_own = scatter_sum(grad_normed.astype(BF16), "seq").astype(F32)
-    unit_one, spread_one = normalize(hidden_own.astype(F32))
-    grad_front = grad_middle + norm_backward(unit_one, spread_one, grad_normed_own * gain_one)
-    input_grad = grad_front.astype(BF16)
-
-    def mine(value):
-        return lax.dynamic_update_slice_in_dim(
-            jnp.zeros((D,), F32), value.reshape(-1), me * head_cols, 0
-        )
-
-    expand_vec = lax.dynamic_update_slice_in_dim(
-        jnp.zeros((dp, FF // dp), F32), bias_expand_grad.reshape(dp, units), me * units, 1
-    )
-    vectors = [
-        gain_one_grad, shift_one_grad, mine(bias_qkv_grad[:head_cols]),
-        mine(bias_qkv_grad[2 * head_cols :]), output_bias_grad, gain_two_grad.reshape(-1),
-        shift_two_grad.reshape(-1), reduce_bias_grad,
-    ]
-    small_grad = jnp.concatenate([v.reshape(dp, share) for v in vectors] + [expand_vec], axis=1)
-    small_grad = jnp.pad(
-        small_grad.astype(BF16), ((0, 0), (0, (tall - share) * width - small_grad.shape[1]))
-    ).reshape(dp, tall - share, width)
-    packed_grad = jnp.concatenate([qkv_grad.reshape(dp, share, width), small_grad], axis=1)
-    packed_grad = scatter_sum(packed_grad, "dp")[0]
-    wo_grad = scatter_sum(wo_grad, "dp")
-
-    packed_grad = gather(packed_grad[None], "seq")
-    wo_grad = gather(wo_grad[None], "seq")
-    w1_grad = gather(w1_grad[None], "seq")
-    w2_grad = gather(w2_grad, "seq").astype(F32)
+
+    def own(vector):
+        return lax.dynamic_slice_in_dim(vector.reshape(-1), mine_dp * share, share, 0)
+
+    w2_grad = w2_grad.reshape(FF // dp, D).astype(F32)
     w1_grad = (
         w1_grad.reshape(seq, share, dp, units).transpose(1, 2, 0, 3).reshape(share, FF).astype(F32)
     )
     wo_grad = wo_grad.transpose(1, 0, 2).reshape(share, D).astype(F32)
-    qkv_grad = packed_grad[:, :share].reshape(seq, share, 3, head_cols).astype(F32)
+    qkv_grad = qkv_grad.reshape(seq, share, 3, head_cols).astype(F32)
     qkv_grad = qkv_grad.transpose(2, 1, 0, 3).reshape(3, share, D)
-    small_grad = jnp.sum(
-        packed_grad[:, share : share + extra].reshape(seq, extra * width).astype(F32), axis=0
-    )
-    pieces = [small_grad[i * share : (i + 1) * share] for i in range(8)]
-    expand_bias_grad = small_grad[8 * share : 8 * share + FF // dp]
+    bias = totals[8 : 8 + seq]
+    expand_bias_grad = lax.dynamic_slice_in_dim(
+        totals[8 + seq : 8 + 2 * seq, :quarter].reshape(seq, dp, units), mine_dp, 1, 1
+    ).reshape(FF // dp)
     return (
         layer_output[None],
         input_grad[None],
-        pieces[0],
-        pieces[1],
+        own(totals[0]),
+        own(totals[1]),
         qkv_grad[0],
-        pieces[2],
+        own(bias[:, :head_cols]),
         qkv_grad[1],
         qkv_grad[2],
-        pieces[3],
+        own(bias[:, head_cols : 2 * head_cols]),
         wo_grad,
-        pieces[4],
-        pieces[5],
-        pieces[6],
+        own(totals[2]),
+        own(totals[3]),
+        own(totals[4]),
         w1_grad,
         expand_bias_grad,
         w2_grad,
-        pieces[7],
+        own(totals[5]),
     )
 
 

time: 720 us -> 573 us (0.80)
  waiting for transfers between devices: 265 us -> 0 us
  Pallas kernels: 245 us -> 490 us
  matrix products: 47.9 us -> 0 us
  other arithmetic: 50.7 us -> 7.28 us
  between operations: 17.3 us -> 1.85 us
  local copies, waits for them, and re-layouts: 76.8 us -> 65.1 us
  blocking collectives: 7.46 us -> 0 us
    pallas_call x2, Pallas kernels: 68.5 us -> 348 us  [the longest x1 182 us: tail(): pl.pallas_call(functools.partial(tail_kernel, place), in_specs=[inside] *...]
    reduce_scatter x7 -> x0, waiting for transfers between devices: 258 us -> none  [scatter_sum(): return lax.psum_scatter(value, axes, scatter_dimension=axis, tiled=True)]
    dot_general x6 -> x0, matrix products: 47.9 us -> none  [dot(): lax.dot_general(left, right, (contract, ((), ())), preferred_element_type...]
    pallas_call x1, Pallas kernels: 177 us -> 141 us  [front(): pl.pallas_call(functools.partial(front_kernel, place), in_specs=[pl.Block...]
    reduce_sum x11 -> x0, other arithmetic: 23.2 us -> none  [the longest x2 5.71 us: norm_backward(): jnp.mean(grad_unit, axis=-1, keepdims=True)]
    transpose x2 -> x0, other arithmetic: 7.6 us -> none  [the longest x1 4.16 us: per_device(): jnp.concatenate([dk, dv], axis=0).transpose(1, 0, 2)]
    all_gather x1 -> x0, blocking collectives: 7.46 us -> none  [gather(): return lax.all_gather(value, axes, axis=axis, tiled=True)]
  transfers between devices with their start and end apart: 11 -> 0, of which waited for: 7 -> 0; matrix products, arithmetic and copies ran while one was open for 20% -> 0% of each run, Pallas kernels for 4% -> 0%
where the time goes in v3:
time: 573 us; the launch traced here: 564 us
  Pallas kernels  490 us (86%)
  local copies, waits for them, and re-layouts  65.1 us (11%)
  other arithmetic  7.28 us (1%)
    pallas_call x1, Pallas kernels, tail(): pl.pallas_call(functools.partial(tail_kernel, place), in_specs=[inside] *...  182 us
    pallas_call x1, Pallas kernels, feed(): pl.pallas_call(functools.partial(feed_kernel, place), in_specs=[pl.BlockS...  166 us
    pallas_call x1, Pallas kernels, front(): pl.pallas_call(functools.partial(front_kernel, place), in_specs=[pl.Block...  141 us
    convert_element_type x3, local copies, waits for them, and re-layouts, per_device(): w1_grad.reshape(seq, share, dp, units).transpose(1, 2, 0, 3)  20.5 us

profile of v3, /device:TPU:0, one launch (start us, length us, event | category | flops | bytes accessed | tf_op | source)
XLA Modules:
  0.0 563.8 jit_solution(9735457024808534868)
XLA Ops:
  1.4 1.3 fusion.1
  10.6 1.3 stack.50.sm_in
  12.1 1.0 constant_dynamic-slice_fusion.17
  13.1 1.0 constant_dynamic-slice_fusion.16
  15.0 1.8 constant_dynamic-slice_fusion.7.w2_in
  16.7 1.6 constant_dynamic-slice_fusion.8
  18.3 1.1 concatenate.7.w1_in
  19.4 141.4 %front.1 = (bf16[4,384,1280]{2,1,0:T(8,128)(2,1)}, bf16[4,384,1280]{2,1,0:T(8,128)(2,1)}, bf16[8,16,1280]{2,1,0:T(8,128)(2,1)}, bf16[8,160,960]{2,1,0:T(8,128)(2...) custom-call(s32[1]{0:T(128)} %bitcast.1.length_ref, ...), custom_call_target="tpu_custom_call" | custom-call | tf_op jit(solution)/shard_map/front/pallas_call | solution.py:395
  160.8 1.7 convert_reduce_fusion.vec_ref
  162.5 166.5 %feed.1 = (bf16[4,384,1280]{2,1,0:T(8,128)(2,1)}, f32[384,1280]{1,0:T(8,128)}, f32[384,1280]{1,0:T(8,128)}, bf16[4,384,1280]{2,1,0:T(8,128)(2,1)}, bf16[4,160,12...) custom-call(s32[1]{0:T(128)} %bitcast.1.length_ref, ...), custom_call_target="tpu_custom_call" | custom-call | tf_op jit(solution)/shard_map/feed/pallas_call | solution.py:731
  329.0 181.7 %tail.1 = (bf16[384,1280]{1,0:T(8,128)(2,1)}, bf16[384,1280]{1,0:T(8,128)(2,1)}, f32[16,1280]{1,0:T(8,128)}, bf16[4,160,1280]{2,1,0:T(8,128)(2,1)}, bf16[4,160,1...) custom-call(f32[16,1280]{1,0:T(8,128)} %convert_reduce_fusion.vec_ref, ...), custom_call_target="tpu_custom_call" | custom-call | tf_op jit(solution)/shard_map/tail/pallas_call | solution.py:1081
  513.8 1.1 fusion.3
  517.6 1.2 convert_bitcast_fusion
  519.5 1.5 reshape.108
  521.0 2.3 bitcast_convert_fusion
  523.2 3.6 reshape.111
  526.9 7.3 %fusion.2 = (f32[1,160,4,320]{3,0,1,2:T(1,128)S(1)}, f32[1,160,4,320]{3,0,1,2:T(1,128)S(1)}, f32[1,160,4,320]{3,0,1,2:T(1,128)S(1)}) fusion(f32[3,160,4,320]{3,0,1,2:T(4,128)} %bitcast.28), kind=kLoop, calls=%fused_computation.26 | loop fusion | bytes 4915200 | tf_op jit(solution)/shard_map/slice | solution.py:1242
  534.8 1.5 squeeze.29
  537.0 1.5 squeeze.28
  539.1 1.5 squeeze.27
  540.6 4.5 reshape.112
  545.1 8.2 %copy.46 = f32[160,8,4,160]{3,2,1,0:T(4,128)} copy(f32[160,8,4,160]{3,1,0,2:T(8,128)} %bitcast.23) | data formatting | bytes 6553600 | tf_op jit(solution)/shard_map/convert_element_type | solution.py:1225
  553.3 7.8 %reshape.109 = f32[160,5120]{1,0:T(8,128)} reshape(f32[160,8,4,160]{3,2,1,0:T(4,128)} %copy.46) | data formatting | bytes 6553600 | tf_op jit(solution)/shard_map/convert_element_type | solution.py:1225
  561.1 0.9 copy.61
  (68 shorter events, 18.7 us)
Async XLA Ops:
  0.7 11.3 %copy-start = (bf16[160,1280]{1,0:T(8,128)(2,1)S(1)}, bf16[160,1280]{1,0:T(8,128)(2,1)}, u32[]{:S(2)}) copy-start(bf16[160,1280]{1,0:T(8,128)(2,1)} %param.25) | copy-start | bytes 1228804
  517.6 3.4 copy-start.2
  521.0 2.3 copy-start.4
  539.1 1.5 copy-start.3
  553.3 7.8 %copy-start.6 = (bf16[384,1280]{1,0:T(8,128)(2,1)S(1)}, bf16[384,1280]{1,0:T(8,128)(2,1)}, u32[]{:S(2)}) copy-start(bf16[384,1280]{1,0:T(8,128)(2,1)} %get-tuple-element.64) | copy-start | bytes 2949124
  553.3 10.3 %copy-start.1 = (bf16[160,1280]{1,0:T(8,128)(2,1)S(1)}, bf16[160,1280]{1,0:T(8,128)(2,1)}, u32[]{:S(2)}) copy-start(bf16[160,1280]{1,0:T(8,128)(2,1)} %param.25) | copy-start | bytes 1228804
  561.1 1.6 copy-start.5

commit v4 on v3

--- a/solution.py
+++ b/solution.py
@@ -114,14 +114,19 @@
 
 
 class GatherDp:
-    def __init__(self, place, group, sems, own, slab):
-        self.p, self.g, self.own, self.slab = place, group, own, slab
+    def __init__(self, place, group, sems, own, slab, on=None):
+        self.p, self.g, self.own, self.slab, self.on = place, group, own, slab, on
         self.zsend, self.zrecv, self.xsend, self.xrecv = sems
 
+    def when(self, block, act):
+        if self.on is None:
+            act()
+        else:
+            pl.when(self.on(block))(act)
+
     def z_copy(self, k):
-        src = self.own
-        return send(src, self.slab(self.p.d), self.zsend.at[self.g, k], self.zrecv.at[self.g, k],
-                    (self.p.at_z(k), self.p.s))
+        return send(self.own, self.slab(self.p.d), self.zsend.at[self.g, k],
+                    self.zrecv.at[self.g, k], (self.p.at_z(k), self.p.s))
 
     def x_copy(self, k, j):
         block = self.p.block(k, 0)
@@ -129,18 +134,30 @@
         return send(src, self.slab(block), self.xsend.at[self.g, k, j],
                     self.xrecv.at[self.g, k, j], (self.p.at_x(j), self.p.s))
 
-    def start(self):
-        for j in range(1, self.p.xs):
-            self.x_copy(0, j).start()
-        for k in range(self.p.zs - 1, 0, -1):
-            self.z_copy(k).start()
+    def start_x(self):
+        def act():
+            for j in range(1, self.p.xs):
+                self.x_copy(0, j).start()
+
+        self.when(self.p.d, act)
+
+    def start_z(self):
+        def act():
+            for k in range(self.p.zs - 1, 0, -1):
+                self.z_copy(k).start()
+
+        self.when(self.p.d, act)
 
     def forward(self, k):
         place = self.p
-        send(self.own, self.slab(place.block(k, 0)), self.zsend.at[self.g, k],
-             self.zrecv.at[self.g, k], (place.at_z(k), place.s)).wait_recv()
-        for j in range(1, place.xs):
-            self.x_copy(k, j).start()
+
+        def act():
+            send(self.own, self.slab(place.block(k, 0)), self.zsend.at[self.g, k],
+                 self.zrecv.at[self.g, k], (place.at_z(k), place.s)).wait_recv()
+            for j in range(1, place.xs):
+                self.x_copy(k, j).start()
+
+        self.when(place.block(k, 0), act)
 
     def forward_all(self):
         for k in range(1, self.p.zs):
@@ -150,16 +167,21 @@
         place = self.p
         for k in range(place.zs):
             for j in range(1, place.xs):
-                send(self.own, self.slab(place.block(k, j)), self.xsend.at[self.g, k, j],
-                     self.xrecv.at[self.g, k, j], (place.at_x(j), place.s)).wait_recv()
+                wait = send(self.own, self.slab(place.block(k, j)), self.xsend.at[self.g, k, j],
+                            self.xrecv.at[self.g, k, j], (place.at_x(j), place.s)).wait_recv
+                self.when(place.block(k, j), wait)
 
     def drain(self):
         place = self.p
-        for k in range(1, place.zs):
-            self.z_copy(k).wait_send()
+
+        def act():
+            for k in range(1, place.zs):
+                self.z_copy(k).wait_send()
+
+        self.when(place.d, act)
         for k in range(place.zs):
             for j in range(1, place.xs):
-                self.x_copy(k, j).wait_send()
+                self.when(place.block(k, 0), self.x_copy(k, j).wait_send)
 
 
 class GatherSeq:
@@ -210,9 +232,16 @@
 QSCALE = SCALE * LOG2E
 
 
+def own_length(lengths_ref, order_ref):
+    length = 0
+    for clip in range(lengths_ref.shape[0]):
+        length = length + jnp.where(order_ref[0] == clip, lengths_ref[clip], 0)
+    return length
+
+
 def front_kernel(
-    place, length_ref, x_in, cot_in, sm_in, wq_in, wo_in, w1_in,
-    x_out, cot_out, sm_out, wq_out, wo_out, w1_out, normed_out, qt_out, kt_out, k_out,
+    place, lengths_ref, order_ref, x_in, sm_in, wq_in, wo_in, w1_in,
+    x_out, vec_out, wq_out, wo_out, w1_out, normed_out, qt_out, kt_out, k_out,
     v_out, mix_out, lse_ref,
     xs, nr, sm, wq, wt, qt, kt, vt, kn, vn, mix,
     zsend, zrecv, xsend, xrecv, ssend, srecv, local,
@@ -234,31 +263,35 @@
 
     g_sm = over_dp(0, sm_in, sm)
     g_wq = over_dp(1, wq_in, wq)
-    g_wo = over_dp(2, wo_in, wo_out)
+    g_wo = GatherDp(place, 2, dp_sems, wo_in, lambda d: wo_out.at[d],
+                    lambda d: lax.rem(d, seq) == place.s)
     g_w1 = over_dp(3, w1_in, w1_out)
     g_x = over_seq(0, x_in, xs)
-    g_cot = over_seq(1, cot_in, cot_out)
-
+    wo_sets = [
+        GatherSeq(place, 1 + heads + i, seq_sems, wo_out.at[i * seq + place.s],
+                  lambda s, i=i: wo_out.at[i * seq + s])
+        for i in range(place.dp // seq)
+    ]
     locals_in = [
         pltpu.make_async_copy(x_in, xs.at[place.s], local.at[0]),
         pltpu.make_async_copy(sm_in, sm.at[place.d], local.at[1]),
         pltpu.make_async_copy(wq_in, wq.at[place.d], local.at[2]),
     ]
-    own_blocks = [
-        pltpu.make_async_copy(cot_in, cot_out.at[place.s], local.at[3]),
-        pltpu.make_async_copy(wo_in, wo_out.at[place.d], local.at[4]),
-        pltpu.make_async_copy(w1_in, w1_out.at[place.d], local.at[5]),
-    ]
+    w1_own = pltpu.make_async_copy(w1_in, w1_out.at[place.d], local.at[5])
+    wo_own = pltpu.make_async_copy(wo_in, wo_out.at[place.d], local.at[4])
     for copy in locals_in:
         copy.start()
-    g_sm.start()
+    g_sm.start_x()
+    g_sm.start_z()
     g_x.start()
-    g_wq.start()
-    for copy in own_blocks:
-        copy.start()
+    g_wq.start_x()
+    for group in (g_wq, g_wo, g_w1):
+        group.start_z()
+    w1_own.start()
+    pl.when(g_wo.on(place.d))(wo_own.start)
 
     column = lax.broadcasted_iota(jnp.int32, (slots, 1), 0)
-    penalty = jnp.where(column >= length_ref[0], -1e30, 0.0).astype(BF16)
+    penalty = jnp.where(column >= own_length(lengths_ref, order_ref), -1e30, 0.0).astype(BF16)
     ones_row = jnp.where(
         lax.broadcasted_iota(jnp.int32, (128 - HEAD_DIM, slots), 0) == 0, 1.0, 0.0
     ).astype(BF16)
@@ -271,11 +304,11 @@
         copy.wait()
     g_sm.forward_all()
     g_wq.forward_all()
-    g_wo.start()
-    g_w1.start()
-    g_cot.start()
+    g_wo.start_x()
+    g_w1.start_x()
     g_sm.arrive()
-    vectors = jnp.sum(sm[...].astype(F32), axis=0)
+    vectors = jnp.sum(sm[...], axis=0)
+    vec_out[...] = vectors
     gain, shift = vectors[0:1], vectors[1:2]
 
     def norm_block(block):
@@ -315,7 +348,7 @@
     results = [
         pltpu.make_async_copy(src, dst, local.at[7 + i])
         for i, (src, dst) in enumerate(
-            [(xs, x_out), (sm, sm_out), (wq, wq_out), (nr, normed_out), (qt, qt_out), (kt, kt_out),
+            [(xs, x_out), (wq, wq_out), (nr, normed_out), (qt, qt_out), (kt, kt_out),
              (kn, k_out), (vn, v_out)]
         )
     ]
@@ -323,6 +356,11 @@
         copy.start()
 
     block = 256
+    g_wo.forward_all()
+    g_wo.arrive()
+    pl.when(g_wo.on(place.d))(wo_own.wait)
+    for group in wo_sets:
+        group.start()
 
     def attend(head):
         def one(i, _):
@@ -339,7 +377,7 @@
         lax.fori_loop(0, slots // block, one, 0)
 
     g_mix = [
-        GatherSeq(place, 2 + head, seq_sems, mix.at[place.s, head],
+        GatherSeq(place, 1 + head, seq_sems, mix.at[place.s, head],
                   lambda s, head=head: mix.at[s, head])
         for head in range(heads)
     ]
@@ -347,11 +385,13 @@
         attend(head)
         g_mix[head].start()
         if head == 0:
-            g_wo.forward_all()
-            for j in range(1, place.ys):
-                g_cot.arrive_y(j)
-        if head == 1:
-            g_w1.forward_all()
+            g_w1.forward(1)
+        if head == min(1, heads - 1):
+            for group in wo_sets:
+                for j in range(1, place.ys):
+                    group.arrive_y(j)
+            for k in range(2, place.zs):
+                g_w1.forward(k)
     for head in range(heads):
         for j in range(1, place.ys):
             g_mix[head].arrive_y(j)
@@ -360,17 +400,17 @@
             g_mix[head].arrive_core(j)
     mix_copy = pltpu.make_async_copy(mix, mix_out, local.at[15])
     mix_copy.start()
-    for j in range(place.ys):
-        g_cot.arrive_core(j)
-    for group in (g_wo, g_w1):
-        group.arrive()
-    for group in (g_sm, g_wq, g_wo, g_w1, g_x, g_cot, *g_mix):
+    for group in wo_sets:
+        for j in range(place.ys):
+            group.arrive_core(j)
+    g_w1.arrive()
+    for group in (g_sm, g_wq, g_wo, g_w1, g_x, *wo_sets, *g_mix):
         group.drain()
-    for copy in (*own_blocks, *results, mix_copy):
+    for copy in (w1_own, *results, mix_copy):
         copy.wait()
 
 
-def front(place, length, x, cot, small, wqkv, wo, w1):
+def front(place, lengths, order, x, small, wqkv, wo, w1):
     dp, seq = place.dp, place.seq
     rows = x.shape[0]
     slots = rows * seq
@@ -379,8 +419,7 @@
     anyspace = pl.BlockSpec(memory_space=pl.ANY)
     shapes = [
         (seq, rows, D),
-        (seq, rows, D),
-        (dp, *small.shape),
+        small.shape,
         (dp, share, width),
         (dp, *wo.shape),
         (dp, *w1.shape),
@@ -394,14 +433,18 @@
     vm = lambda *shape: pltpu.VMEM(shape, BF16)
     return pl.pallas_call(
         functools.partial(front_kernel, place),
-        in_specs=[pl.BlockSpec(memory_space=pltpu.SMEM)] + [anyspace] * 6,
-        out_specs=[anyspace] * len(shapes) + [pl.BlockSpec(memory_space=pltpu.VMEM)],
-        out_shape=[jax.ShapeDtypeStruct(shape, BF16) for shape in shapes]
+        in_specs=[pl.BlockSpec(memory_space=pltpu.SMEM)] * 2 + [anyspace] * 5,
+        out_specs=[anyspace, pl.BlockSpec(memory_space=pltpu.VMEM)]
+        + [anyspace] * (len(shapes) - 2)
+        + [pl.BlockSpec(memory_space=pltpu.VMEM)],
+        out_shape=[
+            jax.ShapeDtypeStruct(shape, F32 if i == 1 else BF16) for i, shape in enumerate(shapes)
+        ]
         + [jax.ShapeDtypeStruct((heads, 1, slots), F32)],
         scratch_shapes=[
             vm(seq, rows, D),
             vm(slots, D),
-            vm(dp, *small.shape),
+            pltpu.VMEM((dp, *small.shape), F32),
             vm(dp, share, width),
             vm(width, D),
             vm(heads, 128, slots),
@@ -412,11 +455,11 @@
             vm(seq, heads, HEAD_DIM, slots),
         ]
         + dp_semaphores(place, 4)
-        + seq_semaphores(place, 2 + heads)
+        + seq_semaphores(place, 1 + heads + dp // seq)
         + [pltpu.SemaphoreType.DMA((16,))],
         compiler_params=params(collective_id=0, has_side_effects=True),
         name="front",
-    )(length, x, cot, small, wqkv, wo, w1)
+    )(lengths, order, x, small, wqkv, wo, w1)
 
 
 class ScatterSeq:
@@ -437,59 +480,57 @@
 
 
 class ScatterDp:
-    def __init__(self, place, group, sems, part, from_x, total, from_z):
-        self.p, self.g = place, group
-        self.part, self.from_x, self.total, self.from_z = part, from_x, total, from_z
+    def __init__(self, place, group, sems, out, part, from_x, from_z):
+        self.p, self.g, self.out, self.part = place, group, out, part
+        self.from_x, self.from_z = from_x, from_z
         self.zsend, self.zrecv, self.xsend, self.xrecv = sems
-
-    def x_copy(self, j, zi):
+        self.order = list(range(1, place.zs)) + [0]
+
+    def block(self, k, j):
         place = self.p
-        target = lax.rem(place.x + j, place.xs)
-        return send(self.part(zi * place.xs + target), self.from_x(j, zi),
-                    self.xsend.at[self.g, zi, j], self.xrecv.at[self.g, zi, j],
-                    (place.at_x(j), place.s))
+        return lax.rem(place.z + k, place.zs) * place.xs + lax.rem(place.x + j, place.xs)
+
+    def x_copy(self, j, k):
+        return send(self.out(self.block(k, j)), self.from_x(j - 1, k),
+                    self.xsend.at[self.g, k, j], self.xrecv.at[self.g, k, j],
+                    (self.p.at_x(j), self.p.s))
 
     def start_x(self):
-        for zi in range(self.p.zs):
+        for k in self.order:
             for j in range(1, self.p.xs):
-                self.x_copy(j, zi).start()
-
-    def fold(self, zi):
-        place = self.p
-        value = self.part(zi * place.xs + place.x)[...].astype(F32)
-        for j in range(1, place.xs):
-            self.x_copy(j, zi).wait_recv()
-            value = value + self.from_x(j, zi)[...].astype(F32)
-        self.total(zi)[...] = value.astype(BF16)
+                self.x_copy(j, k).start()
+
+    def z_copy(self, k):
+        return send(self.part(k, self.block(k, 0)), self.from_z(k - 1),
+                    self.zsend.at[self.g, k], self.zrecv.at[self.g, k], (self.p.at_z(k), self.p.s))
+
+    def fold(self, k):
+        own = self.part(k, self.block(k, 0))
+        value = own[...].astype(F32)
+        for j in range(1, self.p.xs):
+            self.x_copy(j, k).wait_recv()
+            value = value + self.from_x(j - 1, k)[...].astype(F32)
+        own[...] = value.astype(BF16)
+        if k:
+            self.z_copy(k).start()
 
     def fold_all(self):
-        for zi in range(self.p.zs):
-            self.fold(zi)
-
-    def z_copy(self, k):
-        place = self.p
-        return send(self.total(lax.rem(place.z + k, place.zs)), self.from_z(k),
-                    self.zsend.at[self.g, k], self.zrecv.at[self.g, k], (place.at_z(k), place.s))
-
-    def start_z(self):
-        for k in range(self.p.zs - 1, 0, -1):
-            self.z_copy(k).start()
-
-    def finish(self, own):
-        value = own[...].astype(F32)
+        for k in self.order:
+            self.fold(k)
+
+    def finish(self):
+        value = self.part(0, self.block(0, 0))[...].astype(F32)
         for k in range(1, self.p.zs):
             self.z_copy(k).wait_recv()
-            value = value + self.from_z(k)[...].astype(F32)
-        return value
-
-    def drain_x(self):
-        for zi in range(self.p.zs):
+            value = value + self.from_z(k - 1)[...].astype(F32)
+        return value.astype(BF16)
+
+    def drain(self):
+        for k in self.order:
             for j in range(1, self.p.xs):
-                self.x_copy(j, zi).wait_send()
-
-    def drain_z(self):
-        for k in range(1, self.p.zs):
-            self.z_copy(k).wait_send()
+                self.x_copy(j, k).wait_send()
+            if k:
+                self.z_copy(k).wait_send()
 
 
 def whole_tiles(*heights):
@@ -497,10 +538,10 @@
 
 
 def feed_kernel(
-    place, length_ref, x_in, mix_in, cot_in, wo_in, w1_in, w2_in, vec_ref,
-    gb_out, middle_out, grad_out, part_out, s1_out, s2_out, sums_ref,
+    place, lengths_ref, order_ref, x_in, mix_in, cot_in, wo_in, w1_in, w2_in, vec_ref,
+    gb_out, middle_out, grad_out, part_out, g1_out, s2_ref, sums_ref,
     xa, mixv, gv, wo, w1, w2, second, act, slope, unit, ds, own, from_core, from_y,
-    from_x1, from_x2, *rest,
+    from_x2, from_z2, *rest,
 ):
     zsend, zrecv, xsend, xrecv, ssend, srecv, local = rest[-7:]
     gb = xa
@@ -515,25 +556,29 @@
     place.barrier()
     dp_sems = (zsend, zrecv, xsend, xrecv)
     seq_sems = (ssend, srecv)
-    if whole_tiles(share, units):
-        w1_part = lambda d: w1.at[pl.ds(pl.multiple_of(d * share, 16), share), :]
+    aligned = whole_tiles(share, units)
+    if aligned:
         w2_part = lambda d: w2.at[pl.ds(pl.multiple_of(d * units, 16), units), :]
-        total1 = lambda zi: wo.at[pl.ds(zi * share, share), pl.ds(0, width)]
-        total2 = lambda zi: wo.at[pl.ds(place.zs * share + zi * units, units), :]
+        g2_part = lambda d: wo.at[pl.ds(pl.multiple_of(d * units, 16), units), :]
+        g1_part = lambda d: w1.at[pl.ds(pl.multiple_of(d * share, 16), share), :]
     else:
-        w1_split, w2_split, total1_split, total2_split = rest[:4]
-        w1_part, w2_part = (lambda d: w1_split.at[d]), (lambda d: w2_split.at[d])
-        total1, total2 = (lambda zi: total1_split.at[zi]), (lambda zi: total2_split.at[zi])
+        w2_split, g2_split, g1_split = rest[:3]
+        w2_part, g2_part = (lambda d: w2_split.at[d]), (lambda d: g2_split.at[d])
+        g1_part = lambda d: g1_split.at[d]
+    if aligned:
+        w2_in = w2_in.at[pl.ds(pl.multiple_of(place.s * units, 16), units), :]
     gather = GatherDp(place, 0, dp_sems, w2_in, w2_part)
-    gather.start()
+    cots = GatherSeq(place, 2, seq_sems, cot_in, lambda s: gv.at[s])
+    gather.start_x()
+    gather.start_z()
+    cots.start()
     loads = [
         pltpu.make_async_copy(src, dst, local.at[i])
-        for i, (src, dst) in enumerate(
-            [(mix_in, mixv), (wo_in, wo), (w1_in, w1), (cot_in, gv), (x_in, xa)]
-        )
+        for i, (src, dst) in enumerate([(mix_in, mixv), (wo_in, wo), (w1_in, w1), (x_in, xa)])
     ]
     w2_own = pltpu.make_async_copy(w2_in, w2_part(place.d), local.at[5])
-    for copy in (*loads, w2_own):
+    cot_own = pltpu.make_async_copy(cot_in, gv.at[place.s], local.at[6])
+    for copy in (*loads, w2_own, cot_own):
         copy.start()
     gain, shift, bias_out, bias1 = vec_ref[3:4], vec_ref[4:5], vec_ref[2:3], vec_ref[6:7, :width]
     own_chunk = place.s // joined
@@ -563,20 +608,49 @@
         act[lines, :] = (expanded * phi).astype(BF16)
         density = jnp.exp(-0.5 * expanded * expanded) * 0.3989422804014327
         slope[lines, :] = (phi + expanded * density).astype(BF16)
-        valid = (
-            i * chunk + lax.broadcasted_iota(jnp.int32, (chunk, 1), 0) < length_ref[0]
-        )
+        return 0
+
+    lax.fori_loop(0, slots // chunk, forward, 0)
+    cot_own.wait()
+    for j in range(1, place.ys):
+        cots.arrive_y(j)
+    for j in range(place.ys):
+        cots.arrive_core(j)
+    cots.drain()
+
+    length = own_length(lengths_ref, order_ref)
+
+    def mask(i, _):
+        valid = i * chunk + lax.broadcasted_iota(jnp.int32, (chunk, 1), 0) < length
         cot = gv[pl.ds(i * joined, joined)].reshape(chunk, D)
         gv[pl.ds(i * joined, joined)] = jnp.where(valid, cot.astype(F32), 0.0).astype(BF16).reshape(
             joined, rows, D
         )
         return 0
 
-    lax.fori_loop(0, slots // chunk, forward, 0)
-    gather.forward_all()
+    lax.fori_loop(0, slots // chunk, mask, 0)
+    gather.forward(1)
+
+    step = 256 if width % 256 == 0 else 128
+
+    def w2_grad(i, _):
+        cols = pl.ds(pl.multiple_of(i * step, 128), step)
+        value = dot(act[:, cols], gv[...].reshape(slots, D), ((0,), (0,)))
+        wo[pl.ds(pl.multiple_of(i * step, 128), step), :] = value.astype(BF16)
+        return 0
+
+    lax.fori_loop(0, width // step, w2_grad, 0)
+    for k in range(2, place.zs):
+        gather.forward(k)
+    if not aligned:
+        for d in range(place.dp):
+            g2_split[d] = wo[d * units : (d + 1) * units, :]
+    r2 = ScatterDp(place, 1, dp_sems, g2_part, lambda k, d: g2_part(d),
+                   lambda j, k: from_x2.at[j, k], lambda k: from_z2.at[k])
+    r2.start_x()
     w2_own.wait()
     gather.arrive()
-    if not whole_tiles(share, units):
+    if not aligned:
         for d in range(place.dp):
             w2[d * units : (d + 1) * units, :] = w2_split[d]
 
@@ -628,13 +702,7 @@
     for copy in keep_parts:
         copy.start()
 
-    step = 256 if width % 256 == 0 else 128
-
-    def w2_grad(i, _):
-        cols = pl.ds(pl.multiple_of(i * step, 128), step)
-        value = dot(act[:, cols], gv[...].reshape(slots, D), ((0,), (0,)))
-        w2[pl.ds(pl.multiple_of(i * step, 128), step), :] = value.astype(BF16)
-        return 0
+    r2.fold(r2.order[0])
 
     def w1_grad(i, _):
         cols = pl.ds(pl.multiple_of(i * 256, 128), 256)
@@ -642,14 +710,18 @@
         w1[pl.ds(pl.multiple_of(i * 256, 128), 256), :] = value.astype(BF16)
         return 0
 
-    lax.fori_loop(0, width // step, w2_grad, 0)
-    if not whole_tiles(share, units):
+    lax.fori_loop(0, D // 256, w1_grad, 0)
+    if not aligned:
         for d in range(place.dp):
-            w2_split[d] = w2[d * units : (d + 1) * units, :]
-    r2 = ScatterDp(place, 1, dp_sems, w2_part, lambda j, zi: from_x2.at[j - 1, zi], total2, None)
-    r1 = ScatterDp(place, 2, dp_sems, w1_part, lambda j, zi: from_x1.at[j - 1, zi], total1, None)
-    r2.start_x()
-
+            g1_split[d] = w1[d * share : (d + 1) * share, :]
+    keep = [
+        pltpu.make_async_copy(g1_part(d), g1_out.at[d], local.at[9 + seq + d])
+        for d in range(place.dp)
+    ]
+    for copy in keep:
+        copy.start()
+    for k in r2.order[1:-1]:
+        r2.fold(k)
     scatter.core_copy(0).wait_recv()
     value = ds[place.s].astype(F32) + from_core[0].astype(F32)
     for j in range(1, place.ys):
@@ -669,26 +741,10 @@
     middle_out[...] = middle
     grad_out[...] = grad_middle
 
-    lax.fori_loop(0, D // 256, w1_grad, 0)
-    if not whole_tiles(share, units):
-        for d in range(place.dp):
-            w1_split[d] = w1[d * share : (d + 1) * share, :]
-    r1.start_x()
-    r2.fold_all()
-    keep = [
-        pltpu.make_async_copy(total2(zi), s2_out.at[zi], local.at[9 + seq + zi])
-        for zi in range(place.zs)
-    ] + [
-        pltpu.make_async_copy(total1(zi), s1_out.at[zi], local.at[9 + seq + place.zs + zi])
-        for zi in range(place.zs)
-    ]
-    for copy in keep[: place.zs]:
-        copy.start()
+    r2.fold(0)
     for j in range(1, place.ys):
         spread_out.arrive_y(j)
-    r1.fold_all()
-    for copy in keep[place.zs :]:
-        copy.start()
+    s2_ref[...] = r2.finish()
     for j in range(place.ys):
         spread_out.arrive_core(j)
     save = pltpu.make_async_copy(gb, gb_out, local.at[8])
@@ -698,13 +754,12 @@
     for j in range(1, place.ys):
         scatter.y_copy(j, ds.at[place.s]).wait_send()
     spread_out.drain()
-    r2.drain_x()
-    r1.drain_x()
+    r2.drain()
     for copy in (*keep_parts, *keep, save):
         copy.wait()
 
 
-def feed(place, length, x, mix, cot, wo, w1, w2, vectors):
+def feed(place, lengths, order, x, mix, cot, wo, w1, w2, vectors):
     seq, rows, _ = x.shape
     slots = seq * rows
     chunk = chunk_of(slots)
@@ -716,21 +771,20 @@
     vm = lambda *shape: pltpu.VMEM(shape, BF16)
     if not whole_tiles(share, units):
         split = [
-            vm(place.dp, share, width), vm(place.dp, units, D), vm(place.zs, share, width),
-            vm(place.zs, units, D),
+            vm(place.dp, units, D), vm(place.dp, units, D), vm(place.dp, share, width),
         ]
     outs = [
         ((seq, rows, D), BF16, anyspace),
         ((rows, D), F32, inside),
         ((rows, D), F32, inside),
         ((seq, rows, D), BF16, anyspace),
-        ((place.zs, share, width), BF16, anyspace),
-        ((place.zs, units, D), BF16, anyspace),
+        ((place.dp, share, width), BF16, anyspace),
+        ((units, D), BF16, inside),
         ((8, D), F32, inside),
     ]
     return pl.pallas_call(
         functools.partial(feed_kernel, place),
-        in_specs=[pl.BlockSpec(memory_space=pltpu.SMEM)] + [anyspace] * 6 + [inside],
+        in_specs=[pl.BlockSpec(memory_space=pltpu.SMEM)] * 2 + [anyspace] * 6 + [inside],
         out_specs=[spec for _, _, spec in outs],
         out_shape=[jax.ShapeDtypeStruct(shape, kind) for shape, kind, _ in outs],
         scratch_shapes=[
@@ -748,16 +802,16 @@
             pltpu.VMEM((chunk, D), F32),
             vm(place.ys, rows, D),
             vm(max(place.ys - 1, 1), rows, D),
-            vm(max(place.xs - 1, 1), place.zs, share, width),
             vm(max(place.xs - 1, 1), place.zs, units, D),
+            vm(place.zs - 1, units, D),
         ]
         + split
-        + dp_semaphores(place, 3)
-        + seq_semaphores(place, 2)
-        + [pltpu.SemaphoreType.DMA((9 + seq + 2 * place.zs,))],
+        + dp_semaphores(place, 2)
+        + seq_semaphores(place, 3)
+        + [pltpu.SemaphoreType.DMA((9 + seq + place.dp,))],
         compiler_params=params(collective_id=1, has_side_effects=True),
         name="feed",
-    )(length, x, mix, cot, wo, w1, w2, vectors)
+    )(lengths, order, x, mix, cot, wo, w1, w2, vectors)
 
 
 class SumSmall:
@@ -802,10 +856,10 @@
 
 def tail_kernel(
     place, vec_ref, sums_ref, lse_ref, middle_ref, gmid_ref,
-    qt_in, kt_in, k_in, v_in, gb_in, mix_in, wo_in, wq_in, normed_in, x_in, part_in, s1_in, s2_in,
+    qt_in, kt_in, k_in, v_in, gb_in, mix_in, wo_in, wq_in, normed_in, x_in, part_in, g1_in, s2_in,
     layer_ref, input_ref, total_ref, w1_out, w2_out, wq_out, wo_out,
     qt, kt, kn, vn, got, gbv, mixv, normed, wq, dqkv, wo_rows, gbs, dk_sum, dv_sum, xbuf, outp,
-    core_a, y_a, core_b, y_b, pq, po, xq, xo, tq, to, zq, zo, z1, z2, r1, r2, rq, ro, own1, own2,
+    core_a, y_a, core_b, y_b, pq, po, p1, xq, xo, x1, zq, zo, z1, r1, rq, ro,
     values, landing, *rest,
 ):
     zsend, zrecv, xsend, xrecv, ssend, srecv, vsend, vrecv, local = rest[-9:]
@@ -827,24 +881,25 @@
     else:
         pq_split, po_split = rest[:2]
         q_part, o_part = (lambda d: pq_split.at[d]), (lambda d: po_split.at[d])
-    g1 = ScatterDp(place, 0, dp_sems, None, None, lambda zi: s1_in.at[zi], lambda k: z1.at[k - 1])
-    g2 = ScatterDp(place, 1, dp_sems, None, None, lambda zi: s2_in.at[zi], lambda k: z2.at[k - 1])
-    gq = ScatterDp(place, 2, dp_sems, q_part, lambda j, zi: xq.at[j - 1, zi],
-                   lambda zi: tq.at[zi], lambda k: zq.at[k - 1])
-    go = ScatterDp(place, 3, dp_sems, o_part, lambda j, zi: xo.at[j - 1, zi],
-                   lambda zi: to.at[zi], lambda k: zo.at[k - 1])
+    g1 = ScatterDp(place, 0, dp_sems, lambda d: g1_in.at[d], lambda k, d: p1.at[k],
+                   lambda j, k: x1.at[j, k], lambda k: z1.at[k])
+    gq = ScatterDp(place, 1, dp_sems, q_part, lambda k, d: q_part(d),
+                   lambda j, k: xq.at[j, k], lambda k: zq.at[k])
+    go = ScatterDp(place, 2, dp_sems, o_part, lambda k, d: o_part(d),
+                   lambda j, k: xo.at[j, k], lambda k: zo.at[k])
     out_sum = ScatterSeq(place, 0, seq_sems, lambda s: part_in.at[s], lambda j: core_a.at[j],
                          lambda j: y_a.at[j - 1])
     e1_sum = ScatterSeq(place, 1, seq_sems, lambda s: e1.at[s], lambda j: core_b.at[j],
                         lambda j: y_b.at[j - 1])
-    final2 = GatherSeq(place, 2, seq_sems, r2, lambda s: w2_out.at[s])
+    final2 = GatherSeq(place, 2, seq_sems, s2_in, lambda s: w2_out.at[s])
     final1 = GatherSeq(place, 3, seq_sems, r1, lambda s: w1_out.at[s])
     final_o = GatherSeq(place, 4, seq_sems, ro, lambda s: wo_out.at[s])
     final_q = GatherSeq(place, 5, seq_sems, rq, lambda s: wq_out.at[s])
 
     first = [(gb_in, gbv), (wo_in.at[pl.ds(pl.multiple_of(place.s * wide, 16), wide), :], wo_rows),
              (mix_in, mixv), (qt_in, qt), (kt_in, kt), (k_in, kn), (v_in, vn)]
-    later = [(normed_in, normed), (wq_in, wq), (s1_in.at[place.z], own1), (s2_in.at[place.z], own2)]
+    later = [(normed_in, normed), (wq_in, wq)]
+    later += [(g1_in.at[g1.block(k, 0)], p1.at[k]) for k in range(place.zs)]
     later += [(part_in.at[place.at_y(j, place.c)], outp.at[j]) for j in range(place.ys)]
     loads = [
         pltpu.make_async_copy(src, dst, local.at[i]) for i, (src, dst) in enumerate(first + later)
@@ -852,8 +907,7 @@
     free = len(loads)
     for copy in loads:
         copy.start()
-    g2.start_z()
-    g1.start_z()
+    g1.start_x()
     for j in list(range(1, place.ys)) + [0]:
         out_sum.core_copy(j).start()
     for copy in loads[: len(first)]:
@@ -922,8 +976,8 @@
             outp[j] = (outp[j].astype(F32) + core_a[j].astype(F32)).astype(BF16)
             out_sum.y_copy(j, outp.at[j]).start()
 
-    def publish(group, own, result, final):
-        result[...] = group.finish(own).astype(BF16)
+    def publish(group, result, final):
+        result[...] = group.finish()
         final.start()
 
     for head in range(heads):
@@ -932,13 +986,14 @@
             for copy in loads[len(first) :]:
                 copy.wait()
             out_fold()
+            final2.start()
+            g1.fold(g1.order[0])
+        if head == min(1, heads - 1):
+            for k in g1.order[1:-1]:
+                g1.fold(k)
+        if head == heads - 1:
+            g1.fold(0)
             go.fold_all()
-            go.start_z()
-        if head == min(1, heads - 1):
-            publish(g2, own2, r2, final2)
-        if head == min(2, heads - 1):
-            publish(g1, own1, r1, final1)
-            publish(go, to.at[place.z], ro, final_o)
 
     def q_grad(i, _):
         cols = pl.ds(pl.multiple_of(i * 256, 128), 256)
@@ -992,7 +1047,8 @@
     small = SumSmall(place, values, landing, (vsend, vrecv))
     small.start(0)
     gq.fold_all()
-    gq.start_z()
+    publish(g1, r1, final1)
+    publish(go, ro, final_o)
     for hop in range(3):
         values[hop + 1] = small.fold(hop)
         small.start(hop + 1)
@@ -1021,10 +1077,10 @@
         BF16
     )
     total_ref[...] = small.fold(3)
-    publish(gq, tq.at[place.z], rq, final_q)
+    publish(gq, rq, final_q)
     keep = [
         pltpu.make_async_copy(src, dst.at[place.s], local.at[free + 2 + i])
-        for i, (src, dst) in enumerate([(r1, w1_out), (r2, w2_out), (rq, wq_out), (ro, wo_out)])
+        for i, (src, dst) in enumerate([(r1, w1_out), (s2_in, w2_out), (rq, wq_out), (ro, wo_out)])
     ]
     for copy in keep:
         copy.start()
@@ -1042,16 +1098,14 @@
             group.core_copy(j).wait_send()
         for j in range(1, place.ys):
             group.y_copy(j, outp.at[j]).wait_send()
-    for group in (gq, go):
-        group.drain_x()
-    for group in (g1, g2, gq, go):
-        group.drain_z()
+    for group in (g1, gq, go):
+        group.drain()
     small.drain()
     for copy in keep:
         copy.wait()
 
 
-def tail(place, vectors, sums, lse, middle, gmid, qt, kt, kn, vn, gb, mix, wo, wq, normed, x, part, s1, s2):
+def tail(place, vectors, sums, lse, middle, gmid, qt, kt, kn, vn, gb, mix, wo, wq, normed, x, part, g1, s2):
     seq, rows, _ = x.shape
     slots = seq * rows
     chunk = chunk_of(slots)
@@ -1059,7 +1113,7 @@
     heads = kt.shape[0]
     wide = heads * HEAD_DIM
     share = D // place.dp
-    width, units = s1.shape[2], s2.shape[1]
+    width, units = g1.shape[2], s2.shape[0]
     ys, xs, zs = place.ys, max(place.xs - 1, 1), place.zs
     anyspace = pl.BlockSpec(memory_space=pl.ANY)
     inside = pl.BlockSpec(memory_space=pltpu.VMEM)
@@ -1106,42 +1160,161 @@
             vm(max(ys - 1, 1), rows, D),
             vm(D, 3 * wide),
             vm(D, wide),
+            vm(zs, share, width),
             vm(xs, zs, share, 3 * wide),
             vm(xs, zs, share, wide),
-            vm(zs, share, 3 * wide),
-            vm(zs, share, wide),
+            vm(xs, zs, share, width),
             vm(zs - 1, share, 3 * wide),
             vm(zs - 1, share, wide),
             vm(zs - 1, share, width),
-            vm(zs - 1, units, D),
             vm(share, width),
-            vm(units, D),
             vm(share, 3 * wide),
             vm(share, wide),
-            vm(share, width),
-            vm(units, D),
             pltpu.VMEM((4, tall, D), F32),
             pltpu.VMEM((hops, tall, D), F32),
         ]
         + split
-        + dp_semaphores(place, 4)
+        + dp_semaphores(place, 3)
         + seq_semaphores(place, 6)
         + [
             pltpu.SemaphoreType.DMA((hops,)),
             pltpu.SemaphoreType.DMA((hops,)),
-            pltpu.SemaphoreType.DMA((24 + ys,)),
+            pltpu.SemaphoreType.DMA((24 + ys + zs,)),
         ],
         compiler_params=params(collective_id=2, has_side_effects=True),
         name="tail",
-    )(vectors, sums, lse, middle, gmid, qt, kt, kn, vn, gb, mix, wo, wq, normed, x, part, s1, s2)
-
-
-def gather(value, axes, axis=0):
-    return lax.all_gather(value, axes, axis=axis, tiled=True)
-
-
-def scatter_sum(value, axes, axis=0):
-    return lax.psum_scatter(value, axes, scatter_dimension=axis, tiled=True)
+    )(vectors, sums, lse, middle, gmid, qt, kt, kn, vn, gb, mix, wo, wq, normed, x, part, g1, s2)
+
+
+def prep_kernel(place, q_ref, k_ref, v_ref, w1_ref, vec_ref, b1_ref, small_ref, wqkv_ref, w1_out):
+    place.locate()
+    dp, seq = place.dp, place.seq
+    share = D // dp
+    wide = D // seq
+    units = FF // (dp * seq)
+    small_ref[...] = jnp.zeros_like(small_ref)
+    for s in range(seq):
+
+        @pl.when(place.s == s)
+        def _():
+            for i, ref in enumerate((q_ref, k_ref, v_ref)):
+                wqkv_ref[:, i * wide : (i + 1) * wide] = ref[:, s * wide : (s + 1) * wide]
+            for d in range(dp):
+                first = d * (FF // dp) + s * units
+                w1_out[:, d * units : (d + 1) * units] = w1_ref[:, first : first + units]
+
+    vec = vec_ref[...]
+    for d in range(dp):
+        home = (d * share) // wide
+        first = d * share - home * wide
+
+        @pl.when(place.d == d)
+        def _():
+            small_ref[0:6, d * share : (d + 1) * share] = vec[0:6]
+            small_ref[6:7, d * units : (d + 1) * units] = b1_ref[pl.ds(place.s, 1), :]
+
+            @pl.when(place.s == home)
+            def _():
+                small_ref[8:10, first : first + share] = vec[6:8]
+
+
+def prep(place, q, k, v, w1, vectors, b1):
+    wide = D // place.seq
+    share = q.shape[0]
+    inside = pl.BlockSpec(memory_space=pltpu.VMEM)
+    return pl.pallas_call(
+        functools.partial(prep_kernel, place),
+        in_specs=[inside] * 6,
+        out_specs=[inside] * 3,
+        out_shape=[
+            jax.ShapeDtypeStruct((16, D), F32),
+            jax.ShapeDtypeStruct((share, 3 * wide), BF16),
+            jax.ShapeDtypeStruct((share, FF // place.seq), BF16),
+        ],
+        compiler_params=params(),
+        name="prep",
+    )(q, k, v, w1, vectors, b1)
+
+
+def finish_kernel(
+    place, w1_ref, w2_ref, wq_ref, wo_ref, total_ref, layer_ref, input_ref,
+    layer_out, input_out, w1_out, w2_out, q_out, k_out, v_out, wo_out, g1_out, s1_out, bo_out, g2_out, s2_out, b2_out,
+    bq_out, bv_out, b1_out, lines,
+):
+    place.locate()
+    dp, seq = place.dp, place.seq
+    share = D // dp
+    wide = D // seq
+    units = FF // (dp * seq)
+    w2_out[...] = w2_ref[...].astype(F32)
+    for s in range(seq):
+        cols = slice(s * wide, (s + 1) * wide)
+        for i, out in enumerate((q_out, k_out, v_out)):
+            out[:, cols] = wq_ref[s, :, i * wide : (i + 1) * wide].astype(F32)
+        wo_out[:, cols] = wo_ref[s].astype(F32)
+        for d in range(dp):
+            first = d * (FF // dp) + s * units
+            w1_out[:, first : first + units] = w1_ref[s, :, d * units : (d + 1) * units].astype(F32)
+
+    @pl.when(pl.program_id(0) == 0)
+    def _():
+        layer_out[...] = layer_ref[...]
+        input_out[...] = input_ref[...]
+        lines[...] = total_ref[0:8]
+        for s in range(seq):
+            cols = slice(s * wide, (s + 1) * wide)
+            lines[6:7, cols] = total_ref[8 + s : 9 + s, :wide]
+            lines[7:8, cols] = total_ref[8 + s : 9 + s, wide : 2 * wide]
+        outs = (g1_out, s1_out, bo_out, g2_out, s2_out, b2_out, bq_out, bv_out)
+        for d in range(dp):
+
+            @pl.when(place.d == d)
+            def _():
+                for i, out in enumerate(outs):
+                    out[...] = lines[i : i + 1, d * share : (d + 1) * share]
+                for s in range(seq):
+                    row = 8 + seq + s
+                    b1_out[:, s * units : (s + 1) * units] = total_ref[
+                        row : row + 1, d * units : (d + 1) * units
+                    ]
+
+
+def finish(place, w1, w2, wq, wo, totals, layer, grad):
+    dp, seq = place.dp, place.seq
+    share, units, wide = D // dp, w2.shape[1], D // seq
+    tile = 32 if share % 32 == 0 and units == share else share
+    steps = share // tile
+    tall = units // steps
+    mat = lambda *tail: pl.BlockSpec((seq, tile, *tail), lambda i: (0, i, 0))
+    out = lambda cols: pl.BlockSpec((tile, cols), lambda i: (i, 0))
+    small = pl.BlockSpec((1, share), lambda i: (0, 0))
+    f32 = lambda *shape: jax.ShapeDtypeStruct(shape, F32)
+    return pl.pallas_call(
+        functools.partial(finish_kernel, place),
+        grid=(steps,),
+        in_specs=[
+            mat(w1.shape[2]),
+            pl.BlockSpec((seq, tall, D), lambda i: (0, i, 0)),
+            mat(wq.shape[2]),
+            mat(wo.shape[2]),
+            pl.BlockSpec(totals.shape, lambda i: (0, 0)),
+            pl.BlockSpec(layer.shape, lambda i: (0, 0)),
+            pl.BlockSpec(layer.shape, lambda i: (0, 0)),
+        ],
+        out_specs=[pl.BlockSpec(layer.shape, lambda i: (0, 0))] * 2
+        + [out(FF), pl.BlockSpec((seq, tall, D), lambda i: (0, i, 0))]
+        + [out(D)] * 4
+        + [small] * 8
+        + [pl.BlockSpec((1, FF // dp), lambda i: (0, 0))],
+        out_shape=[jax.ShapeDtypeStruct(layer.shape, BF16)] * 2
+        + [f32(share, FF), f32(seq, units, D)]
+        + [f32(share, D)] * 4
+        + [f32(1, share)] * 8
+        + [f32(1, FF // dp)],
+        scratch_shapes=[pltpu.VMEM((8, D), F32)],
+        compiler_params=params(),
+        name="finish",
+    )(w1, w2, wq, wo, totals, layer, grad)
 
 
 def per_device(
@@ -1152,103 +1325,44 @@
     dp = lax.axis_size("dp")
     seq = lax.axis_size("seq")
     me = lax.axis_index("seq")
-    rows_here = hidden_in.shape[1]
-    slots = rows_here * seq
-    share = D // dp
-    head_cols = D // seq
-    heads = HEADS // seq
+    slots = hidden_in.shape[1] * seq
     units = FF // (dp * seq)
     quarter = dp * units
 
-    hidden_own = hidden_in[0]
-    matches = clip_order[0] == jnp.arange(clip_lengths.shape[0], dtype=jnp.int32)
-    length = jnp.sum(jnp.where(matches, clip_lengths, 0)).reshape(1)
-
     spot = Place(dp, seq)
-    mine_dp = lax.axis_index("dp")
-
-    def columns(weight):
-        return lax.dynamic_slice_in_dim(weight, me * head_cols, head_cols, 1)
-
-    width = 3 * head_cols
-    extra = -(-(8 * share + FF // dp) // width)
-    tall = -(-(share + extra) // 16) * 16
-
-    def spread(vector):
-        return lax.dynamic_update_slice_in_dim(jnp.zeros((D,), BF16), vector, mine_dp * share, 0)
-
-    def head_part(vector):
-        part = lax.dynamic_slice_in_dim(spread(vector), me * head_cols, head_cols, 0)
-        return jnp.pad(part, (0, D - head_cols))
-
-    expand_own = lax.dynamic_slice_in_dim(expand_bias, me * units, units, 0)
-    expand_row = lax.dynamic_update_slice_in_dim(
-        jnp.zeros((quarter,), BF16), expand_own, mine_dp * units, 0
+    vectors = jnp.stack(
+        [first_gain, first_shift, output_bias, second_gain, second_shift, reduce_bias, query_bias,
+         value_bias]
+    ).astype(F32)
+    b1 = expand_bias.reshape(seq, units).astype(F32)
+    small, wqkv_share, w1_share = prep(
+        spot, query_weight, key_weight, value_weight, expand_weight, vectors, b1
     )
-    blank = jnp.zeros((D,), BF16)
-    small = jnp.stack(
-        [spread(first_gain), spread(first_shift), spread(output_bias), spread(second_gain),
-         spread(second_shift), spread(reduce_bias), jnp.pad(expand_row, (0, D - quarter)), blank,
-         head_part(query_bias), head_part(value_bias)] + [blank] * 6
+    x, vectors, w_qkv, w_out, w_expand, normed, qt, kt, keys, values, mix, lse = front(
+        spot, clip_lengths, clip_order, hidden_in[0], small, wqkv_share, output_weight, w1_share
     )
-    wqkv_share = jnp.concatenate(
-        [columns(query_weight), columns(key_weight), columns(value_weight)], axis=1
-    )
-    w1_share = jnp.concatenate(
-        [
-            lax.dynamic_slice_in_dim(expand_weight, d * (FF // dp) + me * units, units, 1)
-            for d in range(dp)
-        ],
-        axis=1,
-    )
-    w2_share = lax.dynamic_slice_in_dim(reduce_weight, me * units, units, 0)
-    (
-        x, cot, small, w_qkv, w_out, w_expand, normed, qt, kt, keys, values, mix, lse,
-    ) = front(spot, length, hidden_own, cotangent[0], small, wqkv_share, output_weight, w1_share)
     w_out = w_out.reshape(D, D)
     w_expand = w_expand.reshape(D, quarter)
-    vectors = jnp.sum(small.astype(F32), axis=0)
     mix = mix.reshape(D, slots)
-    grad_branch, middle, grad_middle, out_part, s1, s2, sums = feed(
-        spot, length, x, mix, cot, w_out, w_expand, w2_share, vectors
+    if not whole_tiles(units):
+        reduce_weight = lax.dynamic_slice_in_dim(reduce_weight, me * units, units, 0)
+    grad_branch, middle, grad_middle, out_part, g1, s2, sums = feed(
+        spot, clip_lengths, clip_order, x, mix, cotangent[0], w_out, w_expand, reduce_weight,
+        vectors,
     )
     layer_output, input_grad, totals, w1_grad, w2_grad, qkv_grad, wo_grad = tail(
         spot, vectors, sums, lse, middle, grad_middle, qt, kt, keys, values, grad_branch, mix,
-        w_out, w_qkv, normed, x, out_part, s1, s2,
+        w_out, w_qkv, normed, x, out_part, g1, s2,
     )
-
-    def own(vector):
-        return lax.dynamic_slice_in_dim(vector.reshape(-1), mine_dp * share, share, 0)
-
-    w2_grad = w2_grad.reshape(FF // dp, D).astype(F32)
-    w1_grad = (
-        w1_grad.reshape(seq, share, dp, units).transpose(1, 2, 0, 3).reshape(share, FF).astype(F32)
+    results = finish(
+        spot, w1_grad, w2_grad, qkv_grad, wo_grad, totals, layer_output, input_grad
     )
-    wo_grad = wo_grad.transpose(1, 0, 2).reshape(share, D).astype(F32)
-    qkv_grad = qkv_grad.reshape(seq, share, 3, head_cols).astype(F32)
-    qkv_grad = qkv_grad.transpose(2, 1, 0, 3).reshape(3, share, D)
-    bias = totals[8 : 8 + seq]
-    expand_bias_grad = lax.dynamic_slice_in_dim(
-        totals[8 + seq : 8 + 2 * seq, :quarter].reshape(seq, dp, units), mine_dp, 1, 1
-    ).reshape(FF // dp)
+    layer_output, input_grad, *results = results
+    (w1_grad, w2_grad, wq_grad, wk_grad, wv_grad, wo_grad) = results[:6]
+    g1, s1, bo, g2, s2, b2, bq, bv, b1 = (value.reshape(-1) for value in results[6:])
     return (
-        layer_output[None],
-        input_grad[None],
-        own(totals[0]),
-        own(totals[1]),
-        qkv_grad[0],
-        own(bias[:, :head_cols]),
-        qkv_grad[1],
-        qkv_grad[2],
-        own(bias[:, head_cols : 2 * head_cols]),
-        wo_grad,
-        own(totals[2]),
-        own(totals[3]),
-        own(totals[4]),
-        w1_grad,
-        expand_bias_grad,
-        w2_grad,
-        own(totals[5]),
+        layer_output[None], input_grad[None], g1, s1, wq_grad, bq, wk_grad, wv_grad, bv, wo_grad,
+        bo, g2, s2, w1_grad, b1, w2_grad.reshape(FF // dp, D), b2,
     )
 
 

time: 573 us -> 425 us (0.74)
  Pallas kernels: 490 us -> 410 us
  local copies, waits for them, and re-layouts: 65.1 us -> 6.65 us
    pallas_call x1, Pallas kernels: 182 us -> 137 us  [tail(): pl.pallas_call(functools.partial(tail_kernel, place), in_specs=[inside] *...]
    pallas_call x1, Pallas kernels: 166 us -> 136 us  [feed(): pl.pallas_call(functools.partial(feed_kernel, place), in_specs=[pl.BlockS...]
    convert_element_type x5 -> x1, local copies, waits for them, and re-layouts: 22.6 us -> 1.36 us  [per_device(): b1 = expand_bias.reshape(seq, units).astype(F32)]
    pallas_call x1, Pallas kernels: 141 us -> 125 us  [front(): pl.pallas_call(functools.partial(front_kernel, place), in_specs=[pl.Block...]
    slice x7 -> x0, local copies, waits for them, and re-layouts: 12 us -> none  [the longest x2 7.96 us: per_device(): qkv_grad[2]]
    pallas_call x0 -> x2, Pallas kernels: none -> 11.8 us  [the longest x1 8.88 us: finish(): pl.pallas_call(functools.partial(finish_kernel, place), grid=(steps,), in...]
    dynamic_slice x14 -> x0, local copies, waits for them, and re-layouts: 9.64 us -> none  [the longest x5 3.2 us: own(): lax.dynamic_slice_in_dim(vector.reshape(-1), mine_dp * share, share, 0)]
where the time goes in v4:
time: 425 us; the launch traced here: 420 us
  Pallas kernels  410 us (96%)
  local copies, waits for them, and re-layouts  6.65 us (2%)
    pallas_call x1, Pallas kernels, tail(): pl.pallas_call(functools.partial(tail_kernel, place), in_specs=[inside] *...  137 us
    pallas_call x1, Pallas kernels, feed(): pl.pallas_call(functools.partial(feed_kernel, place), in_specs=[pl.BlockS...  136 us
    pallas_call x1, Pallas kernels, front(): pl.pallas_call(functools.partial(front_kernel, place), in_specs=[pl.Block...  125 us
    pallas_call x1, Pallas kernels, finish(): pl.pallas_call(functools.partial(finish_kernel, place), grid=(steps,), in...  8.88 us

profile of v4, /device:TPU:0, one launch (start us, length us, event | category | flops | bytes accessed | tf_op | source)
XLA Modules:
  0.0 420.2 jit_solution(4724959479839460585)
XLA Ops:
  1.3 0.7 stack.27
  2.0 0.7 stack.28
  2.6 0.7 stack.33
  3.3 0.7 stack.34
  3.9 0.7 stack.29
  4.6 0.7 stack.30
  5.3 0.7 stack.31
  5.9 0.7 stack.32
  6.6 0.6 convert_element_type.8.vec_ref
  7.2 1.4 reshape.89.b1_ref
  8.6 2.9 prep.1
  11.5 125.3 %front.1 = (bf16[4,384,1280]{2,1,0:T(8,128)(2,1)}, f32[16,1280]{1,0:T(8,128)}, bf16[8,160,960]{2,1,0:T(8,128)(2,1)}, bf16[8,160,1280]{2,1,0:T(8,128)(2,1)}, bf16...) custom-call(s32[8]{0:T(128)} %lengths_ref.3, ...), custom_call_target="tpu_custom_call" | custom-call | tf_op jit(solution)/shard_map/front/pallas_call | solution.py:434
  136.8 135.7 %feed.1 = (bf16[4,384,1280]{2,1,0:T(8,128)(2,1)}, f32[384,1280]{1,0:T(8,128)}, f32[384,1280]{1,0:T(8,128)}, bf16[4,384,1280]{2,1,0:T(8,128)(2,1)}, bf16[8,160,12...) custom-call(s32[8]{0:T(128)} %lengths_ref.3, s32[1]{0:T(128)S(6)} %copy.36.order_ref, ...), custom_call_target="tpu_custom_call" | custom-call | tf_op jit(solution)/shard_map/feed/pallas_call | solution.py:785
  272.5 137.1 %tail.1 = (bf16[384,1280]{1,0:T(8,128)(2,1)}, bf16[384,1280]{1,0:T(8,128)(2,1)}, f32[16,1280]{1,0:T(8,128)}, bf16[4,160,1280]{2,1,0:T(8,128)(2,1)}, bf16[4,160,1...) custom-call(f32[16,1280]{1,0:T(8,128)} %get-tuple-element.66.vec_ref, ...), custom_call_target="tpu_custom_call" | custom-call | tf_op jit(solution)/shard_map/tail/pallas_call | solution.py:1135
  409.6 8.9 %finish.1 = (bf16[384,1280]{1,0:T(8,128)(2,1)}, bf16[384,1280]{1,0:T(8,128)(2,1)}, f32[160,5120]{1,0:T(8,128)}, f32[4,160,1280]{2,1,0:T(8,128)}, f32[160,1280]{1...) custom-call(bf16[4,160,1280]{2,1,0:T(8,128)(2,1)} %get-tuple-element, ...), custom_call_target="tpu_custom_call" | custom-call | tf_op jit(solution)/shard_map/finish/pallas_call | solution.py:1292
  418.5 1.3 reduce
  (1 shorter events, 0.0 us)

commit v5 on v4

--- a/solution.py
+++ b/solution.py
@@ -54,6 +54,7 @@
         self.xs = 1 << ((dp.bit_length() - 1) // 2)
         self.zs = dp // self.xs
         self.ys = seq // 2
+        self.z_order = sorted(range(1, self.zs), key=lambda k: min(k, self.zs - k))
 
     def locate(self):
         self.d, self.s = lax.axis_index("dp"), lax.axis_index("seq")
@@ -114,8 +115,11 @@
 
 
 class GatherDp:
-    def __init__(self, place, group, sems, own, slab, on=None):
+    def __init__(self, place, group, sems, own, slab, on=None, ahead=()):
         self.p, self.g, self.own, self.slab, self.on = place, group, own, slab, on
+        self.staged = on is None
+        self.ahead = dict(zip(place.z_order, ahead))
+        self.rest = place.z_order[len(self.ahead) :]
         self.zsend, self.zrecv, self.xsend, self.xrecv = sems
 
     def when(self, block, act):
@@ -130,20 +134,21 @@
 
     def x_copy(self, k, j):
         block = self.p.block(k, 0)
-        src = self.own if k == 0 else self.slab(block)
+        src = self.own if k == 0 else self.ahead.get(k, self.slab(block))
         return send(src, self.slab(block), self.xsend.at[self.g, k, j],
                     self.xrecv.at[self.g, k, j], (self.p.at_x(j), self.p.s))
 
     def start_x(self):
         def act():
-            for j in range(1, self.p.xs):
-                self.x_copy(0, j).start()
+            for k in [0, *self.ahead]:
+                for j in range(1, self.p.xs):
+                    self.x_copy(k, j).start()
 
         self.when(self.p.d, act)
 
     def start_z(self):
         def act():
-            for k in range(self.p.zs - 1, 0, -1):
+            for k in self.rest[:2] if self.staged else self.rest:
                 self.z_copy(k).start()
 
         self.when(self.p.d, act)
@@ -156,11 +161,14 @@
                  self.zrecv.at[self.g, k], (place.at_z(k), place.s)).wait_recv()
             for j in range(1, place.xs):
                 self.x_copy(k, j).start()
+            later = self.rest.index(k) + 2
+            if self.staged and later < len(self.rest):
+                self.z_copy(self.rest[later]).start()
 
         self.when(place.block(k, 0), act)
 
     def forward_all(self):
-        for k in range(1, self.p.zs):
+        for k in self.p.z_order:
             self.forward(k)
 
     def arrive(self):
@@ -175,7 +183,7 @@
         place = self.p
 
         def act():
-            for k in range(1, place.zs):
+            for k in self.rest:
                 self.z_copy(k).wait_send()
 
         self.when(place.d, act)
@@ -232,6 +240,13 @@
 QSCALE = SCALE * LOG2E
 
 
+def own_rows(place, w2):
+    units = FF // (place.dp * place.seq)
+    if whole_tiles(units):
+        return w2.at[pl.ds(pl.multiple_of(place.s * units, 16), units), :]
+    return w2
+
+
 def own_length(lengths_ref, order_ref):
     length = 0
     for clip in range(lengths_ref.shape[0]):
@@ -240,11 +255,11 @@
 
 
 def front_kernel(
-    place, lengths_ref, order_ref, x_in, sm_in, wq_in, wo_in, w1_in,
-    x_out, vec_out, wq_out, wo_out, w1_out, normed_out, qt_out, kt_out, k_out,
+    place, lengths_ref, order_ref, x_in, sm_in, wq_in, wo_in, w1_in, w2_in,
+    x_out, vec_out, wq_out, wo_out, w1_out, w2_out, normed_out, qt_out, kt_out, k_out,
     v_out, mix_out, lse_ref,
-    xs, nr, sm, wq, wt, qt, kt, vt, kn, vn, mix,
-    zsend, zrecv, xsend, xrecv, ssend, srecv, local,
+    xs, nr, nt, biases, sm, wq, wt, qt, kt, vt, kn, vn, mix,
+    zsend, zrecv, xsend, xrecv, ssend, srecv, swap_send, swap_recv, local,
 ):
     place.locate()
     seq, rows = x_out.shape[0], x_out.shape[1]
@@ -264,14 +279,25 @@
     g_sm = over_dp(0, sm_in, sm)
     g_wq = over_dp(1, wq_in, wq)
     g_wo = GatherDp(place, 2, dp_sems, wo_in, lambda d: wo_out.at[d],
-                    lambda d: lax.rem(d, seq) == place.s)
+                    lambda d: lax.rem(d, 2) == place.c)
     g_w1 = over_dp(3, w1_in, w1_out)
     g_x = over_seq(0, x_in, xs)
-    wo_sets = [
-        GatherSeq(place, 1 + heads + i, seq_sems, wo_out.at[i * seq + place.s],
-                  lambda s, i=i: wo_out.at[i * seq + s])
-        for i in range(place.dp // seq)
-    ]
+
+    swaps = [(k, j) for k in range(place.zs) for j in range(place.xs) if (k, j) != (0, 0)]
+
+    def swap(k, j):
+        slab = wo_out.at[place.block(k, j)]
+        return send(slab, slab, swap_send.at[k, j], swap_recv.at[k, j], (place.d, place.partner))
+
+    def swap_start():
+        for k, j in swaps:
+            pl.when(g_wo.on(place.block(k, j)))(swap(k, j).start)
+
+    def swap_finish():
+        for k, j in swaps:
+            pl.when(g_wo.on(place.block(k, j)))(swap(k, j).wait_send)
+            pl.when(~g_wo.on(place.block(k, j)))(swap(k, j).wait_recv)
+
     locals_in = [
         pltpu.make_async_copy(x_in, xs.at[place.s], local.at[0]),
         pltpu.make_async_copy(sm_in, sm.at[place.d], local.at[1]),
@@ -285,10 +311,9 @@
     g_sm.start_z()
     g_x.start()
     g_wq.start_x()
-    for group in (g_wq, g_wo, g_w1):
-        group.start_z()
+    g_wq.start_z()
     w1_own.start()
-    pl.when(g_wo.on(place.d))(wo_own.start)
+    wo_own.start()
 
     column = lax.broadcasted_iota(jnp.int32, (slots, 1), 0)
     penalty = jnp.where(column >= own_length(lengths_ref, order_ref), -1e30, 0.0).astype(BF16)
@@ -302,14 +327,30 @@
 
     for copy in locals_in:
         copy.wait()
-    g_sm.forward_all()
-    g_wq.forward_all()
-    g_wo.start_x()
-    g_w1.start_x()
+    turns = list(place.z_order)
+    g_sm.forward(turns[0])
+    for k in turns[1:2]:
+        g_sm.forward(k)
+    g_wq.forward(turns[0])
+    for k in turns[2:]:
+        g_sm.forward(k)
+    turns.pop(0)
+    if turns:
+        g_wq.forward(turns.pop(0))
     g_sm.arrive()
-    vectors = jnp.sum(sm[...], axis=0)
-    vec_out[...] = vectors
-    gain, shift = vectors[0:1], vectors[1:2]
+    part, units = sm.shape[2], w1_in.shape[1] // place.dp
+    vec_out[...] = jnp.zeros_like(vec_out)
+    for d in range(place.dp):
+        vec_out[0:6, d * part : (d + 1) * part] = sm[d, 0:6, :]
+        vec_out[7:9, d * part : (d + 1) * part] = sm[d, 7:9, :]
+        vec_out[6:7, d * units : (d + 1) * units] = sm[d, 6:7, :units]
+    for s in range(seq):
+
+        @pl.when(place.s == s)
+        def _():
+            biases[0:2] = vec_out[7:9, s * wide : (s + 1) * wide]
+
+    gain, shift = vec_out[0:1], vec_out[1:2]
 
     def norm_block(block):
         unit, _ = normalize(xs[block].astype(F32))
@@ -319,36 +360,53 @@
     norm_block(place.s)
     norm_block(g_x.arrive_core(0))
     for j in range(1, place.ys):
+        if turns:
+            g_wq.forward(turns.pop(0))
         norm_block(g_x.arrive_y(j))
+    for k in turns:
+        g_wq.forward(k)
+    g_wo.start_z()
+    for j in range(1, place.ys):
         norm_block(g_x.arrive_core(j))
+    chunk = chunk_of(slots)
+
+    def turn_block(block, _):
+        spot = pl.ds(pl.multiple_of(block * chunk, 128), chunk)
+        nt[:, spot] = jnp.transpose(nr[spot, :])
+        return 0
+
+    lax.fori_loop(0, slots // chunk, turn_block, 0)
     g_wq.arrive()
+    g_wo.start_x()
     share = wq.shape[1]
     wt[...] = jnp.transpose(wq[...].reshape(place.dp * share, 3 * wide))
-    bias = jnp.transpose(vectors[8:16])
-
-    chunk = chunk_of(slots)
+    bias = jnp.transpose(biases[...])
+    g_wo.forward_all()
+    g_w1.start_z()
+    g_w1.start_x()
 
     def project_block(block, _):
         cols = pl.ds(pl.multiple_of(block * chunk, 128), chunk)
-        lines = pl.ds(pl.multiple_of(block * chunk, 128), chunk)
-        tokens = dot(wt[...], nr[lines, :], ((1,), (1,)))
-        query = (tokens[:wide] + bias[:wide, 0:1]).astype(BF16)
-        key = tokens[wide : 2 * wide].astype(BF16)
-        value = (tokens[2 * wide :] + bias[:wide, 1:2]).astype(BF16)
+        tokens = dot(wt[...], nt[:, cols])
         for head in range(heads):
+            first = 3 * head * HEAD_DIM
             part = slice(head * HEAD_DIM, (head + 1) * HEAD_DIM)
-            qt[head, :HEAD_DIM, cols] = query[part]
-            kt[head, :, cols] = key[part]
-            vt[head, :, cols] = value[part]
-            kn[head, lines, :HEAD_DIM] = jnp.transpose(key[part])
-            vn[head, lines, :] = jnp.transpose(value[part])
+            query = tokens[first : first + HEAD_DIM] + bias[part, 0:1]
+            key = tokens[first + HEAD_DIM : first + 2 * HEAD_DIM].astype(BF16)
+            value = tokens[first + 2 * HEAD_DIM : first + 3 * HEAD_DIM] + bias[part, 1:2]
+            value = value.astype(BF16)
+            qt[head, :HEAD_DIM, cols] = query.astype(BF16)
+            kt[head, :, cols] = key
+            vt[head, :, cols] = value
+            kn[head, cols, :HEAD_DIM] = jnp.transpose(key)
+            vn[head, cols, :] = jnp.transpose(value)
         return 0
 
     lax.fori_loop(0, slots // chunk, project_block, 0)
     results = [
         pltpu.make_async_copy(src, dst, local.at[7 + i])
         for i, (src, dst) in enumerate(
-            [(xs, x_out), (wq, wq_out), (nr, normed_out), (qt, qt_out), (kt, kt_out),
+            [(xs, x_out), (wq, wq_out), (nt, normed_out), (qt, qt_out), (kt, kt_out),
              (kn, k_out), (vn, v_out)]
         )
     ]
@@ -356,14 +414,15 @@
         copy.start()
 
     block = 256
-    g_wo.forward_all()
-    g_wo.arrive()
-    pl.when(g_wo.on(place.d))(wo_own.wait)
-    for group in wo_sets:
-        group.start()
 
     def attend(head):
         def one(i, _):
+            if head == min(1, heads - 1):
+
+                @pl.when(i == slots // block // 2)
+                def _():
+                    g_w1.forward(place.z_order[0])
+
             cols = pl.ds(pl.multiple_of(i * block, 128), block)
             scores = dot(kn[head], qt[head, :, cols])
             top = jnp.max(scores, axis=0, keepdims=True)
@@ -384,14 +443,19 @@
     for head in range(heads):
         attend(head)
         g_mix[head].start()
-        if head == 0:
-            g_w1.forward(1)
         if head == min(1, heads - 1):
-            for group in wo_sets:
-                for j in range(1, place.ys):
-                    group.arrive_y(j)
-            for k in range(2, place.zs):
-                g_w1.forward(k)
+            g_wo.arrive()
+            swap_start()
+            g_w1.forward(place.z_order[1])
+    for k in place.z_order[2:]:
+        g_w1.forward(k)
+    w2_own = own_rows(place, w2_in)
+    w2_ahead = [
+        send(w2_own, w2_out.at[i], zsend.at[4, k], zrecv.at[4, k], (place.at_z(k), place.s))
+        for i, k in enumerate(place.z_order[:2])
+    ]
+    for copy in w2_ahead:
+        copy.start()
     for head in range(heads):
         for j in range(1, place.ys):
             g_mix[head].arrive_y(j)
@@ -400,17 +464,15 @@
             g_mix[head].arrive_core(j)
     mix_copy = pltpu.make_async_copy(mix, mix_out, local.at[15])
     mix_copy.start()
-    for group in wo_sets:
-        for j in range(place.ys):
-            group.arrive_core(j)
     g_w1.arrive()
-    for group in (g_sm, g_wq, g_wo, g_w1, g_x, *wo_sets, *g_mix):
+    swap_finish()
+    for group in (g_sm, g_wq, g_wo, g_w1, g_x, *g_mix):
         group.drain()
-    for copy in (w1_own, *results, mix_copy):
+    for copy in (*w2_ahead, w1_own, wo_own, *results, mix_copy):
         copy.wait()
 
 
-def front(place, lengths, order, x, small, wqkv, wo, w1):
+def front(place, lengths, order, x, small, wqkv, wo, w1, w2):
     dp, seq = place.dp, place.seq
     rows = x.shape[0]
     slots = rows * seq
@@ -419,11 +481,12 @@
     anyspace = pl.BlockSpec(memory_space=pl.ANY)
     shapes = [
         (seq, rows, D),
-        small.shape,
+        (16, D),
         (dp, share, width),
         (dp, *wo.shape),
         (dp, *w1.shape),
-        (slots, D),
+        (len(place.z_order[:2]), FF // (dp * seq), D),
+        (D, slots),
         (heads, 128, slots),
         (heads, HEAD_DIM, slots),
         (heads, slots, 128),
@@ -433,7 +496,7 @@
     vm = lambda *shape: pltpu.VMEM(shape, BF16)
     return pl.pallas_call(
         functools.partial(front_kernel, place),
-        in_specs=[pl.BlockSpec(memory_space=pltpu.SMEM)] * 2 + [anyspace] * 5,
+        in_specs=[pl.BlockSpec(memory_space=pltpu.SMEM)] * 2 + [anyspace] * 6,
         out_specs=[anyspace, pl.BlockSpec(memory_space=pltpu.VMEM)]
         + [anyspace] * (len(shapes) - 2)
         + [pl.BlockSpec(memory_space=pltpu.VMEM)],
@@ -444,6 +507,8 @@
         scratch_shapes=[
             vm(seq, rows, D),
             vm(slots, D),
+            vm(D, slots),
+            pltpu.VMEM((8, heads * HEAD_DIM), F32),
             pltpu.VMEM((dp, *small.shape), F32),
             vm(dp, share, width),
             vm(width, D),
@@ -454,12 +519,13 @@
             vm(heads, slots, HEAD_DIM),
             vm(seq, heads, HEAD_DIM, slots),
         ]
-        + dp_semaphores(place, 4)
-        + seq_semaphores(place, 1 + heads + dp // seq)
+        + dp_semaphores(place, 5)
+        + seq_semaphores(place, 1 + heads)
+        + [pltpu.SemaphoreType.DMA((place.zs, place.xs))] * 2
         + [pltpu.SemaphoreType.DMA((16,))],
         compiler_params=params(collective_id=0, has_side_effects=True),
         name="front",
-    )(lengths, order, x, small, wqkv, wo, w1)
+    )(lengths, order, x, small, wqkv, wo, w1, w2)
 
 
 class ScatterSeq:
@@ -484,19 +550,19 @@
         self.p, self.g, self.out, self.part = place, group, out, part
         self.from_x, self.from_z = from_x, from_z
         self.zsend, self.zrecv, self.xsend, self.xrecv = sems
-        self.order = list(range(1, place.zs)) + [0]
+        self.order = place.z_order + [0]
 
     def block(self, k, j):
         place = self.p
         return lax.rem(place.z + k, place.zs) * place.xs + lax.rem(place.x + j, place.xs)
 
     def x_copy(self, j, k):
-        return send(self.out(self.block(k, j)), self.from_x(j - 1, k),
+        return send(self.out(k, j, self.block(k, j)), self.from_x(j - 1, k),
                     self.xsend.at[self.g, k, j], self.xrecv.at[self.g, k, j],
                     (self.p.at_x(j), self.p.s))
 
-    def start_x(self):
-        for k in self.order:
+    def start_x(self, steps=None):
+        for k in self.order if steps is None else steps:
             for j in range(1, self.p.xs):
                 self.x_copy(j, k).start()
 
@@ -504,13 +570,16 @@
         return send(self.part(k, self.block(k, 0)), self.from_z(k - 1),
                     self.zsend.at[self.g, k], self.zrecv.at[self.g, k], (self.p.at_z(k), self.p.s))
 
-    def fold(self, k):
+    def fold_x(self, k):
         own = self.part(k, self.block(k, 0))
         value = own[...].astype(F32)
         for j in range(1, self.p.xs):
             self.x_copy(j, k).wait_recv()
             value = value + self.from_x(j - 1, k)[...].astype(F32)
-        own[...] = value.astype(BF16)
+        own[...] = value.astype(own.dtype)
+
+    def fold(self, k):
+        self.fold_x(k)
         if k:
             self.z_copy(k).start()
 
@@ -523,14 +592,25 @@
         for k in range(1, self.p.zs):
             self.z_copy(k).wait_recv()
             value = value + self.from_z(k - 1)[...].astype(F32)
-        return value.astype(BF16)
-
-    def drain(self):
-        for k in self.order:
+        return value.astype(self.part(0, self.block(0, 0)).dtype)
+
+    def drain_x(self, steps=None):
+        for k in self.order if steps is None else steps:
             for j in range(1, self.p.xs):
                 self.x_copy(j, k).wait_send()
-            if k:
-                self.z_copy(k).wait_send()
+
+    def drain_z(self):
+        for k in self.p.z_order:
+            self.z_copy(k).wait_send()
+
+    def drain(self):
+        self.drain_x()
+        self.drain_z()
+
+
+def split_steps(place):
+    order = place.z_order + [0]
+    return order[: place.zs // 2], order[place.zs // 2 :]
 
 
 def whole_tiles(*heights):
@@ -538,10 +618,10 @@
 
 
 def feed_kernel(
-    place, lengths_ref, order_ref, x_in, mix_in, cot_in, wo_in, w1_in, w2_in, vec_ref,
+    place, lengths_ref, order_ref, x_in, mix_in, cot_in, wo_in, w1_in, w2_in, ahead_in, vec_ref,
     gb_out, middle_out, grad_out, part_out, g1_out, s2_ref, sums_ref,
     xa, mixv, gv, wo, w1, w2, second, act, slope, unit, ds, own, from_core, from_y,
-    from_x2, from_z2, *rest,
+    from_x1, from_x2, from_z2, *rest,
 ):
     zsend, zrecv, xsend, xrecv, ssend, srecv, local = rest[-7:]
     gb = xa
@@ -565,9 +645,9 @@
         w2_split, g2_split, g1_split = rest[:3]
         w2_part, g2_part = (lambda d: w2_split.at[d]), (lambda d: g2_split.at[d])
         g1_part = lambda d: g1_split.at[d]
-    if aligned:
-        w2_in = w2_in.at[pl.ds(pl.multiple_of(place.s * units, 16), units), :]
-    gather = GatherDp(place, 0, dp_sems, w2_in, w2_part)
+    w2_in = own_rows(place, w2_in)
+    ahead = [ahead_in.at[i] for i in range(len(place.z_order[:2]))]
+    gather = GatherDp(place, 0, dp_sems, w2_in, w2_part, ahead=ahead)
     cots = GatherSeq(place, 2, seq_sems, cot_in, lambda s: gv.at[s])
     gather.start_x()
     gather.start_z()
@@ -578,7 +658,11 @@
     ]
     w2_own = pltpu.make_async_copy(w2_in, w2_part(place.d), local.at[5])
     cot_own = pltpu.make_async_copy(cot_in, gv.at[place.s], local.at[6])
-    for copy in (*loads, w2_own, cot_own):
+    w2_ready = [
+        pltpu.make_async_copy(src, w2_part(gather.p.block(k, 0)), local.at[7 + i])
+        for i, (k, src) in enumerate(gather.ahead.items())
+    ]
+    for copy in (*loads, w2_own, cot_own, *w2_ready):
         copy.start()
     gain, shift, bias_out, bias1 = vec_ref[3:4], vec_ref[4:5], vec_ref[2:3], vec_ref[6:7, :width]
     own_chunk = place.s // joined
@@ -608,6 +692,11 @@
         act[lines, :] = (expanded * phi).astype(BF16)
         density = jnp.exp(-0.5 * expanded * expanded) * 0.3989422804014327
         slope[lines, :] = (phi + expanded * density).astype(BF16)
+        @pl.when(i == slots // chunk - 1)
+        def _():
+            for k in gather.rest[:1]:
+                gather.forward(k)
+
         return 0
 
     lax.fori_loop(0, slots // chunk, forward, 0)
@@ -629,7 +718,6 @@
         return 0
 
     lax.fori_loop(0, slots // chunk, mask, 0)
-    gather.forward(1)
 
     step = 256 if width % 256 == 0 else 128
 
@@ -640,15 +728,16 @@
         return 0
 
     lax.fori_loop(0, width // step, w2_grad, 0)
-    for k in range(2, place.zs):
+    for k in gather.rest[1:]:
         gather.forward(k)
     if not aligned:
         for d in range(place.dp):
             g2_split[d] = wo[d * units : (d + 1) * units, :]
-    r2 = ScatterDp(place, 1, dp_sems, g2_part, lambda k, d: g2_part(d),
+    r2 = ScatterDp(place, 1, dp_sems, lambda k, j, d: g2_part(d), lambda k, d: g2_part(d),
                    lambda j, k: from_x2.at[j, k], lambda k: from_z2.at[k])
     r2.start_x()
-    w2_own.wait()
+    for copy in (w2_own, *w2_ready):
+        copy.wait()
     gather.arrive()
     if not aligned:
         for d in range(place.dp):
@@ -674,54 +763,51 @@
         ds[block] = (ds[block].astype(F32) + from_core[j].astype(F32)).astype(BF16)
         scatter.y_copy(j, ds.at[block]).start()
 
+    turns = list(r2.order[:-1])
     for j in list(range(1, place.ys)) + [0]:
         if joined == 1:
             backward(place.at_y(j, 1 - place.c))
             scatter.core_copy(j).start()
+            if turns and j != 1:
+                r2.fold(turns.pop(0))
             backward(place.at_y(j, place.c))
         else:
             backward(lax.rem(place.y + j, place.ys))
             scatter.core_copy(j).start()
         if j:
             fold_y(j)
+            if turns:
+                r2.fold(turns.pop(0))
 
     gather.drain()
-
-    def emit(i, _):
-        lines = lines_of(i, chunk)
-        unit[lines, :] = dot(act[lines, :], w2[...]).astype(BF16)
-        return 0
-
-    lax.fori_loop(0, slots // chunk, emit, 0)
-    keep_parts = [
-        pltpu.make_async_copy(
-            unit.at[pl.ds(i * rows, rows), :], part_out.at[i], local.at[9 + i]
-        )
-        for i in range(seq)
-    ]
-    for copy in keep_parts:
-        copy.start()
-
-    r2.fold(r2.order[0])
 
     def w1_grad(i, _):
         cols = pl.ds(pl.multiple_of(i * 256, 128), 256)
         value = dot(second[:, cols], slope[...], ((0,), (0,)))
-        w1[pl.ds(pl.multiple_of(i * 256, 128), 256), :] = value.astype(BF16)
+        keep1[pl.ds(pl.multiple_of(i * 256, 128), 256), :] = value.astype(BF16)
         return 0
 
+    keep1 = w1
     lax.fori_loop(0, D // 256, w1_grad, 0)
     if not aligned:
         for d in range(place.dp):
             g1_split[d] = w1[d * share : (d + 1) * share, :]
+    r1 = ScatterDp(place, 2, dp_sems, lambda k, j, d: g1_part(d), lambda k, d: g1_part(d),
+                   lambda j, k: from_x1.at[j, k], None)
+    early, late = split_steps(place)
+    r1.start_x(early)
     keep = [
-        pltpu.make_async_copy(g1_part(d), g1_out.at[d], local.at[9 + seq + d])
-        for d in range(place.dp)
+        pltpu.make_async_copy(
+            g1_part(r1.block(k, j)), g1_out.at[k, j], local.at[9 + seq + k * place.xs + j]
+        )
+        for k in late
+        for j in range(place.xs)
     ]
     for copy in keep:
         copy.start()
-    for k in r2.order[1:-1]:
+    for k in turns:
         r2.fold(k)
+
     scatter.core_copy(0).wait_recv()
     value = ds[place.s].astype(F32) + from_core[0].astype(F32)
     for j in range(1, place.ys):
@@ -741,7 +827,29 @@
     middle_out[...] = middle
     grad_out[...] = grad_middle
 
+    def emit(i, _):
+        lines = lines_of(i, chunk)
+        unit[lines, :] = dot(act[lines, :], w2[...]).astype(BF16)
+        return 0
+
+    lax.fori_loop(0, slots // chunk, emit, 0)
+    keep_parts = [
+        pltpu.make_async_copy(
+            unit.at[pl.ds(i * rows, rows), :], part_out.at[i], local.at[9 + i]
+        )
+        for i in range(seq)
+    ]
+    for copy in keep_parts:
+        copy.start()
     r2.fold(0)
+    for k in early:
+        r1.fold_x(k)
+        keep.append(
+            pltpu.make_async_copy(
+                g1_part(r1.block(k, 0)), g1_out.at[k, 0], local.at[9 + seq + k * place.xs]
+            )
+        )
+        keep[-1].start()
     for j in range(1, place.ys):
         spread_out.arrive_y(j)
     s2_ref[...] = r2.finish()
@@ -755,11 +863,12 @@
         scatter.y_copy(j, ds.at[place.s]).wait_send()
     spread_out.drain()
     r2.drain()
+    r1.drain_x(early)
     for copy in (*keep_parts, *keep, save):
         copy.wait()
 
 
-def feed(place, lengths, order, x, mix, cot, wo, w1, w2, vectors):
+def feed(place, lengths, order, x, mix, cot, wo, w1, w2, ahead, vectors):
     seq, rows, _ = x.shape
     slots = seq * rows
     chunk = chunk_of(slots)
@@ -778,13 +887,13 @@
         ((rows, D), F32, inside),
         ((rows, D), F32, inside),
         ((seq, rows, D), BF16, anyspace),
-        ((place.dp, share, width), BF16, anyspace),
+        ((place.zs, place.xs, share, width), BF16, anyspace),
         ((units, D), BF16, inside),
         ((8, D), F32, inside),
     ]
     return pl.pallas_call(
         functools.partial(feed_kernel, place),
-        in_specs=[pl.BlockSpec(memory_space=pltpu.SMEM)] * 2 + [anyspace] * 6 + [inside],
+        in_specs=[pl.BlockSpec(memory_space=pltpu.SMEM)] * 2 + [anyspace] * 7 + [inside],
         out_specs=[spec for _, _, spec in outs],
         out_shape=[jax.ShapeDtypeStruct(shape, kind) for shape, kind, _ in outs],
         scratch_shapes=[
@@ -802,56 +911,17 @@
             pltpu.VMEM((chunk, D), F32),
             vm(place.ys, rows, D),
             vm(max(place.ys - 1, 1), rows, D),
+            vm(max(place.xs - 1, 1), place.zs, share, width),
             vm(max(place.xs - 1, 1), place.zs, units, D),
             vm(place.zs - 1, units, D),
         ]
         + split
-        + dp_semaphores(place, 2)
+        + dp_semaphores(place, 3)
         + seq_semaphores(place, 3)
         + [pltpu.SemaphoreType.DMA((9 + seq + place.dp,))],
         compiler_params=params(collective_id=1, has_side_effects=True),
         name="feed",
-    )(lengths, order, x, mix, cot, wo, w1, w2, vectors)
-
-
-class SumSmall:
-    def __init__(self, place, values, landing, sems):
-        self.p, self.values, self.landing = place, values, landing
-        self.sends, self.recvs = sems
-        self.hops = [
-            [((place.d, place.partner))],
-            [(place.d, place.at_y(j, place.c)) for j in range(1, place.ys)],
-            [(place.at_x(j), place.s) for j in range(1, place.xs)],
-            [(place.at_z(k), place.s) for k in range(1, place.zs)],
-        ]
-
-    def copies(self, hop):
-        first = sum(len(peers) for peers in self.hops[:hop])
-        return [
-            (first + i, send(self.values.at[hop], self.landing.at[first + i],
-                             self.sends.at[first + i], self.recvs.at[first + i], peer))
-            for i, peer in enumerate(self.hops[hop])
-        ]
-
-    def start(self, hop):
-        for _, copy in self.copies(hop):
-            copy.start()
-
-    def fold(self, hop):
-        value = self.values[hop]
-        for i, copy in self.copies(hop):
-            copy.wait_recv()
-            value = value + self.landing[i]
-        return value
-
-    def drain(self):
-        for hop in range(4):
-            for _, copy in self.copies(hop):
-                copy.wait_send()
-
-
-def small_hops(place):
-    return 1 + (place.ys - 1) + (place.xs - 1) + (place.zs - 1)
+    )(lengths, order, x, mix, cot, wo, w1, w2, ahead, vectors)
 
 
 def tail_kernel(
@@ -859,10 +929,10 @@
     qt_in, kt_in, k_in, v_in, gb_in, mix_in, wo_in, wq_in, normed_in, x_in, part_in, g1_in, s2_in,
     layer_ref, input_ref, total_ref, w1_out, w2_out, wq_out, wo_out,
     qt, kt, kn, vn, got, gbv, mixv, normed, wq, dqkv, wo_rows, gbs, dk_sum, dv_sum, xbuf, outp,
-    core_a, y_a, core_b, y_b, pq, po, p1, xq, xo, x1, zq, zo, z1, r1, rq, ro,
-    values, landing, *rest,
+    core_a, y_a, core_b, y_b, pq, ours, po, p1, x1, xq, xo, zq, zo, z1, r1, r2, rq, ro,
+    line, ps, xsm, zsm, hop, far, *rest,
 ):
-    zsend, zrecv, xsend, xrecv, ssend, srecv, vsend, vrecv, local = rest[-9:]
+    zsend, zrecv, xsend, xrecv, ssend, srecv, local = rest[-7:]
     place.locate()
     seq, rows, _ = x_in.shape
     slots = seq * rows
@@ -872,34 +942,49 @@
     heads = kt.shape[0]
     wide = heads * HEAD_DIM
     share = D // place.dp
+    units = s2_in.shape[0]
     place.barrier()
     dp_sems, seq_sems = (zsend, zrecv, xsend, xrecv), (ssend, srecv)
     e1 = gbv
+    triple = 3 * HEAD_DIM
+    groups = pq.shape[0]
+    each = heads // groups
     if whole_tiles(share):
-        q_part = lambda d: pq.at[pl.ds(pl.multiple_of(d * share, 16), share), :]
+        q_part = lambda h, d: pq.at[h, pl.ds(pl.multiple_of(d * share, 16), share), :]
         o_part = lambda d: po.at[pl.ds(pl.multiple_of(d * share, 16), share), :]
     else:
         pq_split, po_split = rest[:2]
-        q_part, o_part = (lambda d: pq_split.at[d]), (lambda d: po_split.at[d])
-    g1 = ScatterDp(place, 0, dp_sems, lambda d: g1_in.at[d], lambda k, d: p1.at[k],
-                   lambda j, k: x1.at[j, k], lambda k: z1.at[k])
-    gq = ScatterDp(place, 1, dp_sems, q_part, lambda k, d: q_part(d),
-                   lambda j, k: xq.at[j, k], lambda k: zq.at[k])
-    go = ScatterDp(place, 2, dp_sems, o_part, lambda k, d: o_part(d),
+        q_part, o_part = (lambda h, d: pq_split.at[h, d]), (lambda d: po_split.at[d])
+    early, late = split_steps(place)
+    g1 = ScatterDp(place, 0, dp_sems, lambda k, j, d: g1_in.at[k, j],
+                   lambda k, d: p1.at[late.index(k)] if k in late else g1_in.at[k, 0],
+                   lambda j, k: x1.at[j, late.index(k)], lambda k: z1.at[k])
+    go = ScatterDp(place, 1, dp_sems, lambda k, j, d: o_part(d), lambda k, d: o_part(d),
                    lambda j, k: xo.at[j, k], lambda k: zo.at[k])
+    small = ScatterDp(place, 2, dp_sems, lambda k, j, d: ps.at[d], lambda k, d: ps.at[d],
+                      lambda j, k: xsm.at[j, k], lambda k: zsm.at[k])
+    gq = [
+        ScatterDp(place, 3 + h, dp_sems, lambda k, j, d, h=h: q_part(h, d),
+                  lambda k, d, h=h: q_part(h, d), lambda j, k, h=h: xq.at[h, j, k],
+                  lambda k, h=h: zq.at[h, k])
+        for h in range(groups)
+    ]
     out_sum = ScatterSeq(place, 0, seq_sems, lambda s: part_in.at[s], lambda j: core_a.at[j],
                          lambda j: y_a.at[j - 1])
     e1_sum = ScatterSeq(place, 1, seq_sems, lambda s: e1.at[s], lambda j: core_b.at[j],
                         lambda j: y_b.at[j - 1])
-    final2 = GatherSeq(place, 2, seq_sems, s2_in, lambda s: w2_out.at[s])
+    final2 = GatherSeq(place, 2, seq_sems, r2, lambda s: w2_out.at[s])
     final1 = GatherSeq(place, 3, seq_sems, r1, lambda s: w1_out.at[s])
     final_o = GatherSeq(place, 4, seq_sems, ro, lambda s: wo_out.at[s])
-    final_q = GatherSeq(place, 5, seq_sems, rq, lambda s: wq_out.at[s])
+    final_q = [
+        GatherSeq(place, 7 + h, seq_sems, rq.at[h], lambda s, h=h: wq_out.at[s, h])
+        for h in range(groups)
+    ]
 
     first = [(gb_in, gbv), (wo_in.at[pl.ds(pl.multiple_of(place.s * wide, 16), wide), :], wo_rows),
              (mix_in, mixv), (qt_in, qt), (kt_in, kt), (k_in, kn), (v_in, vn)]
     later = [(normed_in, normed), (wq_in, wq)]
-    later += [(g1_in.at[g1.block(k, 0)], p1.at[k]) for k in range(place.zs)]
+    later += [(s2_in, r2)] + [(g1_in.at[k, 0], p1.at[i]) for i, k in enumerate(late)]
     later += [(part_in.at[place.at_y(j, place.c)], outp.at[j]) for j in range(place.ys)]
     loads = [
         pltpu.make_async_copy(src, dst, local.at[i]) for i, (src, dst) in enumerate(first + later)
@@ -907,10 +992,12 @@
     free = len(loads)
     for copy in loads:
         copy.start()
-    g1.start_x()
+    for k in early:
+        g1.z_copy(k).start()
+    g1.start_x(late)
     for j in list(range(1, place.ys)) + [0]:
         out_sum.core_copy(j).start()
-    for copy in loads[: len(first)]:
+    for copy in loads[:2]:
         copy.wait()
 
     def lines_of(index, size, step=16):
@@ -929,6 +1016,7 @@
         return 0
 
     lax.fori_loop(0, count, turn, 0)
+    loads[2].wait()
 
     def wo_grad(i, _):
         lines = pl.ds(pl.multiple_of(i * 256, 128), 256)
@@ -945,6 +1033,7 @@
 
     def head_back(head):
         part = slice(head * HEAD_DIM, (head + 1) * HEAD_DIM)
+        first = head * triple
         dk_sum[...] = jnp.zeros_like(dk_sum)
         dv_sum[...] = jnp.zeros_like(dv_sum)
 
@@ -959,16 +1048,27 @@
             dv_sum[...] += dot(probs.astype(BF16), grad, ((1,), (1,)))
             dk_sum[...] += dot(grad_scores, qt[head, :HEAD_DIM, cols], ((1,), (1,)))
             turned = dot(kt[head], grad_scores) * SCALE
-            dqkv[pl.ds(pl.multiple_of(i * block, 128), block), part] = jnp.transpose(turned).astype(BF16)
+            lines = pl.ds(pl.multiple_of(i * block, 128), block)
+            dqkv[lines, first : first + HEAD_DIM] = jnp.transpose(turned).astype(BF16)
             return 0
 
         lax.fori_loop(0, slots // block, one, 0)
-        dqkv[:, wide + head * HEAD_DIM : wide + (head + 1) * HEAD_DIM] = (
-            dk_sum[...] * SCALE
-        ).astype(BF16)
-        dqkv[:, 2 * wide + head * HEAD_DIM : 2 * wide + (head + 1) * HEAD_DIM] = dv_sum[...].astype(
-            BF16
-        )
+        dqkv[:, first + HEAD_DIM : first + 2 * HEAD_DIM] = (dk_sum[...] * SCALE).astype(BF16)
+        dqkv[:, first + 2 * HEAD_DIM : first + triple] = dv_sum[...].astype(BF16)
+
+    def q_grads(group):
+        ours[...] = dqkv[:, group * each * triple : (group + 1) * each * triple]
+
+        def q_grad(i, _):
+            lines = pl.ds(pl.multiple_of(i * 256, 128), 256)
+            pq[group, lines, :] = dot(normed[lines, :], ours[...]).astype(BF16)
+            return 0
+
+        lax.fori_loop(0, D // 256, q_grad, 0)
+        if not whole_tiles(share):
+            for d in range(place.dp):
+                pq_split[group, d] = pq[group, d * share : (d + 1) * share, :]
+        gq[group].start_x()
 
     def out_fold():
         for j in range(1, place.ys):
@@ -980,39 +1080,38 @@
         result[...] = group.finish()
         final.start()
 
+    for copy in loads[3:]:
+        copy.wait()
+    out_fold()
+    final2.start()
     for head in range(heads):
         head_back(head)
         if head == 0:
-            for copy in loads[len(first) :]:
-                copy.wait()
-            out_fold()
-            final2.start()
-            g1.fold(g1.order[0])
+            for k in late:
+                g1.fold(k)
         if head == min(1, heads - 1):
-            for k in g1.order[1:-1]:
-                g1.fold(k)
+            go.fold_all()
+        if (head + 1) % each == 0:
+            q_grads(head // each)
+        if head == min(2, heads - 1):
+            publish(g1, r1, final1)
         if head == heads - 1:
-            g1.fold(0)
-            go.fold_all()
-
-    def q_grad(i, _):
-        cols = pl.ds(pl.multiple_of(i * 256, 128), 256)
-        pq[cols, :] = dot(normed[:, cols], dqkv[...], ((0,), (0,))).astype(BF16)
-        return 0
-
-    lax.fori_loop(0, D // 256, q_grad, 0)
-    if not whole_tiles(share):
-        for d in range(place.dp):
-            pq_split[d] = pq[d * share : (d + 1) * share, :]
-    gq.start_x()
-    total = sums_ref[...]
+            for group in range(groups - 1):
+                gq[group].fold_all()
+            publish(go, ro, final_o)
+
+    line[...] = jnp.zeros_like(line)
+    line[0:6] = sums_ref[0:6]
     bias_sum = jnp.sum(dqkv[...].astype(F32), axis=0, keepdims=True)
-    values[0] = jnp.zeros_like(values[0])
-    values[0, 0:8] = total
-    values[0, pl.ds(8 + place.s, 1), :wide] = bias_sum[:, :wide]
-    values[0, pl.ds(8 + place.s, 1), wide : 2 * wide] = bias_sum[:, 2 * wide :]
-    values[0, pl.ds(8 + seq + place.s, 1), :] = total[7:8]
-    values[0, 7:8] = jnp.zeros((1, D), F32)
+    for s in range(seq):
+
+        @pl.when(place.s == s)
+        def _():
+            for head in range(heads):
+                to = slice(s * wide + head * HEAD_DIM, s * wide + (head + 1) * HEAD_DIM)
+                at = head * triple
+                line[6:7, to] = bias_sum[:, at : at + HEAD_DIM]
+                line[7:8, to] = bias_sum[:, at + 2 * HEAD_DIM : at + triple]
 
     order = []
     for j in list(range(1, place.ys)) + [0]:
@@ -1034,8 +1133,8 @@
         x_load(at, slot).wait()
         grad = dot(dqkv[lines_of(at, chunk), :], wq[...].reshape(D, 3 * wide), ((1,), (1,)))
         normal, spread = normalize(xbuf[slot].reshape(chunk, D).astype(F32))
-        values[0, 0:1] += jnp.sum(grad * normal, axis=0, keepdims=True)
-        values[0, 1:2] += jnp.sum(grad, axis=0, keepdims=True)
+        line[0:1] += jnp.sum(grad * normal, axis=0, keepdims=True)
+        line[1:2] += jnp.sum(grad, axis=0, keepdims=True)
         e1[pl.ds(at * joined, joined)] = grad.astype(BF16).reshape(joined, rows, D)
         if joined == 2 or not both:
             e1_sum.core_copy(j).start()
@@ -1044,18 +1143,15 @@
             e1_sum.core_copy(j).wait_recv()
             e1[target] = (e1[target].astype(F32) + core_b[j].astype(F32)).astype(BF16)
             e1_sum.y_copy(j, e1.at[target]).start()
-    small = SumSmall(place, values, landing, (vsend, vrecv))
-    small.start(0)
-    gq.fold_all()
-    publish(g1, r1, final1)
-    publish(go, ro, final_o)
-    for hop in range(3):
-        values[hop + 1] = small.fold(hop)
-        small.start(hop + 1)
-    for final in (final2, final1, final_o):
-        for j in range(1, place.ys):
-            final.arrive_y(j)
-
+    for d in range(place.dp):
+        ps[d] = jnp.zeros_like(ps[d])
+        ps[d, 0:8] = line[:, d * share : (d + 1) * share]
+        ps[d, pl.ds(8 + place.s, 1), :units] = sums_ref[7:8, d * units : (d + 1) * units]
+    small.start_x()
+    small.fold_all()
+    gq[groups - 1].fold_all()
+    for group in range(groups - 1):
+        publish(gq[group], rq.at[group], final_q[group])
     value = outp[0].astype(F32)
     out_sum.core_copy(0).wait_recv()
     value = value + core_a[0].astype(F32)
@@ -1063,6 +1159,31 @@
         out_sum.y_copy(j, outp.at[j]).wait_recv()
         value = value + y_a[j - 1].astype(F32)
     layer_ref[...] = (middle_ref[...] + (value + vec_ref[5:6])).astype(BF16)
+
+    hop[0] = small.finish()
+    near = send(hop.at[0], far.at[0], ssend.at[5, 1, 0], srecv.at[5, 1, 0],
+                (place.d, place.partner))
+    near.start()
+    for final in (final2, final1, final_o):
+        for j in range(1, place.ys):
+            final.arrive_y(j)
+    near.wait_recv()
+    hop[1] = hop[0] + far[0]
+    across = [
+        send(hop.at[1], far.at[j], ssend.at[5, 0, j], srecv.at[5, 0, j],
+             (place.d, place.at_y(j, place.c)))
+        for j in range(1, place.ys)
+    ]
+    for copy in across:
+        copy.start()
+    keep = [
+        pltpu.make_async_copy(src, dst.at[place.s], local.at[free + 2 + i])
+        for i, (src, dst) in enumerate([(r1, w1_out), (r2, w2_out), (ro, wo_out), (rq, wq_out)])
+    ]
+    for copy in keep[:3]:
+        copy.start()
+    publish(gq[groups - 1], rq.at[groups - 1], final_q[groups - 1])
+    keep[3].start()
 
     value = e1[place.s].astype(F32)
     e1_sum.core_copy(0).wait_recv()
@@ -1076,31 +1197,31 @@
     input_ref[...] = (gmid_ref[...] + norm_backward(normal, spread, value * vec_ref[0:1])).astype(
         BF16
     )
-    total_ref[...] = small.fold(3)
-    publish(gq, rq, final_q)
-    keep = [
-        pltpu.make_async_copy(src, dst.at[place.s], local.at[free + 2 + i])
-        for i, (src, dst) in enumerate([(r1, w1_out), (s2_in, w2_out), (rq, wq_out), (ro, wo_out)])
-    ]
-    for copy in keep:
-        copy.start()
-    for final in (final2, final1, final_o):
+    for final in final_q:
+        for j in range(1, place.ys):
+            final.arrive_y(j)
+    value = hop[1]
+    for j, copy in enumerate(across):
+        copy.wait_recv()
+        value = value + far[j + 1]
+    total_ref[...] = value
+    finals = (final1, final2, final_o, *final_q)
+    for final in finals:
         for j in range(place.ys):
             final.arrive_core(j)
-    for j in range(1, place.ys):
-        final_q.arrive_y(j)
-    for j in range(place.ys):
-        final_q.arrive_core(j)
-    for final in (final1, final2, final_o, final_q):
+    for final in finals:
         final.drain()
     for group in (out_sum, e1_sum):
         for j in range(place.ys):
             group.core_copy(j).wait_send()
         for j in range(1, place.ys):
             group.y_copy(j, outp.at[j]).wait_send()
-    for group in (g1, gq, go):
+    for group in (*gq, go, small):
         group.drain()
-    small.drain()
+    g1.drain_x(late)
+    g1.drain_z()
+    for copy in (near, *across):
+        copy.wait_send()
     for copy in keep:
         copy.wait()
 
@@ -1113,25 +1234,26 @@
     heads = kt.shape[0]
     wide = heads * HEAD_DIM
     share = D // place.dp
-    width, units = g1.shape[2], s2.shape[0]
+    width, units = g1.shape[3], s2.shape[0]
     ys, xs, zs = place.ys, max(place.xs - 1, 1), place.zs
     anyspace = pl.BlockSpec(memory_space=pl.ANY)
     inside = pl.BlockSpec(memory_space=pltpu.VMEM)
     vm = lambda *shape: pltpu.VMEM(shape, BF16)
-    tall = 8 + 2 * seq
-    hops = small_hops(place)
+    tall = 16
+    each = 2 if heads % 2 == 0 else 1
+    groups, triple = heads // each, 3 * HEAD_DIM * each
     outs = [
         ((rows, D), BF16, inside),
         ((rows, D), BF16, inside),
-        ((tall, D), F32, inside),
+        ((tall, share), F32, inside),
         ((seq, share, width), BF16, anyspace),
         ((seq, units, D), BF16, anyspace),
-        ((seq, share, 3 * wide), BF16, anyspace),
+        ((seq, groups, share, triple), BF16, anyspace),
         ((seq, share, wide), BF16, anyspace),
     ]
     split = []
     if not whole_tiles(share):
-        split = [vm(place.dp, share, 3 * wide), vm(place.dp, share, wide)]
+        split = [vm(groups, place.dp, share, triple), vm(place.dp, share, wide)]
     return pl.pallas_call(
         functools.partial(tail_kernel, place),
         in_specs=[inside] * 5 + [anyspace] * 13,
@@ -1145,7 +1267,7 @@
             vm(wide, slots),
             vm(seq, rows, D),
             vm(D, slots),
-            vm(slots, D),
+            vm(D, slots),
             vm(place.dp, share, 3 * wide),
             vm(slots, 3 * wide),
             vm(wide, D),
@@ -1158,99 +1280,92 @@
             vm(max(ys - 1, 1), rows, D),
             vm(ys, rows, D),
             vm(max(ys - 1, 1), rows, D),
-            vm(D, 3 * wide),
+            vm(groups, D, triple),
+            vm(slots, triple),
             vm(D, wide),
-            vm(zs, share, width),
-            vm(xs, zs, share, 3 * wide),
+            vm(zs - zs // 2, share, width),
+            vm(xs, zs - zs // 2, share, width),
+            vm(groups, xs, zs, share, triple),
             vm(xs, zs, share, wide),
-            vm(xs, zs, share, width),
-            vm(zs - 1, share, 3 * wide),
+            vm(groups, zs - 1, share, triple),
             vm(zs - 1, share, wide),
             vm(zs - 1, share, width),
             vm(share, width),
-            vm(share, 3 * wide),
+            vm(units, D),
+            vm(groups, share, triple),
             vm(share, wide),
-            pltpu.VMEM((4, tall, D), F32),
-            pltpu.VMEM((hops, tall, D), F32),
+            pltpu.VMEM((8, D), F32),
+            pltpu.VMEM((place.dp, tall, share), F32),
+            pltpu.VMEM((xs, zs, tall, share), F32),
+            pltpu.VMEM((zs - 1, tall, share), F32),
+            pltpu.VMEM((2, tall, share), F32),
+            pltpu.VMEM((ys, tall, share), F32),
         ]
         + split
-        + dp_semaphores(place, 3)
-        + seq_semaphores(place, 6)
-        + [
-            pltpu.SemaphoreType.DMA((hops,)),
-            pltpu.SemaphoreType.DMA((hops,)),
-            pltpu.SemaphoreType.DMA((24 + ys + zs,)),
-        ],
+        + dp_semaphores(place, 3 + heads)
+        + seq_semaphores(place, 7 + heads)
+        + [pltpu.SemaphoreType.DMA((24 + ys,))],
         compiler_params=params(collective_id=2, has_side_effects=True),
         name="tail",
     )(vectors, sums, lse, middle, gmid, qt, kt, kn, vn, gb, mix, wo, wq, normed, x, part, g1, s2)
 
 
-def prep_kernel(place, q_ref, k_ref, v_ref, w1_ref, vec_ref, b1_ref, small_ref, wqkv_ref, w1_out):
+def prep_kernel(place, q_ref, k_ref, v_ref, w1_ref, wqkv_ref, w1_out):
     place.locate()
     dp, seq = place.dp, place.seq
-    share = D // dp
     wide = D // seq
     units = FF // (dp * seq)
-    small_ref[...] = jnp.zeros_like(small_ref)
     for s in range(seq):
 
         @pl.when(place.s == s)
         def _():
             for i, ref in enumerate((q_ref, k_ref, v_ref)):
-                wqkv_ref[:, i * wide : (i + 1) * wide] = ref[:, s * wide : (s + 1) * wide]
+                for head in range(wide // HEAD_DIM):
+                    to = (3 * head + i) * HEAD_DIM
+                    at = s * wide + head * HEAD_DIM
+                    wqkv_ref[:, to : to + HEAD_DIM] = ref[:, at : at + HEAD_DIM]
             for d in range(dp):
                 first = d * (FF // dp) + s * units
                 w1_out[:, d * units : (d + 1) * units] = w1_ref[:, first : first + units]
 
-    vec = vec_ref[...]
-    for d in range(dp):
-        home = (d * share) // wide
-        first = d * share - home * wide
-
-        @pl.when(place.d == d)
-        def _():
-            small_ref[0:6, d * share : (d + 1) * share] = vec[0:6]
-            small_ref[6:7, d * units : (d + 1) * units] = b1_ref[pl.ds(place.s, 1), :]
-
-            @pl.when(place.s == home)
-            def _():
-                small_ref[8:10, first : first + share] = vec[6:8]
-
-
-def prep(place, q, k, v, w1, vectors, b1):
+
+def prep(place, q, k, v, w1):
     wide = D // place.seq
     share = q.shape[0]
     inside = pl.BlockSpec(memory_space=pltpu.VMEM)
     return pl.pallas_call(
         functools.partial(prep_kernel, place),
-        in_specs=[inside] * 6,
-        out_specs=[inside] * 3,
+        in_specs=[inside] * 4,
+        out_specs=[inside] * 2,
         out_shape=[
-            jax.ShapeDtypeStruct((16, D), F32),
             jax.ShapeDtypeStruct((share, 3 * wide), BF16),
             jax.ShapeDtypeStruct((share, FF // place.seq), BF16),
         ],
         compiler_params=params(),
         name="prep",
-    )(q, k, v, w1, vectors, b1)
+    )(q, k, v, w1)
 
 
 def finish_kernel(
     place, w1_ref, w2_ref, wq_ref, wo_ref, total_ref, layer_ref, input_ref,
     layer_out, input_out, w1_out, w2_out, q_out, k_out, v_out, wo_out, g1_out, s1_out, bo_out, g2_out, s2_out, b2_out,
-    bq_out, bv_out, b1_out, lines,
+    bq_out, bv_out, b1_out,
 ):
     place.locate()
     dp, seq = place.dp, place.seq
     share = D // dp
     wide = D // seq
     units = FF // (dp * seq)
+    each = wide // HEAD_DIM // wq_ref.shape[1]
     w2_out[...] = w2_ref[...].astype(F32)
     for s in range(seq):
         cols = slice(s * wide, (s + 1) * wide)
-        for i, out in enumerate((q_out, k_out, v_out)):
-            out[:, cols] = wq_ref[s, :, i * wide : (i + 1) * wide].astype(F32)
+        for head in range(wide // HEAD_DIM):
+            to = slice(s * wide + head * HEAD_DIM, s * wide + (head + 1) * HEAD_DIM)
+            for i, out in enumerate((q_out, k_out, v_out)):
+                first = ((head % each) * 3 + i) * HEAD_DIM
+                part = wq_ref[s, head // each, :, first : first + HEAD_DIM]
+                out[:, to] = part.astype(F32)
         wo_out[:, cols] = wo_ref[s].astype(F32)
         for d in range(dp):
             first = d * (FF // dp) + s * units
@@ -1260,23 +1375,11 @@
     def _():
         layer_out[...] = layer_ref[...]
         input_out[...] = input_ref[...]
-        lines[...] = total_ref[0:8]
+        outs = (g1_out, s1_out, bo_out, g2_out, s2_out, b2_out, bq_out, bv_out)
+        for i, out in enumerate(outs):
+            out[...] = total_ref[i : i + 1]
         for s in range(seq):
-            cols = slice(s * wide, (s + 1) * wide)
-            lines[6:7, cols] = total_ref[8 + s : 9 + s, :wide]
-            lines[7:8, cols] = total_ref[8 + s : 9 + s, wide : 2 * wide]
-        outs = (g1_out, s1_out, bo_out, g2_out, s2_out, b2_out, bq_out, bv_out)
-        for d in range(dp):
-
-            @pl.when(place.d == d)
-            def _():
-                for i, out in enumerate(outs):
-                    out[...] = lines[i : i + 1, d * share : (d + 1) * share]
-                for s in range(seq):
-                    row = 8 + seq + s
-                    b1_out[:, s * units : (s + 1) * units] = total_ref[
-                        row : row + 1, d * units : (d + 1) * units
-                    ]
+            b1_out[:, s * units : (s + 1) * units] = total_ref[8 + s : 9 + s, :units]
 
 
 def finish(place, w1, w2, wq, wo, totals, layer, grad):
@@ -1295,7 +1398,7 @@
         in_specs=[
             mat(w1.shape[2]),
             pl.BlockSpec((seq, tall, D), lambda i: (0, i, 0)),
-            mat(wq.shape[2]),
+            pl.BlockSpec((seq, wq.shape[1], tile, wq.shape[3]), lambda i: (0, 0, i, 0)),
             mat(wo.shape[2]),
             pl.BlockSpec(totals.shape, lambda i: (0, 0)),
             pl.BlockSpec(layer.shape, lambda i: (0, 0)),
@@ -1311,7 +1414,6 @@
         + [f32(share, D)] * 4
         + [f32(1, share)] * 8
         + [f32(1, FF // dp)],
-        scratch_shapes=[pltpu.VMEM((8, D), F32)],
         compiler_params=params(),
         name="finish",
     )(w1, w2, wq, wo, totals, layer, grad)
@@ -1330,25 +1432,23 @@
     quarter = dp * units
 
     spot = Place(dp, seq)
-    vectors = jnp.stack(
-        [first_gain, first_shift, output_bias, second_gain, second_shift, reduce_bias, query_bias,
-         value_bias]
-    ).astype(F32)
-    b1 = expand_bias.reshape(seq, units).astype(F32)
-    small, wqkv_share, w1_share = prep(
-        spot, query_weight, key_weight, value_weight, expand_weight, vectors, b1
-    )
-    x, vectors, w_qkv, w_out, w_expand, normed, qt, kt, keys, values, mix, lse = front(
-        spot, clip_lengths, clip_order, hidden_in[0], small, wqkv_share, output_weight, w1_share
+    b1 = lax.dynamic_slice_in_dim(expand_bias, me * units, units, 0)
+    rows = [first_gain, first_shift, output_bias, second_gain, second_shift, reduce_bias,
+            jnp.pad(b1, (0, D // dp - units)), query_bias, value_bias]
+    small = jnp.pad(jnp.stack(rows).astype(F32), ((0, 16 - len(rows)), (0, 0)))
+    if not whole_tiles(units):
+        reduce_weight = lax.dynamic_slice_in_dim(reduce_weight, me * units, units, 0)
+    wqkv_share, w1_share = prep(spot, query_weight, key_weight, value_weight, expand_weight)
+    x, vectors, w_qkv, w_out, w_expand, w2_ahead, normed, qt, kt, keys, values, mix, lse = front(
+        spot, clip_lengths, clip_order, hidden_in[0], small, wqkv_share, output_weight, w1_share,
+        reduce_weight,
     )
     w_out = w_out.reshape(D, D)
     w_expand = w_expand.reshape(D, quarter)
     mix = mix.reshape(D, slots)
-    if not whole_tiles(units):
-        reduce_weight = lax.dynamic_slice_in_dim(reduce_weight, me * units, units, 0)
     grad_branch, middle, grad_middle, out_part, g1, s2, sums = feed(
         spot, clip_lengths, clip_order, x, mix, cotangent[0], w_out, w_expand, reduce_weight,
-        vectors,
+        w2_ahead, vectors,
     )
     layer_output, input_grad, totals, w1_grad, w2_grad, qkv_grad, wo_grad = tail(
         spot, vectors, sums, lse, middle, grad_middle, qt, kt, keys, values, grad_branch, mix,

time: 425 us -> 341 us (0.80)
  Pallas kernels: 410 us -> 327 us
    pallas_call x1, Pallas kernels: 136 us -> 101 us  [feed(): pl.pallas_call(functools.partial(feed_kernel, place), in_specs=[pl.BlockS...]
    pallas_call x1, Pallas kernels: 137 us -> 103 us  [tail(): pl.pallas_call(functools.partial(tail_kernel, place), in_specs=[inside] *...]
    pallas_call x1, Pallas kernels: 125 us -> 111 us  [front(): pl.pallas_call(functools.partial(front_kernel, place), in_specs=[pl.Block...]
where the time goes in v5:
time: 341 us; the launch traced here: 337 us
  Pallas kernels  327 us (96%)
  local copies, waits for them, and re-layouts  6.07 us (2%)
    pallas_call x1, Pallas kernels, front(): pl.pallas_call(functools.partial(front_kernel, place), in_specs=[pl.Block...  111 us
    pallas_call x1, Pallas kernels, tail(): pl.pallas_call(functools.partial(tail_kernel, place), in_specs=[inside] *...  103 us
    pallas_call x1, Pallas kernels, feed(): pl.pallas_call(functools.partial(feed_kernel, place), in_specs=[pl.BlockS...  101 us
    pallas_call x1, Pallas kernels, finish(): pl.pallas_call(functools.partial(finish_kernel, place), grid=(steps,), in...  9.07 us

profile of v5, /device:TPU:0, one launch (start us, length us, event | category | flops | bytes accessed | tf_op | source)
XLA Modules:
  0.0 336.6 jit_solution(743267043479446301)
XLA Ops:
  1.3 0.8 dynamic_slice.3
  2.1 0.7 stack.30
  2.7 0.7 stack.31
  3.4 0.7 stack.37
  4.0 0.7 stack.38
  4.7 0.7 stack.32
  5.4 0.7 stack.33
  6.0 0.7 stack.34
  6.7 0.7 stack.35
  7.4 0.6 pad_convert_fusion.sm_in
  8.0 3.1 prep.1
  11.1 110.8 %front.1 = (bf16[4,384,1280]{2,1,0:T(8,128)(2,1)}, f32[16,1280]{1,0:T(8,128)}, bf16[8,160,960]{2,1,0:T(8,128)(2,1)}, bf16[8,160,1280]{2,1,0:T(8,128)(2,1)}, bf16...) custom-call(s32[8]{0:T(128)} %lengths_ref.3, ...), custom_call_target="tpu_custom_call" | custom-call | tf_op jit(solution)/shard_map/front/pallas_call | solution.py:497
  121.9 100.9 %feed.1 = (bf16[4,384,1280]{2,1,0:T(8,128)(2,1)}, f32[384,1280]{1,0:T(8,128)}, f32[384,1280]{1,0:T(8,128)}, bf16[4,384,1280]{2,1,0:T(8,128)(2,1)}, bf16[4,2,160,...) custom-call(s32[8]{0:T(128)} %lengths_ref.3, s32[1]{0:T(128)S(6)} %copy.36.order_ref, ...), custom_call_target="tpu_custom_call" | custom-call | tf_op jit(solution)/shard_map/feed/pallas_call | solution.py:894
  222.7 103.3 %tail.1 = (bf16[384,1280]{1,0:T(8,128)(2,1)}, bf16[384,1280]{1,0:T(8,128)(2,1)}, f32[16,160]{1,0:T(8,128)}, bf16[4,160,1280]{2,1,0:T(8,128)(2,1)}, bf16[4,160,12...) custom-call(f32[16,1280]{1,0:T(8,128)} %get-tuple-element.65.vec_ref, ...), custom_call_target="tpu_custom_call" | custom-call | tf_op jit(solution)/shard_map/tail/pallas_call | solution.py:1257
  326.0 9.1 %finish.1 = (bf16[384,1280]{1,0:T(8,128)(2,1)}, bf16[384,1280]{1,0:T(8,128)(2,1)}, f32[160,5120]{1,0:T(8,128)}, f32[4,160,1280]{2,1,0:T(8,128)}, f32[160,1280]{1...) custom-call(bf16[4,160,1280]{2,1,0:T(8,128)(2,1)} %get-tuple-element, ...), custom_call_target="tpu_custom_call" | custom-call | tf_op jit(solution)/shard_map/finish/pallas_call | solution.py:1395
  335.1 1.3 reduce
  (2 shorter events, 0.1 us)

commit v6 on v5

--- a/solution.py
+++ b/solution.py
@@ -768,18 +768,15 @@
         if joined == 1:
             backward(place.at_y(j, 1 - place.c))
             scatter.core_copy(j).start()
-            if turns and j != 1:
-                r2.fold(turns.pop(0))
             backward(place.at_y(j, place.c))
         else:
             backward(lax.rem(place.y + j, place.ys))
             scatter.core_copy(j).start()
         if j:
             fold_y(j)
-            if turns:
-                r2.fold(turns.pop(0))
 
     gather.drain()
+    r2.fold(turns.pop(0))
 
     def w1_grad(i, _):
         cols = pl.ds(pl.multiple_of(i * 256, 128), 256)
@@ -1126,6 +1123,7 @@
         )
 
     x_load(order[0][0], 0).start()
+    last_folds = list(gq[groups - 1].order)
     for step, (at, j, both) in enumerate(order):
         slot = step % 2
         if step + 1 < len(order):
@@ -1143,13 +1141,16 @@
             e1_sum.core_copy(j).wait_recv()
             e1[target] = (e1[target].astype(F32) + core_b[j].astype(F32)).astype(BF16)
             e1_sum.y_copy(j, e1.at[target]).start()
+        if both and len(last_folds) > 2:
+            gq[groups - 1].fold(last_folds.pop(0))
     for d in range(place.dp):
         ps[d] = jnp.zeros_like(ps[d])
         ps[d, 0:8] = line[:, d * share : (d + 1) * share]
         ps[d, pl.ds(8 + place.s, 1), :units] = sums_ref[7:8, d * units : (d + 1) * units]
     small.start_x()
+    for k in last_folds:
+        gq[groups - 1].fold(k)
     small.fold_all()
-    gq[groups - 1].fold_all()
     for group in range(groups - 1):
         publish(gq[group], rq.at[group], final_q[group])
     value = outp[0].astype(F32)
@@ -1310,15 +1311,21 @@
     )(vectors, sums, lse, middle, gmid, qt, kt, kn, vn, gb, mix, wo, wq, normed, x, part, g1, s2)
 
 
-def prep_kernel(place, q_ref, k_ref, v_ref, w1_ref, wqkv_ref, w1_out):
+def prep_kernel(place, q_ref, k_ref, v_ref, w1_ref, b1_ref, *refs):
+    *vec_refs, small_ref, wqkv_ref, w1_out = refs
     place.locate()
     dp, seq = place.dp, place.seq
     wide = D // seq
     units = FF // (dp * seq)
+    small_ref[...] = jnp.zeros_like(small_ref)
+    for i, ref in zip((0, 1, 2, 3, 4, 5, 7, 8), vec_refs):
+        small_ref[i : i + 1, :] = ref[...].astype(F32).reshape(1, D // dp)
+    b1 = b1_ref[...].astype(F32).reshape(1, FF // dp)
     for s in range(seq):
 
         @pl.when(place.s == s)
         def _():
+            small_ref[6:7, :units] = b1[:, s * units : (s + 1) * units]
             for i, ref in enumerate((q_ref, k_ref, v_ref)):
                 for head in range(wide // HEAD_DIM):
                     to = (3 * head + i) * HEAD_DIM
@@ -1329,27 +1336,28 @@
                 w1_out[:, d * units : (d + 1) * units] = w1_ref[:, first : first + units]
 
 
-def prep(place, q, k, v, w1):
+def prep(place, q, k, v, w1, b1, *vectors):
     wide = D // place.seq
     share = q.shape[0]
     inside = pl.BlockSpec(memory_space=pltpu.VMEM)
     return pl.pallas_call(
         functools.partial(prep_kernel, place),
-        in_specs=[inside] * 4,
-        out_specs=[inside] * 2,
+        in_specs=[inside] * (5 + len(vectors)),
+        out_specs=[inside] * 3,
         out_shape=[
+            jax.ShapeDtypeStruct((16, share), F32),
             jax.ShapeDtypeStruct((share, 3 * wide), BF16),
             jax.ShapeDtypeStruct((share, FF // place.seq), BF16),
         ],
         compiler_params=params(),
         name="prep",
-    )(q, k, v, w1)
+    )(q, k, v, w1, b1, *vectors)
 
 
 def finish_kernel(
     place, w1_ref, w2_ref, wq_ref, wo_ref, total_ref, layer_ref, input_ref,
     layer_out, input_out, w1_out, w2_out, q_out, k_out, v_out, wo_out, g1_out, s1_out, bo_out, g2_out, s2_out, b2_out,
-    bq_out, bv_out, b1_out,
+    bq_out, bv_out, b1_out, line,
 ):
     place.locate()
     dp, seq = place.dp, place.seq
@@ -1377,9 +1385,10 @@
         input_out[...] = input_ref[...]
         outs = (g1_out, s1_out, bo_out, g2_out, s2_out, b2_out, bq_out, bv_out)
         for i, out in enumerate(outs):
-            out[...] = total_ref[i : i + 1]
+            out[...] = total_ref[i : i + 1].reshape(share)
         for s in range(seq):
-            b1_out[:, s * units : (s + 1) * units] = total_ref[8 + s : 9 + s, :units]
+            line[:, s * units : (s + 1) * units] = total_ref[8 + s : 9 + s, :units]
+        b1_out[...] = line[...].reshape(FF // dp)
 
 
 def finish(place, w1, w2, wq, wo, totals, layer, grad):
@@ -1390,7 +1399,7 @@
     tall = units // steps
     mat = lambda *tail: pl.BlockSpec((seq, tile, *tail), lambda i: (0, i, 0))
     out = lambda cols: pl.BlockSpec((tile, cols), lambda i: (i, 0))
-    small = pl.BlockSpec((1, share), lambda i: (0, 0))
+    small = pl.BlockSpec((share,), lambda i: (0,))
     f32 = lambda *shape: jax.ShapeDtypeStruct(shape, F32)
     return pl.pallas_call(
         functools.partial(finish_kernel, place),
@@ -1408,12 +1417,13 @@
         + [out(FF), pl.BlockSpec((seq, tall, D), lambda i: (0, i, 0))]
         + [out(D)] * 4
         + [small] * 8
-        + [pl.BlockSpec((1, FF // dp), lambda i: (0, 0))],
+        + [pl.BlockSpec((FF // dp,), lambda i: (0,))],
         out_shape=[jax.ShapeDtypeStruct(layer.shape, BF16)] * 2
         + [f32(share, FF), f32(seq, units, D)]
         + [f32(share, D)] * 4
-        + [f32(1, share)] * 8
-        + [f32(1, FF // dp)],
+        + [f32(share)] * 8
+        + [f32(FF // dp)],
+        scratch_shapes=[pltpu.VMEM((1, FF // dp), F32)],
         compiler_params=params(),
         name="finish",
     )(w1, w2, wq, wo, totals, layer, grad)
@@ -1432,13 +1442,12 @@
     quarter = dp * units
 
     spot = Place(dp, seq)
-    b1 = lax.dynamic_slice_in_dim(expand_bias, me * units, units, 0)
-    rows = [first_gain, first_shift, output_bias, second_gain, second_shift, reduce_bias,
-            jnp.pad(b1, (0, D // dp - units)), query_bias, value_bias]
-    small = jnp.pad(jnp.stack(rows).astype(F32), ((0, 16 - len(rows)), (0, 0)))
     if not whole_tiles(units):
         reduce_weight = lax.dynamic_slice_in_dim(reduce_weight, me * units, units, 0)
-    wqkv_share, w1_share = prep(spot, query_weight, key_weight, value_weight, expand_weight)
+    small, wqkv_share, w1_share = prep(
+        spot, query_weight, key_weight, value_weight, expand_weight, expand_bias, first_gain,
+        first_shift, output_bias, second_gain, second_shift, reduce_bias, query_bias, value_bias,
+    )
     x, vectors, w_qkv, w_out, w_expand, w2_ahead, normed, qt, kt, keys, values, mix, lse = front(
         spot, clip_lengths, clip_order, hidden_in[0], small, wqkv_share, output_weight, w1_share,
         reduce_weight,
@@ -1459,7 +1468,7 @@
     )
     layer_output, input_grad, *results = results
     (w1_grad, w2_grad, wq_grad, wk_grad, wv_grad, wo_grad) = results[:6]
-    g1, s1, bo, g2, s2, b2, bq, bv, b1 = (value.reshape(-1) for value in results[6:])
+    g1, s1, bo, g2, s2, b2, bq, bv, b1 = results[6:]
     return (
         layer_output[None], input_grad[None], g1, s1, wq_grad, bq, wk_grad, wv_grad, bv, wo_grad,
         bo, g2, s2, w1_grad, b1, w2_grad.reshape(FF // dp, D), b2,

time: 341 us -> 334 us (0.979)
  local copies, waits for them, and re-layouts: 6.07 us -> 0 us
    another operation x10 -> x0, local copies, waits for them, and re-layouts: 5.31 us -> none  [per_device(): small = jnp.pad(jnp.stack(rows).astype(F32), ((0, 16 - len(rows)), (0, 0)))]
where the time goes in v6:
time: 334 us; the launch traced here: 329 us
  Pallas kernels  328 us (98%)
    pallas_call x1, Pallas kernels, front(): pl.pallas_call(functools.partial(front_kernel, place), in_specs=[pl.Block...  111 us
    pallas_call x1, Pallas kernels, tail(): pl.pallas_call(functools.partial(tail_kernel, place), in_specs=[inside] *...  104 us
    pallas_call x1, Pallas kernels, feed(): pl.pallas_call(functools.partial(feed_kernel, place), in_specs=[pl.BlockS...  101 us
    pallas_call x1, Pallas kernels, finish(): pl.pallas_call(functools.partial(finish_kernel, place), grid=(steps,), in...  9.08 us

profile of v6, /device:TPU:0, one launch (start us, length us, event | category | flops | bytes accessed | tf_op | source)
XLA Modules:
  0.0 329.4 jit_solution(14682347460101118679)
XLA Ops:
  1.3 3.1 prep.1
  4.4 110.8 %front.1 = (bf16[4,384,1280]{2,1,0:T(8,128)(2,1)}, f32[16,1280]{1,0:T(8,128)}, bf16[8,160,960]{2,1,0:T(8,128)(2,1)}, bf16[8,160,1280]{2,1,0:T(8,128)(2,1)}, bf16...) custom-call(s32[8]{0:T(128)} %lengths_ref.3, ...), custom_call_target="tpu_custom_call" | custom-call | tf_op jit(solution)/shard_map/front/pallas_call | solution.py:497
  115.2 100.9 %feed.1 = (bf16[4,384,1280]{2,1,0:T(8,128)(2,1)}, f32[384,1280]{1,0:T(8,128)}, f32[384,1280]{1,0:T(8,128)}, bf16[4,384,1280]{2,1,0:T(8,128)(2,1)}, bf16[4,2,160,...) custom-call(s32[8]{0:T(128)} %lengths_ref.3, s32[1]{0:T(128)S(6)} %copy.36.order_ref, ...), custom_call_target="tpu_custom_call" | custom-call | tf_op jit(solution)/shard_map/feed/pallas_call | solution.py:891
  216.1 104.0 %tail.1 = (bf16[384,1280]{1,0:T(8,128)(2,1)}, bf16[384,1280]{1,0:T(8,128)(2,1)}, f32[16,160]{1,0:T(8,128)}, bf16[4,160,1280]{2,1,0:T(8,128)(2,1)}, bf16[4,160,12...) custom-call(f32[16,1280]{1,0:T(8,128)} %get-tuple-element.67.vec_ref, ...), custom_call_target="tpu_custom_call" | custom-call | tf_op jit(solution)/shard_map/tail/pallas_call | solution.py:1258
  320.1 9.1 %finish.1 = (bf16[384,1280]{1,0:T(8,128)(2,1)}, bf16[384,1280]{1,0:T(8,128)(2,1)}, f32[160,5120]{1,0:T(8,128)}, f32[4,160,1280]{2,1,0:T(8,128)}, f32[160,1280]{1...) custom-call(bf16[4,160,1280]{2,1,0:T(8,128)(2,1)} %get-tuple-element, ...), custom_call_target="tpu_custom_call" | custom-call | tf_op jit(solution)/shard_map/finish/pallas_call | solution.py:1404
